TPU v7x, 32 devices: a whole 2x2x4 slice. The times are simulated.
32 devices in a mesh: groups: 2 (over x), seq: 16 (over z, y, core).
Axes of the slice: x: 2, y: 2, z: 4, core: 2. Of those that a mesh axis runs over, the one named last changes fastest.
Arguments:
- queries: bfloat16 [8192, 4096], P(('groups', 'seq')), parts along dimension 0, may hold values from -6 to 6
- keys: bfloat16 [8192, 2048], P(('groups', 'seq')), parts along dimension 0, may hold values from -6 to 6
- values: bfloat16 [8192, 2048], P(('groups', 'seq')), parts along dimension 0, may hold values from -6 to 6
- doc_blocks: int32 [16], P('groups'), parts along dimension 0, may hold values from 1 to 8, 32 in all
Outputs:
- attended: bfloat16 [8192, 4096], P(('groups', 'seq')), parts along dimension 0
There are 2 independent parts, one for each index of `groups`. A program takes and returns all parts, laid end to end along the dimension named above; each array names one. Nothing has to cross between parts.
Inputs may be any that keep to these rules, and one draw needn't show every extreme that they name: `doc_blocks`: the lengths add up to 32; the longest document has exactly 8 units.
All inputs are finite; a program needn't handle non-finite values.
Results may differ from a plain program's by a relative error of at most 0.004.
Values may be sent and summed in bfloat16 or wider, within the bound.
No kernel may reach another device: no remote copies, remote signals or barrier semaphores. Data moves between devices by JAX's collectives and lax.ppermute only.
A program may use at most 64 MiB of HBM per device.

v0:
```python
import functools
import math

import jax
import jax.numpy as jnp
from jax import lax
from jax.experimental import pallas as pl
from jax.experimental.pallas import tpu as pltpu
from jax.sharding import PartitionSpec as P


DH = 128
BLK = 128
CORES = 2
BUCKETS = 4
PART = 32
SCALE = 144.0 ** (-0.5)


def shift(block, pairs):
    return lax.ppermute(block, "seq", pairs)


def attend_kernel(plan, blocks, q_near, q_far, *rest):
    first, heads, _, ratio, window, spans = plan
    pieces = rest[: spans + 1]
    out_near, out_far, q_buf, k_buf, v_buf, o_buf, s_buf, w_buf = rest[spans + 1 :]
    rows = q_near.shape[-2]
    chip_rows = rows * CORES
    me = lax.axis_index("seq")
    core = me % CORES
    chip = me // CORES
    q_width = heads * DH * ratio
    base = spans * chip_rows
    q_cols = slice(first * DH * ratio, first * DH * ratio + q_width)
    mine = pl.multiple_of(core * rows, rows)
    other = pl.multiple_of((1 - core) * rows, rows)
    q_buf[pl.ds(mine, rows)] = q_near[0, :, q_cols]
    q_buf[pl.ds(other, rows)] = q_far[0, :, q_cols]
    for distance in range(spans + 1):
        at = slice(base - distance * chip_rows, base - distance * chip_rows + chip_rows)
        k_buf[at] = pieces[distance][0]
        v_buf[at] = pieces[distance][1]

    units = chip_rows // BLK
    factor = SCALE * math.log2(math.e)
    tile_rows = ratio * BLK

    def one_tile(step, carry):
        group = step // units
        unit = step % units
        number = chip * units + unit
        begin = jnp.int32(0)
        total = jnp.int32(0)
        for doc in range(blocks.shape[0]):
            begin = jnp.where(number >= total, total, begin)
            total = total + blocks[doc]
        count = number - begin + 1
        q_at = pl.ds(pl.multiple_of(unit * BLK, BLK), BLK)
        kv_cols = pl.ds(pl.multiple_of(group * DH, DH), DH)

        def with_keys(shown):
            keys_seen = shown * BLK
            kv_at = pl.ds(pl.multiple_of(base + (unit + 1 - shown) * BLK, BLK), keys_seen)
            tiles = [
                q_buf[q_at, pl.ds(pl.multiple_of((group * ratio + s) * DH, DH), DH)]
                for s in range(ratio)
            ]
            s_buf[:, :keys_seen] = lax.dot_general(
                jnp.concatenate(tiles, axis=0),
                k_buf[kv_at, kv_cols],
                (((1,), (1,)), ((), ())),
                preferred_element_type=jnp.float32,
            )
            hidden = (shown - count) * BLK
            unsure = min(step_units, shown) * BLK
            key = lax.broadcasted_iota(jnp.int32, (PART, unsure), 1)
            totals = []
            for part in range(tile_rows // PART):
                at = slice(part * PART, (part + 1) * PART)
                scores = s_buf[at, :keys_seen]
                front = jnp.where(key >= hidden, scores[:, :unsure], -1e30)
                if unsure < keys_seen:
                    scores = jnp.concatenate([front, scores[:, unsure:]], axis=1)
                else:
                    scores = front
                last = lax.broadcasted_iota(jnp.int32, (PART, BLK), 1)
                row = lax.broadcasted_iota(jnp.int32, (PART, BLK), 0) + part * PART % BLK
                tail = jnp.where(last <= row, scores[:, keys_seen - BLK :], -1e30)
                if keys_seen > BLK:
                    scores = jnp.concatenate([scores[:, : keys_seen - BLK], tail], axis=1)
                else:
                    scores = tail
                top = jnp.max(scores, axis=1, keepdims=True) * factor
                weights = jnp.exp2(scores * factor - top)
                totals.append(jnp.sum(weights, axis=1, keepdims=True))
                w_buf[at, :keys_seen] = weights.astype(jnp.bfloat16)
            blended = jnp.dot(
                w_buf[:, :keys_seen],
                v_buf[kv_at, kv_cols],
                preferred_element_type=jnp.float32,
            )
            blended = (blended / jnp.concatenate(totals, axis=0)).astype(jnp.bfloat16)
            for s in range(ratio):
                cols = pl.ds(pl.multiple_of((group * ratio + s) * DH, DH), DH)
                o_buf[q_at, cols] = blended[s * BLK : (s + 1) * BLK]

        step_units = -(-window // BUCKETS)
        shown = 0
        while shown < window:
            lower, shown = shown, min(shown + step_units, window)
            pl.when((count > lower) & (count <= shown))(functools.partial(with_keys, shown))
        return carry

    lax.fori_loop(0, heads * units, one_tile, 0)
    out_near[...] = o_buf[pl.ds(mine, rows)]
    out_far[...] = o_buf[pl.ds(other, rows)]


def attend(plan, blocks, q_near, q_far, pieces):
    _, heads, _, ratio, window, spans = plan
    rows = q_near.shape[-2]
    chip_rows = rows * CORES
    held = (spans + 1) * chip_rows
    kv_width = heads * DH
    q_width = kv_width * ratio
    scores = heads * ratio * chip_rows * window * BLK
    scratch_bytes = (chip_rows * q_width + held * kv_width) * 4 + ratio * BLK * window * BLK * 6
    near_by = pl.BlockSpec(memory_space=pltpu.VMEM)
    shape = pltpu.VMEM((rows, q_width), q_near.dtype)
    return pl.pallas_call(
        functools.partial(attend_kernel, plan),
        out_shape=(shape, shape),
        in_specs=[pl.BlockSpec(memory_space=pltpu.SMEM)] + [near_by] * (2 + len(pieces)),
        out_specs=(near_by, near_by),
        scratch_shapes=[
            pltpu.VMEM((chip_rows, q_width), jnp.bfloat16),
            pltpu.VMEM((held, kv_width), jnp.bfloat16),
            pltpu.VMEM((held, kv_width), jnp.bfloat16),
            pltpu.VMEM((chip_rows, q_width), jnp.bfloat16),
            pltpu.VMEM((ratio * BLK, window * BLK), jnp.float32),
            pltpu.VMEM((ratio * BLK, window * BLK), jnp.bfloat16),
        ],
        cost_estimate=pl.CostEstimate(
            flops=4 * scores * DH,
            bytes_accessed=2 * (chip_rows * q_width * 2 + held * kv_width * 2),
            transcendentals=scores,
        ),
        compiler_params=pltpu.CompilerParams(vmem_limit_bytes=scratch_bytes + (6 << 20)),
    )(blocks, q_near, q_far, *pieces)


def place_kernel(firsts, half, ratio, *refs):
    count = len(firsts)
    out, sems = refs[2 * count :]
    core = lax.axis_index("seq") % CORES
    stores = []
    for i, first in enumerate(firsts):
        for which, piece in ((core, refs[i]), (1 - core, refs[count + i])):
            col = pl.multiple_of((which * half + first) * ratio * DH, DH)
            store = pltpu.make_async_copy(
                piece, out.at[:, pl.ds(col, piece.shape[1])], sems.at[len(stores)]
            )
            store.start()
            stores.append(store)
    for store in stores:
        store.wait()


def place(firsts, half, ratio, nears, fars, width):
    anywhere = pl.BlockSpec(memory_space=pl.ANY)
    return pl.pallas_call(
        functools.partial(place_kernel, firsts, half, ratio),
        out_shape=pltpu.HBM((nears[0].shape[0], width), nears[0].dtype),
        in_specs=[anywhere] * (2 * len(firsts)),
        out_specs=anywhere,
        scratch_shapes=[pltpu.SemaphoreType.DMA((2 * len(firsts),))],
        compiler_params=pltpu.CompilerParams(vmem_limit_bytes=1 << 20),
        name="place",
    )(*nears, *fars)


def split_kernel(arrays, widths, *refs):
    sources, far, near, sems = refs[:arrays], *refs[arrays:]
    core = lax.axis_index("seq") % CORES
    copies = []
    for which, target in ((1 - core, far), (core, near)):
        for i in range(arrays):
            col = pl.multiple_of(which * widths, DH)
            copy = pltpu.make_async_copy(
                sources[i].at[:, pl.ds(col, widths)], target.at[i], sems.at[len(copies)]
            )
            copy.start()
            copies.append(copy)
    for copy in copies:
        copy.wait()


def split(*arrays):
    rows, columns = arrays[0].shape
    width = columns // CORES
    shape = pltpu.VMEM((len(arrays), rows, width), arrays[0].dtype)
    anywhere = pl.BlockSpec(memory_space=pl.ANY)
    return pl.pallas_call(
        functools.partial(split_kernel, len(arrays), width),
        out_shape=(shape, shape),
        in_specs=[pl.BlockSpec(memory_space=pltpu.HBM)] * len(arrays),
        out_specs=(anywhere, anywhere),
        scratch_shapes=[pltpu.SemaphoreType.DMA((CORES * len(arrays),))],
        compiler_params=pltpu.CompilerParams(vmem_limit_bytes=1 << 20),
        name="split",
    )(*arrays)


def merge_kernel(sizes, near, far, *outs):
    core = lax.axis_index("seq") % CORES
    rows = near.shape[1]
    mine = pl.multiple_of(core * rows, rows)
    other = pl.multiple_of((1 - core) * rows, rows)
    col = 0
    for heads, out in zip(sizes, outs):
        cols = slice(col, col + heads * DH)
        out[:, pl.ds(mine, rows)] = near[:, :, cols]
        out[:, pl.ds(other, rows)] = far[:, :, cols]
        col += heads * DH


def merge(sizes, near, far):
    arrays, rows, _ = near.shape
    near_by = pl.BlockSpec(memory_space=pltpu.VMEM)
    return pl.pallas_call(
        functools.partial(merge_kernel, sizes),
        out_shape=tuple(
            pltpu.VMEM((arrays, rows * CORES, heads * DH), near.dtype) for heads in sizes
        ),
        in_specs=[near_by, near_by],
        out_specs=(near_by,) * len(sizes),
        compiler_params=pltpu.CompilerParams(vmem_limit_bytes=12 << 20),
        name="merge",
    )(near, far)


def choose_kernel(own, came, out):
    row = lax.axis_index("seq") // CORES % 2

    @pl.when(row == 0)
    def _():
        out[...] = own[...]

    @pl.when(row == 1)
    def _():
        out[...] = came[...]


def choose(own, came):
    near_by = pl.BlockSpec(memory_space=pltpu.VMEM)
    return pl.pallas_call(
        choose_kernel,
        out_shape=pltpu.VMEM(own.shape, own.dtype),
        in_specs=[near_by, near_by],
        out_specs=near_by,
        compiler_params=pltpu.CompilerParams(vmem_limit_bytes=6 << 20),
        name="choose",
    )(own, came)


def chunk_heads(half):
    sizes = [2] * (half // 2)
    return sizes + [1] * (half % 2)


def on_device(queries, keys, values, doc_blocks):
    devices = lax.axis_size("seq")
    rows = queries.shape[0]
    q_heads = queries.shape[1] // DH
    kv_heads = keys.shape[1] // DH
    ratio = q_heads // kv_heads
    half = kv_heads // CORES
    chips = devices // CORES
    chip_rows = rows * CORES
    window = rows * devices // BLK // 4
    spans = min(-(-(window - 1) * BLK // chip_rows), chips)

    partner = [(i, i ^ 1) for i in range(devices)]
    next_chip = [(i, i + CORES) for i in range(devices - CORES)]
    next_pair = [(i, i + 2 * CORES) for i in range(devices - 2 * CORES)]
    across = [(i, i ^ CORES) for i in range(devices)]
    paired = spans == 2 and chips % 2 == 0

    kv_send, kv_near = split(keys, values)
    kv_far = shift(kv_send, partner)
    q_send, q_near = split(queries)
    q_far = shift(q_send, partner)

    sizes = chunk_heads(half)
    firsts = [sum(sizes[:i]) for i in range(len(sizes))]

    nears, fars = [], []
    for first, heads, own in zip(firsts, sizes, merge(sizes, kv_near, kv_far)):
        held = [own]
        if paired:
            two_back = shift(own, next_pair)
            chosen = choose(own, two_back)
            one_back = shift(chosen, across)
            held += [one_back, two_back]
        else:
            for _ in range(spans):
                held.append(shift(held[-1], next_chip))
        plan = (first, heads, half, ratio, window, spans)
        out_near, out_far = attend(plan, doc_blocks, q_near, q_far, held)
        nears.append(out_near)
        fars.append(shift(out_far, partner))
    return place(firsts, half, ratio, nears, fars, queries.shape[1])


def solution(mesh):
    spec = P(("groups", "seq"), None)

    return jax.shard_map(
        on_device,
        mesh=mesh,
        in_specs=(spec, spec, spec, P("groups")),
        out_specs=spec,
        check_vma=False,
    )
```

profile of v0, /device:TPU:29, one launch (start us, length us, event | category | flops | bytes accessed | tf_op | source)
XLA Modules:
  0.0 86.4 jit_solution(3555114420884018383)
XLA Ops:
  0.0 0.0 copy-start
  0.0 0.0 copy-start.1
  0.0 1.4 %copy-done.1 = bf16[256,2048]{1,0:T(8,128)(2,1)S(1)} copy-done((bf16[256,2048]{1,0:T(8,128)(2,1)S(1)}, bf16[256,2048]{1,0:T(8,128)(2,1)}, u32[]{:S(2)}) %copy-start.1) | copy-done | bytes 1048600
  1.4 0.0 copy-start.2
  1.4 1.2 %copy-done.2 = bf16[256,2048]{1,0:T(8,128)(2,1)S(1)} copy-done((bf16[256,2048]{1,0:T(8,128)(2,1)S(1)}, bf16[256,2048]{1,0:T(8,128)(2,1)}, u32[]{:S(2)}) %copy-start.2) | copy-done | bytes 1048600
  2.6 0.2 split.3
  2.8 0.7 collective-permute-start.1
  3.6 0.0 copy-done
  3.6 0.2 split.2
  3.8 2.0 %collective-permute-done.1.far = bf16[2,256,1024]{2,1,0:T(8,128)(2,1)S(1)} collective-permute-done((bf16[2,256,1024]{2,1,0:T(8,128)(2,1)S(1)}, bf16[2,256,1024]{2,1,0:T(8,128)(2,1)S(1)}, u32[]{:S(2)}, u32[]{:S(2)}) %collective-permute-start.1) | collective-permute-done | bytes 1048608 | tf_op jit(solution)/shard_map/ppermute | solution.py:21
  5.9 0.2 merge.1
  6.0 1.3 %collective-permute-start.2 = (bf16[2,512,256]{2,1,0:T(8,128)(2,1)S(1)}, bf16[2,512,256]{2,1,0:T(8,128)(2,1)S(1)}, u32[]{:S(2)}, u32[]{:S(2)}) collective-permute-start(bf16[2,512,256]{2,1,0:T(8,128)(2,1)S(1)} %get-tuple-element.25.own.rest_0_), channel_id=1, source_target_pairs={{0,4},{1,5},{2,6},{3,7},{4,8},{5,9},{6,10},{7,11},{8,12},{9,13},{1... | collective-permute-start | bytes 1572872 | tf_op jit(solution)/shard_map/ppermute | solution.py:21
  7.3 0.4 collective-permute-start
  7.8 1.3 %collective-permute-start.4 = (bf16[2,512,256]{2,1,0:T(8,128)(2,1)S(1)}, bf16[2,512,256]{2,1,0:T(8,128)(2,1)S(1)}, u32[]{:S(2)}, u32[]{:S(2)}) collective-permute-start(bf16[2,512,256]{2,1,0:T(8,128)(2,1)S(1)} %get-tuple-element.27.own.rest_0_), channel_id=1, source_target_pairs={{0,4},{1,5},{2,6},{3,7},{4,8},{5,9},{6,10},{7,11},{8,12},{9,13},{1... | collective-permute-start | bytes 1572872 | tf_op jit(solution)/shard_map/ppermute | solution.py:21
  9.1 1.3 %collective-permute-start.6 = (bf16[2,512,256]{2,1,0:T(8,128)(2,1)S(1)}, bf16[2,512,256]{2,1,0:T(8,128)(2,1)S(1)}, u32[]{:S(2)}, u32[]{:S(2)}) collective-permute-start(bf16[2,512,256]{2,1,0:T(8,128)(2,1)S(1)} %get-tuple-element.29.own.rest_0_), channel_id=1, source_target_pairs={{0,4},{1,5},{2,6},{3,7},{4,8},{5,9},{6,10},{7,11},{8,12},{9,13},{1... | collective-permute-start | bytes 1572872 | tf_op jit(solution)/shard_map/ppermute | solution.py:21
  10.4 1.3 %collective-permute-start.8 = (bf16[2,512,256]{2,1,0:T(8,128)(2,1)S(1)}, bf16[2,512,256]{2,1,0:T(8,128)(2,1)S(1)}, u32[]{:S(2)}, u32[]{:S(2)}) collective-permute-start(bf16[2,512,256]{2,1,0:T(8,128)(2,1)S(1)} %get-tuple-element.31.own.rest_0_), channel_id=1, source_target_pairs={{0,4},{1,5},{2,6},{3,7},{4,8},{5,9},{6,10},{7,11},{8,12},{9,13},{1... | collective-permute-start | bytes 1572872 | tf_op jit(solution)/shard_map/ppermute | solution.py:21
  11.7 9.4 %collective-permute-done.2.came.rest_2_ = bf16[2,512,256]{2,1,0:T(8,128)(2,1)S(1)} collective-permute-done((bf16[2,512,256]{2,1,0:T(8,128)(2,1)S(1)}, bf16[2,512,256]{2,1,0:T(8,128)(2,1)S(1)}, u32[]{:S(2)}, u32[]{:S(2)}) %collective-permute-start.2) | collective-permute-done | bytes 524320 | tf_op jit(solution)/shard_map/ppermute | solution.py:21
  21.1 0.0 copy-start.3
  21.1 0.3 collective-permute-start.3
  21.4 10.9 %collective-permute-done.4.came.rest_2_ = bf16[2,512,256]{2,1,0:T(8,128)(2,1)S(1)} collective-permute-done((bf16[2,512,256]{2,1,0:T(8,128)(2,1)S(1)}, bf16[2,512,256]{2,1,0:T(8,128)(2,1)S(1)}, u32[]{:S(2)}, u32[]{:S(2)}) %collective-permute-start.4) | collective-permute-done | bytes 524320 | tf_op jit(solution)/shard_map/ppermute | solution.py:21
  32.3 0.3 collective-permute-start.5
  32.6 10.9 %collective-permute-done.6.came.rest_2_ = bf16[2,512,256]{2,1,0:T(8,128)(2,1)S(1)} collective-permute-done((bf16[2,512,256]{2,1,0:T(8,128)(2,1)S(1)}, bf16[2,512,256]{2,1,0:T(8,128)(2,1)S(1)}, u32[]{:S(2)}, u32[]{:S(2)}) %collective-permute-start.6) | collective-permute-done | bytes 524320 | tf_op jit(solution)/shard_map/ppermute | solution.py:21
  43.5 0.3 collective-permute-start.7
  43.8 10.9 %collective-permute-done.8.came.rest_2_ = bf16[2,512,256]{2,1,0:T(8,128)(2,1)S(1)} collective-permute-done((bf16[2,512,256]{2,1,0:T(8,128)(2,1)S(1)}, bf16[2,512,256]{2,1,0:T(8,128)(2,1)S(1)}, u32[]{:S(2)}, u32[]{:S(2)}) %collective-permute-start.8) | collective-permute-done | bytes 524320 | tf_op jit(solution)/shard_map/ppermute | solution.py:21
  54.8 0.3 collective-permute-start.9
  55.1 0.0 collective-permute-done.q_far
  55.1 0.0 collective-permute-done.3.rest_1_
  55.1 0.0 copy-done.3
  55.1 6.5 %shard_map.46 = (bf16[256,512]{1,0:T(8,128)(2,1)S(1)}, bf16[256,512]{1,0:T(8,128)(2,1)S(1)}) custom-call(s32[8]{0:T(128)S(1)} %copy-done.3, bf16[1,256,2048]{2,1,0:T(8,128)(2,1)S(1)} %get-tuple-element.21.q_near, bf16[1,256,2048]{2,1,0:T(8,128)(2,1)S(1)} %collective-permute-done.q_far, bf16[2,512,256]{2,1,0:T(8,128)(2,1)S(1)} %get-tuple-element.25.own.rest_0_, ...), custom_call_target="tpu_custom_call" | custom-call | flops 1073741824 | bytes 2621440 | tf_op jit(solution)/shard_map/pallas_call | solution.py:131
  61.6 1.6 %collective-permute-start.10 = (bf16[256,512]{1,0:T(8,128)(2,1)S(1)}, bf16[256,512]{1,0:T(8,128)(2,1)S(1)}, u32[]{:S(2)}, u32[]{:S(2)}) collective-permute-start(bf16[256,512]{1,0:T(8,128)(2,1)S(1)} %get-tuple-element.33), channel_id=1, source_target_pairs={{0,1},{1,0},{2,3},{3,2},{4,5},{5,4},{6,7},{7,6},{8,9},{9,8},{10,11... | collective-permute-start | bytes 786440 | tf_op jit(solution)/shard_map/ppermute | solution.py:21
  63.2 0.0 collective-permute-done.5.rest_1_
  63.2 6.5 %shard_map.47 = (bf16[256,512]{1,0:T(8,128)(2,1)S(1)}, bf16[256,512]{1,0:T(8,128)(2,1)S(1)}) custom-call(s32[8]{0:T(128)S(1)} %copy-done.3, bf16[1,256,2048]{2,1,0:T(8,128)(2,1)S(1)} %get-tuple-element.21.q_near, bf16[1,256,2048]{2,1,0:T(8,128)(2,1)S(1)} %collective-permute-done.q_far, bf16[2,512,256]{2,1,0:T(8,128)(2,1)S(1)} %get-tuple-element.27.own.rest_0_, ...), custom_call_target="tpu_custom_call" | custom-call | flops 1073741824 | bytes 2621440 | tf_op jit(solution)/shard_map/pallas_call | solution.py:131
  69.7 0.1 collective-permute-start.11
  69.8 0.0 collective-permute-done.7.rest_1_
  69.8 6.5 %shard_map.48 = (bf16[256,512]{1,0:T(8,128)(2,1)S(1)}, bf16[256,512]{1,0:T(8,128)(2,1)S(1)}) custom-call(s32[8]{0:T(128)S(1)} %copy-done.3, bf16[1,256,2048]{2,1,0:T(8,128)(2,1)S(1)} %get-tuple-element.21.q_near, bf16[1,256,2048]{2,1,0:T(8,128)(2,1)S(1)} %collective-permute-done.q_far, bf16[2,512,256]{2,1,0:T(8,128)(2,1)S(1)} %get-tuple-element.29.own.rest_0_, ...), custom_call_target="tpu_custom_call" | custom-call | flops 1073741824 | bytes 2621440 | tf_op jit(solution)/shard_map/pallas_call | solution.py:131
  76.4 0.6 collective-permute-start.12
  76.9 0.0 collective-permute-done.9.rest_1_
  76.9 6.5 %shard_map.49 = (bf16[256,512]{1,0:T(8,128)(2,1)S(1)}, bf16[256,512]{1,0:T(8,128)(2,1)S(1)}) custom-call(s32[8]{0:T(128)S(1)} %copy-done.3, bf16[1,256,2048]{2,1,0:T(8,128)(2,1)S(1)} %get-tuple-element.21.q_near, bf16[1,256,2048]{2,1,0:T(8,128)(2,1)S(1)} %collective-permute-done.q_far, bf16[2,512,256]{2,1,0:T(8,128)(2,1)S(1)} %get-tuple-element.31.own.rest_0_, ...), custom_call_target="tpu_custom_call" | custom-call | flops 1073741824 | bytes 2621440 | tf_op jit(solution)/shard_map/pallas_call | solution.py:131
  83.5 0.1 collective-permute-start.13
  83.6 0.0 collective-permute-done.10.refs_4_
  83.6 0.0 collective-permute-done.11.refs_5_
  83.6 0.0 collective-permute-done.12.refs_6_
  83.6 1.5 %collective-permute-done.13.refs_7_ = bf16[256,512]{1,0:T(8,128)(2,1)S(1)} collective-permute-done((bf16[256,512]{1,0:T(8,128)(2,1)S(1)}, bf16[256,512]{1,0:T(8,128)(2,1)S(1)}, u32[]{:S(2)}, u32[]{:S(2)}) %collective-permute-start.13) | collective-permute-done | bytes 262176 | tf_op jit(solution)/shard_map/ppermute | solution.py:21
  85.1 1.4 %place.1 = bf16[256,4096]{1,0:T(8,128)(2,1)} custom-call(bf16[256,512]{1,0:T(8,128)(2,1)S(1)} %get-tuple-element.26.refs_0_, bf16[256,512]{1,0:T(8,128)(2,1)S(1)} %get-tuple-element.28.refs_1_, bf16[256,512]{1,0:T(8,128)(2,1)S(1)} %get-tuple-element.30.refs_2_, bf16[256,512]{1,0:T(8,128)(2,1)S(1)} %get-tuple-element.32.refs_3_, ...), custom_call_target="tpu_custom_call" | custom-call | tf_op jit(solution)/shard_map/place/pallas_call | solution.py:172
  (4 shorter events, 0.1 us)
Async XLA Ops:
  0.0 3.6 %copy-start = (bf16[256,4096]{1,0:T(8,128)(2,1)S(1)}, bf16[256,4096]{1,0:T(8,128)(2,1)}, u32[]{:S(2)}) copy-start(bf16[256,4096]{1,0:T(8,128)(2,1)} %refs_0_.2) | copy-start | bytes 6291460
  0.0 1.4 %copy-start.1 = (bf16[256,2048]{1,0:T(8,128)(2,1)S(1)}, bf16[256,2048]{1,0:T(8,128)(2,1)}, u32[]{:S(2)}) copy-start(bf16[256,2048]{1,0:T(8,128)(2,1)} %refs_0_.3) | copy-start | bytes 3145732
  1.4 1.2 %copy-start.2 = (bf16[256,2048]{1,0:T(8,128)(2,1)S(1)}, bf16[256,2048]{1,0:T(8,128)(2,1)}, u32[]{:S(2)}) copy-start(bf16[256,2048]{1,0:T(8,128)(2,1)} %refs_1_.1) | copy-start | bytes 3145732
  2.8 3.0 %collective-permute-start.1 = (bf16[2,256,1024]{2,1,0:T(8,128)(2,1)S(1)}, bf16[2,256,1024]{2,1,0:T(8,128)(2,1)S(1)}, u32[]{:S(2)}, u32[]{:S(2)}) collective-permute-start(bf16[2,256,1024]{2,1,0:T(8,128)(2,1)S(1)} %get-tuple-element.24), channel_id=1, source_target_pairs={{0,1},{1,0},{2,3},{3,2},{4,5},{5,4},{6,7},{7,6},{8,9},{9,8},{10,11... | collective-permute-start | bytes 3145736 | tf_op jit(solution)/shard_map/ppermute | solution.py:21
  6.0 15.0 %collective-permute-start.2 = (bf16[2,512,256]{2,1,0:T(8,128)(2,1)S(1)}, bf16[2,512,256]{2,1,0:T(8,128)(2,1)S(1)}, u32[]{:S(2)}, u32[]{:S(2)}) collective-permute-start(bf16[2,512,256]{2,1,0:T(8,128)(2,1)S(1)} %get-tuple-element.25.own.rest_0_), channel_id=1, source_target_pairs={{0,4},{1,5},{2,6},{3,7},{4,8},{5,9},{6,10},{7,11},{8,12},{9,13},{1... | collective-permute-start | bytes 1572872 | tf_op jit(solution)/shard_map/ppermute | solution.py:21
  7.3 47.7 %collective-permute-start = (bf16[1,256,2048]{2,1,0:T(8,128)(2,1)S(1)}, bf16[1,256,2048]{2,1,0:T(8,128)(2,1)S(1)}, u32[]{:S(2)}, u32[]{:S(2)}) collective-permute-start(bf16[1,256,2048]{2,1,0:T(8,128)(2,1)S(1)} %get-tuple-element.22), channel_id=1, source_target_pairs={{0,1},{1,0},{2,3},{3,2},{4,5},{5,4},{6,7},{7,6},{8,9},{9,8},{10,11... | collective-permute-start | bytes 3145736 | tf_op jit(solution)/shard_map/ppermute | solution.py:21
  7.8 24.5 %collective-permute-start.4 = (bf16[2,512,256]{2,1,0:T(8,128)(2,1)S(1)}, bf16[2,512,256]{2,1,0:T(8,128)(2,1)S(1)}, u32[]{:S(2)}, u32[]{:S(2)}) collective-permute-start(bf16[2,512,256]{2,1,0:T(8,128)(2,1)S(1)} %get-tuple-element.27.own.rest_0_), channel_id=1, source_target_pairs={{0,4},{1,5},{2,6},{3,7},{4,8},{5,9},{6,10},{7,11},{8,12},{9,13},{1... | collective-permute-start | bytes 1572872 | tf_op jit(solution)/shard_map/ppermute | solution.py:21
  9.1 34.4 %collective-permute-start.6 = (bf16[2,512,256]{2,1,0:T(8,128)(2,1)S(1)}, bf16[2,512,256]{2,1,0:T(8,128)(2,1)S(1)}, u32[]{:S(2)}, u32[]{:S(2)}) collective-permute-start(bf16[2,512,256]{2,1,0:T(8,128)(2,1)S(1)} %get-tuple-element.29.own.rest_0_), channel_id=1, source_target_pairs={{0,4},{1,5},{2,6},{3,7},{4,8},{5,9},{6,10},{7,11},{8,12},{9,13},{1... | collective-permute-start | bytes 1572872 | tf_op jit(solution)/shard_map/ppermute | solution.py:21
  10.4 44.4 %collective-permute-start.8 = (bf16[2,512,256]{2,1,0:T(8,128)(2,1)S(1)}, bf16[2,512,256]{2,1,0:T(8,128)(2,1)S(1)}, u32[]{:S(2)}, u32[]{:S(2)}) collective-permute-start(bf16[2,512,256]{2,1,0:T(8,128)(2,1)S(1)} %get-tuple-element.31.own.rest_0_), channel_id=1, source_target_pairs={{0,4},{1,5},{2,6},{3,7},{4,8},{5,9},{6,10},{7,11},{8,12},{9,13},{1... | collective-permute-start | bytes 1572872 | tf_op jit(solution)/shard_map/ppermute | solution.py:21
  21.1 34.0 %copy-start.3 = (s32[8]{0:T(128)S(1)}, s32[8]{0:T(128)}, u32[]{:S(2)}) copy-start(s32[8]{0:T(128)} %blocks.7) | copy-start | bytes 100
  21.1 34.0 %collective-permute-start.3 = (bf16[2,512,256]{2,1,0:T(8,128)(2,1)S(1)}, bf16[2,512,256]{2,1,0:T(8,128)(2,1)S(1)}, u32[]{:S(2)}, u32[]{:S(2)}) collective-permute-start(bf16[2,512,256]{2,1,0:T(8,128)(2,1)S(1)} %choose.4), channel_id=1, source_target_pairs={{0,2},{1,3},{2,0},{3,1},{4,6},{5,7},{6,4},{7,5},{8,10},{9,11},{10,... | collective-permute-start | bytes 1572872 | tf_op jit(solution)/shard_map/ppermute | solution.py:21
  32.3 30.9 %collective-permute-start.5 = (bf16[2,512,256]{2,1,0:T(8,128)(2,1)S(1)}, bf16[2,512,256]{2,1,0:T(8,128)(2,1)S(1)}, u32[]{:S(2)}, u32[]{:S(2)}) collective-permute-start(bf16[2,512,256]{2,1,0:T(8,128)(2,1)S(1)} %choose.5), channel_id=1, source_target_pairs={{0,2},{1,3},{2,0},{3,1},{4,6},{5,7},{6,4},{7,5},{8,10},{9,11},{10,... | collective-permute-start | bytes 1572872 | tf_op jit(solution)/shard_map/ppermute | solution.py:21
  43.5 26.3 %collective-permute-start.7 = (bf16[2,512,256]{2,1,0:T(8,128)(2,1)S(1)}, bf16[2,512,256]{2,1,0:T(8,128)(2,1)S(1)}, u32[]{:S(2)}, u32[]{:S(2)}) collective-permute-start(bf16[2,512,256]{2,1,0:T(8,128)(2,1)S(1)} %choose.6), channel_id=1, source_target_pairs={{0,2},{1,3},{2,0},{3,1},{4,6},{5,7},{6,4},{7,5},{8,10},{9,11},{10,... | collective-permute-start | bytes 1572872 | tf_op jit(solution)/shard_map/ppermute | solution.py:21
  54.8 22.2 %collective-permute-start.9 = (bf16[2,512,256]{2,1,0:T(8,128)(2,1)S(1)}, bf16[2,512,256]{2,1,0:T(8,128)(2,1)S(1)}, u32[]{:S(2)}, u32[]{:S(2)}) collective-permute-start(bf16[2,512,256]{2,1,0:T(8,128)(2,1)S(1)} %choose.7), channel_id=1, source_target_pairs={{0,2},{1,3},{2,0},{3,1},{4,6},{5,7},{6,4},{7,5},{8,10},{9,11},{10,... | collective-permute-start | bytes 1572872 | tf_op jit(solution)/shard_map/ppermute | solution.py:21
  61.6 21.9 %collective-permute-start.10 = (bf16[256,512]{1,0:T(8,128)(2,1)S(1)}, bf16[256,512]{1,0:T(8,128)(2,1)S(1)}, u32[]{:S(2)}, u32[]{:S(2)}) collective-permute-start(bf16[256,512]{1,0:T(8,128)(2,1)S(1)} %get-tuple-element.33), channel_id=1, source_target_pairs={{0,1},{1,0},{2,3},{3,2},{4,5},{5,4},{6,7},{7,6},{8,9},{9,8},{10,11... | collective-permute-start | bytes 786440 | tf_op jit(solution)/shard_map/ppermute | solution.py:21
  69.7 13.8 %collective-permute-start.11 = (bf16[256,512]{1,0:T(8,128)(2,1)S(1)}, bf16[256,512]{1,0:T(8,128)(2,1)S(1)}, u32[]{:S(2)}, u32[]{:S(2)}) collective-permute-start(bf16[256,512]{1,0:T(8,128)(2,1)S(1)} %get-tuple-element.34), channel_id=1, source_target_pairs={{0,1},{1,0},{2,3},{3,2},{4,5},{5,4},{6,7},{7,6},{8,9},{9,8},{10,11... | collective-permute-start | bytes 786440 | tf_op jit(solution)/shard_map/ppermute | solution.py:21
  76.4 7.2 %collective-permute-start.12 = (bf16[256,512]{1,0:T(8,128)(2,1)S(1)}, bf16[256,512]{1,0:T(8,128)(2,1)S(1)}, u32[]{:S(2)}, u32[]{:S(2)}) collective-permute-start(bf16[256,512]{1,0:T(8,128)(2,1)S(1)} %get-tuple-element.35), channel_id=1, source_target_pairs={{0,1},{1,0},{2,3},{3,2},{4,5},{5,4},{6,7},{7,6},{8,9},{9,8},{10,11... | collective-permute-start | bytes 786440 | tf_op jit(solution)/shard_map/ppermute | solution.py:21
  83.5 1.6 %collective-permute-start.13 = (bf16[256,512]{1,0:T(8,128)(2,1)S(1)}, bf16[256,512]{1,0:T(8,128)(2,1)S(1)}, u32[]{:S(2)}, u32[]{:S(2)}) collective-permute-start(bf16[256,512]{1,0:T(8,128)(2,1)S(1)} %get-tuple-element.36), channel_id=1, source_target_pairs={{0,1},{1,0},{2,3},{3,2},{4,5},{5,4},{6,7},{7,6},{8,9},{9,8},{10,11... | collective-permute-start | bytes 786440 | tf_op jit(solution)/shard_map/ppermute | solution.py:21
where the time goes:
time: 86.7 us; the launch traced here: 86.4 us
  waiting for transfers between devices  45.6 us (53%)
  Pallas kernels  28.3 us (33%)
  starting transfers between devices  9.82 us (11%)
  local copies, waits for them, and re-layouts  2.61 us (3%)
    ppermute x14, waiting for transfers between devices, shift(): return lax.ppermute(block, 'seq', pairs)  45.6 us
    pallas_call x4, Pallas kernels, attend(): pl.pallas_call(functools.partial(attend_kernel, plan), out_shape=(shape,...  26.1 us
    ppermute x14, starting transfers between devices, shift(): return lax.ppermute(block, 'seq', pairs)  9.82 us
    unnamed x8, local copies, waits for them, and re-layouts  2.61 us
  transfers between devices with their start and end apart: 14, of which 6 were waited for; matrix products, arithmetic and copies ran while one was open for 0% of the time, Pallas kernels for 31%

commit v1 on v0

v1 whole, which is shorter than its diff:
```python
import functools
import math

import jax
import jax.numpy as jnp
from jax import lax
from jax.experimental import pallas as pl
from jax.experimental.pallas import tpu as pltpu
from jax.sharding import PartitionSpec as P


DH = 128
BLK = 128
CORES = 2
SLOTS = 4
PART = 16
SCALE = 144.0 ** (-0.5)


def shift(block, pairs):
    return lax.ppermute(block, "seq", pairs)


def attend_kernel(plan, spots, blocks, q_near, q_far, *rest):
    first, heads, _, ratio, window, spans = plan
    pieces = rest[: len(spots)]
    out_near, out_far, q_buf, k_buf, v_buf, o_buf, s_buf, w_buf = rest[len(spots) :]
    rows = q_near.shape[-2]
    chip_rows = rows * CORES
    me = lax.axis_index("seq")
    core = me % CORES
    chip = me // CORES
    q_width = heads * DH * ratio
    base = spans * chip_rows
    q_cols = slice(first * DH * ratio, first * DH * ratio + q_width)
    mine = pl.multiple_of(core * rows, rows)
    other = pl.multiple_of((1 - core) * rows, rows)
    q_buf[pl.ds(mine, rows)] = q_near[0, :, q_cols]
    q_buf[pl.ds(other, rows)] = q_far[0, :, q_cols]

    def bring(piece, at, col):
        k_buf[at : at + piece.shape[1]] = piece[0, :, col : col + heads * DH]
        v_buf[at : at + piece.shape[1]] = piece[1, :, col : col + heads * DH]

    for piece, (at, col, side) in zip(pieces, spots):
        if side is None:
            bring(piece, at, col)
        else:
            pl.when(chip % 2 == side)(functools.partial(bring, piece, at, col))

    units = chip_rows // BLK
    factor = SCALE * math.log2(math.e)
    tile_rows = ratio * BLK
    keys_seen = window * BLK
    last = lax.broadcasted_iota(jnp.int32, (BLK, BLK), 1)
    row = lax.broadcasted_iota(jnp.int32, (BLK, BLK), 0)
    causal = jnp.where(last <= row, 0.0, -1e30)
    key = lax.broadcasted_iota(jnp.int32, (8, keys_seen - BLK), 1)
    ones = jnp.ones((keys_seen, DH), jnp.bfloat16)

    def keys_of(unit):
        first_key = base + (unit + 1 - window) * BLK
        return pl.ds(first_key, keys_seen)

    def score(unit, group):
        q_at = pl.ds(unit * BLK, BLK)
        tiles = [
            q_buf[q_at, (group * ratio + s) * DH : (group * ratio + s + 1) * DH]
            for s in range(ratio)
        ]
        s_buf[(unit * heads + group) % SLOTS] = lax.dot_general(
            jnp.concatenate(tiles, axis=0),
            k_buf[keys_of(unit), group * DH : (group + 1) * DH],
            (((1,), (1,)), ((), ())),
            preferred_element_type=jnp.float32,
        )

    def weigh(unit, group):
        number = chip * units + unit
        begin = jnp.int32(0)
        total = jnp.int32(0)
        for doc in range(blocks.shape[0]):
            begin = jnp.where(number >= total, total, begin)
            total = total + blocks[doc]
        hidden = (window - 1 - number + begin) * BLK
        before = jnp.where(key >= hidden, 0.0, -1e30)
        before = jnp.concatenate([before] * (PART // 8), axis=0)
        slot = (unit * heads + group) % SLOTS
        for part in range(tile_rows // PART):
            at = slice(part * PART, (part + 1) * PART)
            low = part * PART % BLK
            bias = jnp.concatenate([before, causal[low : low + PART]], axis=1)
            scores = s_buf[slot, at] * factor + bias
            top = jnp.max(scores, axis=1, keepdims=True)
            w_buf[slot, at] = jnp.exp2(scores - top).astype(jnp.bfloat16)

    def blend(unit, group):
        v_part = v_buf[keys_of(unit), group * DH : (group + 1) * DH]
        blended = jnp.dot(
            w_buf[(unit * heads + group) % SLOTS],
            jnp.concatenate([v_part, ones], axis=1),
            preferred_element_type=jnp.float32,
        )
        blended = (blended[:, :DH] / blended[:, DH:]).astype(jnp.bfloat16)
        for s in range(ratio):
            cols = slice((group * ratio + s) * DH, (group * ratio + s + 1) * DH)
            o_buf[pl.ds(unit * BLK, BLK), cols] = blended[s * BLK : (s + 1) * BLK]

    tiles = [(unit, group) for unit in range(units) for group in range(heads)]
    for step in range(len(tiles) + 2):
        if step < len(tiles):
            score(*tiles[step])
        if 0 <= step - 1 < len(tiles):
            weigh(*tiles[step - 1])
        if 0 <= step - 2:
            blend(*tiles[step - 2])
    out_near[...] = o_buf[pl.ds(mine, rows)]
    out_far[...] = o_buf[pl.ds(other, rows)]


def attend(plan, spots, blocks, q_near, q_far, pieces):
    _, heads, _, ratio, window, spans = plan
    rows = q_near.shape[-2]
    chip_rows = rows * CORES
    held = (spans + 1) * chip_rows
    kv_width = heads * DH
    q_width = kv_width * ratio
    scores = heads * ratio * chip_rows * window * BLK
    scratch_bytes = (chip_rows * q_width + held * kv_width) * 4 + SLOTS * ratio * BLK * window * BLK * 6
    near_by = pl.BlockSpec(memory_space=pltpu.VMEM)
    shape = pltpu.VMEM((rows, q_width), q_near.dtype)
    return pl.pallas_call(
        functools.partial(attend_kernel, plan, spots),
        out_shape=(shape, shape),
        in_specs=[pl.BlockSpec(memory_space=pltpu.SMEM)] + [near_by] * (2 + len(pieces)),
        out_specs=(near_by, near_by),
        scratch_shapes=[
            pltpu.VMEM((chip_rows, q_width), jnp.bfloat16),
            pltpu.VMEM((held, kv_width), jnp.bfloat16),
            pltpu.VMEM((held, kv_width), jnp.bfloat16),
            pltpu.VMEM((chip_rows, q_width), jnp.bfloat16),
            pltpu.VMEM((SLOTS, ratio * BLK, window * BLK), jnp.float32),
            pltpu.VMEM((SLOTS, ratio * BLK, window * BLK), jnp.bfloat16),
        ],
        cost_estimate=pl.CostEstimate(
            flops=4 * scores * DH,
            bytes_accessed=2 * (chip_rows * q_width * 2 + held * kv_width * 2),
            transcendentals=scores,
        ),
        compiler_params=pltpu.CompilerParams(vmem_limit_bytes=scratch_bytes + (6 << 20)),
    )(blocks, q_near, q_far, *pieces)


def place_kernel(firsts, half, ratio, *refs):
    count = len(firsts)
    out, sems = refs[2 * count :]
    core = lax.axis_index("seq") % CORES
    stores = []
    for i, first in enumerate(firsts):
        for which, piece in ((core, refs[i]), (1 - core, refs[count + i])):
            col = pl.multiple_of((which * half + first) * ratio * DH, DH)
            store = pltpu.make_async_copy(
                piece, out.at[:, pl.ds(col, piece.shape[1])], sems.at[len(stores)]
            )
            store.start()
            stores.append(store)
    for store in stores:
        store.wait()


def place(firsts, half, ratio, nears, fars, width):
    anywhere = pl.BlockSpec(memory_space=pl.ANY)
    return pl.pallas_call(
        functools.partial(place_kernel, firsts, half, ratio),
        out_shape=pltpu.HBM((nears[0].shape[0], width), nears[0].dtype),
        in_specs=[anywhere] * (2 * len(firsts)),
        out_specs=anywhere,
        scratch_shapes=[pltpu.SemaphoreType.DMA((2 * len(firsts),))],
        compiler_params=pltpu.CompilerParams(vmem_limit_bytes=1 << 20),
        name="place",
    )(*nears, *fars)


def split_kernel(arrays, widths, *refs):
    sources, far, near, sems = refs[:arrays], *refs[arrays:]
    core = lax.axis_index("seq") % CORES
    copies = []
    for which, target in ((1 - core, far), (core, near)):
        for i in range(arrays):
            col = pl.multiple_of(which * widths, DH)
            copy = pltpu.make_async_copy(
                sources[i].at[:, pl.ds(col, widths)], target.at[i], sems.at[len(copies)]
            )
            copy.start()
            copies.append(copy)
    for copy in copies:
        copy.wait()


def split(*arrays):
    rows, columns = arrays[0].shape
    width = columns // CORES
    shape = pltpu.VMEM((len(arrays), rows, width), arrays[0].dtype)
    anywhere = pl.BlockSpec(memory_space=pl.ANY)
    return pl.pallas_call(
        functools.partial(split_kernel, len(arrays), width),
        out_shape=(shape, shape),
        in_specs=[pl.BlockSpec(memory_space=pltpu.HBM)] * len(arrays),
        out_specs=(anywhere, anywhere),
        scratch_shapes=[pltpu.SemaphoreType.DMA((CORES * len(arrays),))],
        compiler_params=pltpu.CompilerParams(vmem_limit_bytes=1 << 20),
        name="split",
    )(*arrays)


def merge_kernel(slots, near, far, *outs):
    core = lax.axis_index("seq") % CORES
    rows = near.shape[1]

    def fill(shards):
        for (begin, col), out in zip(slots, outs):
            end = begin + out.shape[1]
            for shard, source in enumerate(shards):
                low, high = max(begin, shard * rows), min(end, (shard + 1) * rows)
                if low < high:
                    out[:, low - begin : high - begin] = source[
                        :, low - shard * rows : high - shard * rows, col : col + out.shape[2]
                    ]

    pl.when(core == 0)(functools.partial(fill, (near, far)))
    pl.when(core == 1)(functools.partial(fill, (far, near)))


def merge(shapes, near, far):
    near_by = pl.BlockSpec(memory_space=pltpu.VMEM)
    slots = tuple((begin, col) for begin, col, _, _ in shapes)
    return pl.pallas_call(
        functools.partial(merge_kernel, slots),
        out_shape=tuple(
            pltpu.VMEM((near.shape[0], count, width), near.dtype)
            for _, _, count, width in shapes
        ),
        in_specs=[near_by, near_by],
        out_specs=(near_by,) * len(shapes),
        compiler_params=pltpu.CompilerParams(vmem_limit_bytes=12 << 20),
        name="merge",
    )(near, far)


def choose_kernel(own, came, out):
    row = lax.axis_index("seq") // CORES % 2

    @pl.when(row == 0)
    def _():
        out[...] = own[...]

    @pl.when(row == 1)
    def _():
        out[...] = came[...]


def choose(own, came):
    near_by = pl.BlockSpec(memory_space=pltpu.VMEM)
    return pl.pallas_call(
        choose_kernel,
        out_shape=pltpu.VMEM(own.shape, own.dtype),
        in_specs=[near_by, near_by],
        out_specs=near_by,
        compiler_params=pltpu.CompilerParams(vmem_limit_bytes=6 << 20),
        name="choose",
    )(own, came)


def chunk_heads(half):
    sizes = [2] * (half // 2)
    return sizes + [1] * (half % 2)


def on_device(queries, keys, values, doc_blocks):
    devices = lax.axis_size("seq")
    rows = queries.shape[0]
    q_heads = queries.shape[1] // DH
    kv_heads = keys.shape[1] // DH
    ratio = q_heads // kv_heads
    half = kv_heads // CORES
    chips = devices // CORES
    chip_rows = rows * CORES
    window = rows * devices // BLK // 4
    spans = min(-(-(window - 1) * BLK // chip_rows), chips)

    partner = [(i, i ^ 1) for i in range(devices)]
    next_chip = [(i, i + CORES) for i in range(devices - CORES)]
    next_pair = [(i, i + 2 * CORES) for i in range(devices - 2 * CORES)]
    across = [(i, i ^ CORES) for i in range(devices)]

    kv_send, kv_near = split(keys, values)
    kv_far = shift(kv_send, partner)
    q_send, q_near = split(queries)
    q_far = shift(q_send, partner)

    sizes = chunk_heads(half)
    firsts = [sum(sizes[:i]) for i in range(len(sizes))]

    base = spans * chip_rows
    lead = base - (window - 1) * BLK
    paired = spans == 2 and chips % 2 == 0 and 0 < lead <= rows
    width = half * DH
    kept = lead if paired else 0
    shapes = [
        (kept, first * DH, chip_rows - kept, heads * DH) for first, heads in zip(firsts, sizes)
    ]
    leads, lead_near, lead_far = [], [], []
    parts = 2 if paired else 0
    shapes += [(0, part * width // parts, lead, width // parts) for part in range(parts)]
    merged = merge(shapes, kv_near, kv_far)
    own, leads = merged[: len(sizes)], merged[len(sizes) :]
    for part, block in enumerate(leads):
        lead_near.append(shift(block, across))
        lead_far.append(shift(lead_near[part], next_pair))

    nears, fars = [], []
    for i, (first, heads) in enumerate(zip(firsts, sizes)):
        if paired:
            two_back = shift(own[i], next_pair)
            one_back = shift(choose(own[i], two_back), across)
            part = first * DH * parts // width
            col = first * DH - part * width // parts
            pieces = [own[i], one_back, two_back, leads[part], lead_near[part], lead_far[part]]
            spots = (
                (base + lead, 0, None),
                (base - chip_rows + lead, 0, None),
                (base - 2 * chip_rows + lead, 0, None),
                (base, col, None),
                (base - chip_rows, col, 1),
                (base - chip_rows, col, 0),
            )
        else:
            pieces = [own[i]]
            for _ in range(spans):
                pieces.append(shift(pieces[-1], next_chip))
            spots = tuple((base - back * chip_rows, 0, None) for back in range(spans + 1))
        plan = (first, heads, half, ratio, window, spans)
        out_near, out_far = attend(plan, spots, doc_blocks, q_near, q_far, pieces)
        nears.append(out_near)
        fars.append(shift(out_far, partner))
    return place(firsts, half, ratio, nears, fars, queries.shape[1])


def solution(mesh):
    spec = P(("groups", "seq"), None)

    return jax.shard_map(
        on_device,
        mesh=mesh,
        in_specs=(spec, spec, spec, P("groups")),
        out_specs=spec,
        check_vma=False,
    )
```

time: 86.7 us -> 73.9 us (0.85)
  the two profiles are of different devices: /device:TPU:29 before, /device:TPU:11 now
where the time goes in v1:
time: 73.9 us; the launch traced here: 72.7 us
  starting transfers between devices  26.9 us (36%)
  waiting for transfers between devices  25.8 us (35%)
  Pallas kernels  17.1 us (23%)
  local copies, waits for them, and re-layouts  2.61 us (4%)
    ppermute x18, starting transfers between devices, shift(): return lax.ppermute(block, 'seq', pairs)  26.9 us
    ppermute x18, waiting for transfers between devices, shift(): return lax.ppermute(block, 'seq', pairs)  25.8 us
    pallas_call x4, Pallas kernels, attend(): pl.pallas_call(functools.partial(attend_kernel, plan, spots), out_shape=(...  15 us
    unnamed x8, local copies, waits for them, and re-layouts  2.61 us
  transfers between devices with their start and end apart: 18, of which 7 were waited for; matrix products, arithmetic and copies ran while one was open for 0% of the time, Pallas kernels for 21%

profile of v1, /device:TPU:11, one launch (start us, length us, event | category | flops | bytes accessed | tf_op | source)
XLA Modules:
  0.0 72.7 jit_solution(17945530041060844071)
XLA Ops:
  0.0 1.4 %copy-done.1 = bf16[256,2048]{1,0:T(8,128)(2,1)S(1)} copy-done((bf16[256,2048]{1,0:T(8,128)(2,1)S(1)}, bf16[256,2048]{1,0:T(8,128)(2,1)}, u32[]{:S(2)}) %copy-start.1) | copy-done | bytes 1048600
  1.4 1.2 %copy-done.2 = bf16[256,2048]{1,0:T(8,128)(2,1)S(1)} copy-done((bf16[256,2048]{1,0:T(8,128)(2,1)S(1)}, bf16[256,2048]{1,0:T(8,128)(2,1)}, u32[]{:S(2)}) %copy-start.2) | copy-done | bytes 1048600
  2.6 0.2 split.3
  2.8 0.7 %collective-permute-start.1 = (bf16[2,256,1024]{2,1,0:T(8,128)(2,1)S(1)}, bf16[2,256,1024]{2,1,0:T(8,128)(2,1)S(1)}, u32[]{:S(2)}, u32[]{:S(2)}) collective-permute-start(bf16[2,256,1024]{2,1,0:T(8,128)(2,1)S(1)} %get-tuple-element.26), channel_id=1, source_target_pairs={{0,1},{1,0},{2,3},{3,2},{4,5},{5,4},{6,7},{7,6},{8,9},{9,8},{10,11... | collective-permute-start | bytes 3145736 | tf_op jit(solution)/shard_map/ppermute | solution.py:21
  3.6 0.2 split.2
  3.8 0.1 collective-permute-start
  3.9 1.9 %collective-permute-done.1.far = bf16[2,256,1024]{2,1,0:T(8,128)(2,1)S(1)} collective-permute-done((bf16[2,256,1024]{2,1,0:T(8,128)(2,1)S(1)}, bf16[2,256,1024]{2,1,0:T(8,128)(2,1)S(1)}, u32[]{:S(2)}, u32[]{:S(2)}) %collective-permute-start.1) | collective-permute-done | bytes 1048608 | tf_op jit(solution)/shard_map/ppermute | solution.py:21
  5.9 0.1 merge.1
  6.0 3.2 %collective-permute-start.2 = (bf16[2,384,256]{2,1,0:T(8,128)(2,1)S(1)}, bf16[2,384,256]{2,1,0:T(8,128)(2,1)S(1)}, u32[]{:S(2)}, u32[]{:S(2)}) collective-permute-start(bf16[2,384,256]{2,1,0:T(8,128)(2,1)S(1)} %get-tuple-element.27.own.rest_0_), channel_id=1, source_target_pairs={{0,4},{1,5},{2,6},{3,7},{4,8},{5,9},{6,10},{7,11},{8,12},{9,13},{1... | collective-permute-start | bytes 1179656 | tf_op jit(solution)/shard_map/ppermute | solution.py:21
  9.2 3.2 %collective-permute-start.6 = (bf16[2,384,256]{2,1,0:T(8,128)(2,1)S(1)}, bf16[2,384,256]{2,1,0:T(8,128)(2,1)S(1)}, u32[]{:S(2)}, u32[]{:S(2)}) collective-permute-start(bf16[2,384,256]{2,1,0:T(8,128)(2,1)S(1)} %get-tuple-element.30.own.rest_0_), channel_id=1, source_target_pairs={{0,4},{1,5},{2,6},{3,7},{4,8},{5,9},{6,10},{7,11},{8,12},{9,13},{1... | collective-permute-start | bytes 1179656 | tf_op jit(solution)/shard_map/ppermute | solution.py:21
  12.4 1.9 %collective-permute-start.8 = (bf16[2,384,256]{2,1,0:T(8,128)(2,1)S(1)}, bf16[2,384,256]{2,1,0:T(8,128)(2,1)S(1)}, u32[]{:S(2)}, u32[]{:S(2)}) collective-permute-start(bf16[2,384,256]{2,1,0:T(8,128)(2,1)S(1)} %get-tuple-element.32.own.rest_0_), channel_id=1, source_target_pairs={{0,4},{1,5},{2,6},{3,7},{4,8},{5,9},{6,10},{7,11},{8,12},{9,13},{1... | collective-permute-start | bytes 1179656 | tf_op jit(solution)/shard_map/ppermute | solution.py:21
  14.4 1.3 %collective-permute-start.4 = (bf16[2,128,512]{2,1,0:T(8,128)(2,1)S(1)}, bf16[2,128,512]{2,1,0:T(8,128)(2,1)S(1)}, u32[]{:S(2)}, u32[]{:S(2)}) collective-permute-start(bf16[2,128,512]{2,1,0:T(8,128)(2,1)S(1)} %get-tuple-element.28.rest_3_), channel_id=1, source_target_pairs={{0,2},{1,3},{2,0},{3,1},{4,6},{5,7},{6,4},{7,5},{8,10},{9,11},{10,... | collective-permute-start | bytes 786440 | tf_op jit(solution)/shard_map/ppermute | solution.py:21
  15.7 2.5 %collective-permute-done.2.came.rest_2_ = bf16[2,384,256]{2,1,0:T(8,128)(2,1)S(1)} collective-permute-done((bf16[2,384,256]{2,1,0:T(8,128)(2,1)S(1)}, bf16[2,384,256]{2,1,0:T(8,128)(2,1)S(1)}, u32[]{:S(2)}, u32[]{:S(2)}) %collective-permute-start.2) | collective-permute-done | bytes 393248 | tf_op jit(solution)/shard_map/ppermute | solution.py:21
  18.1 3.3 %collective-permute-start.12 = (bf16[2,384,256]{2,1,0:T(8,128)(2,1)S(1)}, bf16[2,384,256]{2,1,0:T(8,128)(2,1)S(1)}, u32[]{:S(2)}, u32[]{:S(2)}) collective-permute-start(bf16[2,384,256]{2,1,0:T(8,128)(2,1)S(1)} %get-tuple-element.35.own.rest_0_), channel_id=1, source_target_pairs={{0,4},{1,5},{2,6},{3,7},{4,8},{5,9},{6,10},{7,11},{8,12},{9,13},{1... | collective-permute-start | bytes 1179656 | tf_op jit(solution)/shard_map/ppermute | solution.py:21
  21.5 0.1 choose.4
  21.5 0.0 collective-permute-done.q_far
  21.5 1.3 %collective-permute-start.3 = (bf16[2,384,256]{2,1,0:T(8,128)(2,1)S(1)}, bf16[2,384,256]{2,1,0:T(8,128)(2,1)S(1)}, u32[]{:S(2)}, u32[]{:S(2)}) collective-permute-start(bf16[2,384,256]{2,1,0:T(8,128)(2,1)S(1)} %choose.4), channel_id=1, source_target_pairs={{0,2},{1,3},{2,0},{3,1},{4,6},{5,7},{6,4},{7,5},{8,10},{9,11},{10,... | collective-permute-start | bytes 1179656 | tf_op jit(solution)/shard_map/ppermute | solution.py:21
  22.9 0.0 collective-permute-done.4.rest_4_
  22.9 0.2 collective-permute-start.10
  23.1 3.5 %collective-permute-done.6.came.rest_2_ = bf16[2,384,256]{2,1,0:T(8,128)(2,1)S(1)} collective-permute-done((bf16[2,384,256]{2,1,0:T(8,128)(2,1)S(1)}, bf16[2,384,256]{2,1,0:T(8,128)(2,1)S(1)}, u32[]{:S(2)}, u32[]{:S(2)}) %collective-permute-start.6) | collective-permute-done | bytes 393248 | tf_op jit(solution)/shard_map/ppermute | solution.py:21
  26.6 3.2 %collective-permute-start.5 = (bf16[2,128,512]{2,1,0:T(8,128)(2,1)S(1)}, bf16[2,128,512]{2,1,0:T(8,128)(2,1)S(1)}, u32[]{:S(2)}, u32[]{:S(2)}) collective-permute-start(bf16[2,128,512]{2,1,0:T(8,128)(2,1)S(1)} %collective-permute-done.4.rest_4_), channel_id=1, source_target_pairs={{0,4},{1,5},{2,6},{3,7},{4,8},{5,9},{6,10},{7,11},{8,12},{9,13},{1... | collective-permute-start | bytes 786440 | tf_op jit(solution)/shard_map/ppermute | solution.py:21
  29.8 0.1 choose.5
  29.8 5.2 %collective-permute-done.8.came.rest_2_ = bf16[2,384,256]{2,1,0:T(8,128)(2,1)S(1)} collective-permute-done((bf16[2,384,256]{2,1,0:T(8,128)(2,1)S(1)}, bf16[2,384,256]{2,1,0:T(8,128)(2,1)S(1)}, u32[]{:S(2)}, u32[]{:S(2)}) %collective-permute-start.8) | collective-permute-done | bytes 393248 | tf_op jit(solution)/shard_map/ppermute | solution.py:21
  35.0 1.2 %collective-permute-start.7 = (bf16[2,384,256]{2,1,0:T(8,128)(2,1)S(1)}, bf16[2,384,256]{2,1,0:T(8,128)(2,1)S(1)}, u32[]{:S(2)}, u32[]{:S(2)}) collective-permute-start(bf16[2,384,256]{2,1,0:T(8,128)(2,1)S(1)} %choose.5), channel_id=1, source_target_pairs={{0,2},{1,3},{2,0},{3,1},{4,6},{5,7},{6,4},{7,5},{8,10},{9,11},{10,... | collective-permute-start | bytes 1179656 | tf_op jit(solution)/shard_map/ppermute | solution.py:21
  36.3 7.2 %collective-permute-done.12.came.rest_2_ = bf16[2,384,256]{2,1,0:T(8,128)(2,1)S(1)} collective-permute-done((bf16[2,384,256]{2,1,0:T(8,128)(2,1)S(1)}, bf16[2,384,256]{2,1,0:T(8,128)(2,1)S(1)}, u32[]{:S(2)}, u32[]{:S(2)}) %collective-permute-start.12) | collective-permute-done | bytes 393248 | tf_op jit(solution)/shard_map/ppermute | solution.py:21
  43.4 1.2 %collective-permute-start.9 = (bf16[2,384,256]{2,1,0:T(8,128)(2,1)S(1)}, bf16[2,384,256]{2,1,0:T(8,128)(2,1)S(1)}, u32[]{:S(2)}, u32[]{:S(2)}) collective-permute-start(bf16[2,384,256]{2,1,0:T(8,128)(2,1)S(1)} %choose.6), channel_id=1, source_target_pairs={{0,2},{1,3},{2,0},{3,1},{4,6},{5,7},{6,4},{7,5},{8,10},{9,11},{10,... | collective-permute-start | bytes 1179656 | tf_op jit(solution)/shard_map/ppermute | solution.py:21
  44.7 0.0 collective-permute-done.10.rest_4_
  44.7 0.3 collective-permute-start.13
  45.0 4.0 %collective-permute-done.5.rest_5_ = bf16[2,128,512]{2,1,0:T(8,128)(2,1)S(1)} collective-permute-done((bf16[2,128,512]{2,1,0:T(8,128)(2,1)S(1)}, bf16[2,128,512]{2,1,0:T(8,128)(2,1)S(1)}, u32[]{:S(2)}, u32[]{:S(2)}) %collective-permute-start.5) | collective-permute-done | bytes 262176 | tf_op jit(solution)/shard_map/ppermute | solution.py:21
  49.0 3.2 %collective-permute-start.11 = (bf16[2,128,512]{2,1,0:T(8,128)(2,1)S(1)}, bf16[2,128,512]{2,1,0:T(8,128)(2,1)S(1)}, u32[]{:S(2)}, u32[]{:S(2)}) collective-permute-start(bf16[2,128,512]{2,1,0:T(8,128)(2,1)S(1)} %collective-permute-done.10.rest_4_), channel_id=1, source_target_pairs={{0,4},{1,5},{2,6},{3,7},{4,8},{5,9},{6,10},{7,11},{8,12},{9,13},{1... | collective-permute-start | bytes 786440 | tf_op jit(solution)/shard_map/ppermute | solution.py:21
  52.2 0.0 collective-permute-done.3.rest_1_
  52.3 3.7 %shard_map.46 = (bf16[256,512]{1,0:T(8,128)(2,1)S(1)}, bf16[256,512]{1,0:T(8,128)(2,1)S(1)}) custom-call(s32[8]{0:T(128)S(1)} %copy-done.3, bf16[1,256,2048]{2,1,0:T(8,128)(2,1)S(1)} %get-tuple-element.23.q_near, bf16[1,256,2048]{2,1,0:T(8,128)(2,1)S(1)} %collective-permute-done.q_far, bf16[2,384,256]{2,1,0:T(8,128)(2,1)S(1)} %get-tuple-element.27.own.rest_0_, ...), custom_call_target="tpu_custom_call" | custom-call | flops 1073741824 | bytes 2621440 | tf_op jit(solution)/shard_map/pallas_call | solution.py:132
  56.0 1.6 %collective-permute-start.14 = (bf16[256,512]{1,0:T(8,128)(2,1)S(1)}, bf16[256,512]{1,0:T(8,128)(2,1)S(1)}, u32[]{:S(2)}, u32[]{:S(2)}) collective-permute-start(bf16[256,512]{1,0:T(8,128)(2,1)S(1)} %get-tuple-element.37), channel_id=1, source_target_pairs={{0,1},{1,0},{2,3},{3,2},{4,5},{5,4},{6,7},{7,6},{8,9},{9,8},{10,11... | collective-permute-start | bytes 786440 | tf_op jit(solution)/shard_map/ppermute | solution.py:21
  57.6 0.0 collective-permute-done.7.rest_1_
  57.6 3.7 %shard_map.47 = (bf16[256,512]{1,0:T(8,128)(2,1)S(1)}, bf16[256,512]{1,0:T(8,128)(2,1)S(1)}) custom-call(s32[8]{0:T(128)S(1)} %copy-done.3, bf16[1,256,2048]{2,1,0:T(8,128)(2,1)S(1)} %get-tuple-element.23.q_near, bf16[1,256,2048]{2,1,0:T(8,128)(2,1)S(1)} %collective-permute-done.q_far, bf16[2,384,256]{2,1,0:T(8,128)(2,1)S(1)} %get-tuple-element.30.own.rest_0_, ...), custom_call_target="tpu_custom_call" | custom-call | flops 1073741824 | bytes 2621440 | tf_op jit(solution)/shard_map/pallas_call | solution.py:132
  61.3 0.1 collective-permute-start.15
  61.4 0.0 collective-permute-done.11.rest_5_
  61.4 0.0 collective-permute-done.9.rest_1_
  61.4 3.9 %shard_map.48 = (bf16[256,512]{1,0:T(8,128)(2,1)S(1)}, bf16[256,512]{1,0:T(8,128)(2,1)S(1)}) custom-call(s32[8]{0:T(128)S(1)} %copy-done.3, bf16[1,256,2048]{2,1,0:T(8,128)(2,1)S(1)} %get-tuple-element.23.q_near, bf16[1,256,2048]{2,1,0:T(8,128)(2,1)S(1)} %collective-permute-done.q_far, bf16[2,384,256]{2,1,0:T(8,128)(2,1)S(1)} %get-tuple-element.32.own.rest_0_, ...), custom_call_target="tpu_custom_call" | custom-call | flops 1073741824 | bytes 2621440 | tf_op jit(solution)/shard_map/pallas_call | solution.py:132
  65.3 0.5 collective-permute-start.16
  65.8 0.0 collective-permute-done.13.rest_1_
  65.8 3.7 %shard_map.49 = (bf16[256,512]{1,0:T(8,128)(2,1)S(1)}, bf16[256,512]{1,0:T(8,128)(2,1)S(1)}) custom-call(s32[8]{0:T(128)S(1)} %copy-done.3, bf16[1,256,2048]{2,1,0:T(8,128)(2,1)S(1)} %get-tuple-element.23.q_near, bf16[1,256,2048]{2,1,0:T(8,128)(2,1)S(1)} %collective-permute-done.q_far, bf16[2,384,256]{2,1,0:T(8,128)(2,1)S(1)} %get-tuple-element.35.own.rest_0_, ...), custom_call_target="tpu_custom_call" | custom-call | flops 1073741824 | bytes 2621440 | tf_op jit(solution)/shard_map/pallas_call | solution.py:132
  69.5 0.1 collective-permute-start.17
  69.6 0.0 collective-permute-done.14.refs_4_
  69.7 0.0 collective-permute-done.15.refs_5_
  69.7 0.0 collective-permute-done.16.refs_6_
  69.7 1.5 %collective-permute-done.17.refs_7_ = bf16[256,512]{1,0:T(8,128)(2,1)S(1)} collective-permute-done((bf16[256,512]{1,0:T(8,128)(2,1)S(1)}, bf16[256,512]{1,0:T(8,128)(2,1)S(1)}, u32[]{:S(2)}, u32[]{:S(2)}) %collective-permute-start.17) | collective-permute-done | bytes 262176 | tf_op jit(solution)/shard_map/ppermute | solution.py:21
  71.1 1.4 %place.1 = bf16[256,4096]{1,0:T(8,128)(2,1)} custom-call(bf16[256,512]{1,0:T(8,128)(2,1)S(1)} %get-tuple-element.29.refs_0_, bf16[256,512]{1,0:T(8,128)(2,1)S(1)} %get-tuple-element.31.refs_1_, bf16[256,512]{1,0:T(8,128)(2,1)S(1)} %get-tuple-element.34.refs_2_, bf16[256,512]{1,0:T(8,128)(2,1)S(1)} %get-tuple-element.36.refs_3_, ...), custom_call_target="tpu_custom_call" | custom-call | tf_op jit(solution)/shard_map/place/pallas_call | solution.py:173
  (8 shorter events, 0.1 us)
Async XLA Ops:
  0.0 3.6 %copy-start = (bf16[256,4096]{1,0:T(8,128)(2,1)S(1)}, bf16[256,4096]{1,0:T(8,128)(2,1)}, u32[]{:S(2)}) copy-start(bf16[256,4096]{1,0:T(8,128)(2,1)} %refs_0_.2) | copy-start | bytes 6291460
  0.0 1.4 %copy-start.1 = (bf16[256,2048]{1,0:T(8,128)(2,1)S(1)}, bf16[256,2048]{1,0:T(8,128)(2,1)}, u32[]{:S(2)}) copy-start(bf16[256,2048]{1,0:T(8,128)(2,1)} %refs_0_.3) | copy-start | bytes 3145732
  1.4 1.2 %copy-start.2 = (bf16[256,2048]{1,0:T(8,128)(2,1)S(1)}, bf16[256,2048]{1,0:T(8,128)(2,1)}, u32[]{:S(2)}) copy-start(bf16[256,2048]{1,0:T(8,128)(2,1)} %refs_1_.1) | copy-start | bytes 3145732
  2.8 3.0 %collective-permute-start.1 = (bf16[2,256,1024]{2,1,0:T(8,128)(2,1)S(1)}, bf16[2,256,1024]{2,1,0:T(8,128)(2,1)S(1)}, u32[]{:S(2)}, u32[]{:S(2)}) collective-permute-start(bf16[2,256,1024]{2,1,0:T(8,128)(2,1)S(1)} %get-tuple-element.26), channel_id=1, source_target_pairs={{0,1},{1,0},{2,3},{3,2},{4,5},{5,4},{6,7},{7,6},{8,9},{9,8},{10,11... | collective-permute-start | bytes 3145736 | tf_op jit(solution)/shard_map/ppermute | solution.py:21
  3.8 17.7 %collective-permute-start = (bf16[1,256,2048]{2,1,0:T(8,128)(2,1)S(1)}, bf16[1,256,2048]{2,1,0:T(8,128)(2,1)S(1)}, u32[]{:S(2)}, u32[]{:S(2)}) collective-permute-start(bf16[1,256,2048]{2,1,0:T(8,128)(2,1)S(1)} %get-tuple-element.24), channel_id=1, source_target_pairs={{0,1},{1,0},{2,3},{3,2},{4,5},{5,4},{6,7},{7,6},{8,9},{9,8},{10,11... | collective-permute-start | bytes 3145736 | tf_op jit(solution)/shard_map/ppermute | solution.py:21
  6.0 12.1 %collective-permute-start.2 = (bf16[2,384,256]{2,1,0:T(8,128)(2,1)S(1)}, bf16[2,384,256]{2,1,0:T(8,128)(2,1)S(1)}, u32[]{:S(2)}, u32[]{:S(2)}) collective-permute-start(bf16[2,384,256]{2,1,0:T(8,128)(2,1)S(1)} %get-tuple-element.27.own.rest_0_), channel_id=1, source_target_pairs={{0,4},{1,5},{2,6},{3,7},{4,8},{5,9},{6,10},{7,11},{8,12},{9,13},{1... | collective-permute-start | bytes 1179656 | tf_op jit(solution)/shard_map/ppermute | solution.py:21
  9.2 17.3 %collective-permute-start.6 = (bf16[2,384,256]{2,1,0:T(8,128)(2,1)S(1)}, bf16[2,384,256]{2,1,0:T(8,128)(2,1)S(1)}, u32[]{:S(2)}, u32[]{:S(2)}) collective-permute-start(bf16[2,384,256]{2,1,0:T(8,128)(2,1)S(1)} %get-tuple-element.30.own.rest_0_), channel_id=1, source_target_pairs={{0,4},{1,5},{2,6},{3,7},{4,8},{5,9},{6,10},{7,11},{8,12},{9,13},{1... | collective-permute-start | bytes 1179656 | tf_op jit(solution)/shard_map/ppermute | solution.py:21
  12.4 22.6 %collective-permute-start.8 = (bf16[2,384,256]{2,1,0:T(8,128)(2,1)S(1)}, bf16[2,384,256]{2,1,0:T(8,128)(2,1)S(1)}, u32[]{:S(2)}, u32[]{:S(2)}) collective-permute-start(bf16[2,384,256]{2,1,0:T(8,128)(2,1)S(1)} %get-tuple-element.32.own.rest_0_), channel_id=1, source_target_pairs={{0,4},{1,5},{2,6},{3,7},{4,8},{5,9},{6,10},{7,11},{8,12},{9,13},{1... | collective-permute-start | bytes 1179656 | tf_op jit(solution)/shard_map/ppermute | solution.py:21
  14.4 8.5 %collective-permute-start.4 = (bf16[2,128,512]{2,1,0:T(8,128)(2,1)S(1)}, bf16[2,128,512]{2,1,0:T(8,128)(2,1)S(1)}, u32[]{:S(2)}, u32[]{:S(2)}) collective-permute-start(bf16[2,128,512]{2,1,0:T(8,128)(2,1)S(1)} %get-tuple-element.28.rest_3_), channel_id=1, source_target_pairs={{0,2},{1,3},{2,0},{3,1},{4,6},{5,7},{6,4},{7,5},{8,10},{9,11},{10,... | collective-permute-start | bytes 786440 | tf_op jit(solution)/shard_map/ppermute | solution.py:21
  18.1 34.1 %copy-start.3 = (s32[8]{0:T(128)S(1)}, s32[8]{0:T(128)}, u32[]{:S(2)}) copy-start(s32[8]{0:T(128)} %blocks.7) | copy-start | bytes 100
  18.1 25.3 %collective-permute-start.12 = (bf16[2,384,256]{2,1,0:T(8,128)(2,1)S(1)}, bf16[2,384,256]{2,1,0:T(8,128)(2,1)S(1)}, u32[]{:S(2)}, u32[]{:S(2)}) collective-permute-start(bf16[2,384,256]{2,1,0:T(8,128)(2,1)S(1)} %get-tuple-element.35.own.rest_0_), channel_id=1, source_target_pairs={{0,4},{1,5},{2,6},{3,7},{4,8},{5,9},{6,10},{7,11},{8,12},{9,13},{1... | collective-permute-start | bytes 1179656 | tf_op jit(solution)/shard_map/ppermute | solution.py:21
  21.5 30.7 %collective-permute-start.3 = (bf16[2,384,256]{2,1,0:T(8,128)(2,1)S(1)}, bf16[2,384,256]{2,1,0:T(8,128)(2,1)S(1)}, u32[]{:S(2)}, u32[]{:S(2)}) collective-permute-start(bf16[2,384,256]{2,1,0:T(8,128)(2,1)S(1)} %choose.4), channel_id=1, source_target_pairs={{0,2},{1,3},{2,0},{3,1},{4,6},{5,7},{6,4},{7,5},{8,10},{9,11},{10,... | collective-permute-start | bytes 1179656 | tf_op jit(solution)/shard_map/ppermute | solution.py:21
  22.9 21.8 %collective-permute-start.10 = (bf16[2,128,512]{2,1,0:T(8,128)(2,1)S(1)}, bf16[2,128,512]{2,1,0:T(8,128)(2,1)S(1)}, u32[]{:S(2)}, u32[]{:S(2)}) collective-permute-start(bf16[2,128,512]{2,1,0:T(8,128)(2,1)S(1)} %get-tuple-element.33.rest_3_), channel_id=1, source_target_pairs={{0,2},{1,3},{2,0},{3,1},{4,6},{5,7},{6,4},{7,5},{8,10},{9,11},{10,... | collective-permute-start | bytes 786440 | tf_op jit(solution)/shard_map/ppermute | solution.py:21
  26.6 22.5 %collective-permute-start.5 = (bf16[2,128,512]{2,1,0:T(8,128)(2,1)S(1)}, bf16[2,128,512]{2,1,0:T(8,128)(2,1)S(1)}, u32[]{:S(2)}, u32[]{:S(2)}) collective-permute-start(bf16[2,128,512]{2,1,0:T(8,128)(2,1)S(1)} %collective-permute-done.4.rest_4_), channel_id=1, source_target_pairs={{0,4},{1,5},{2,6},{3,7},{4,8},{5,9},{6,10},{7,11},{8,12},{9,13},{1... | collective-permute-start | bytes 786440 | tf_op jit(solution)/shard_map/ppermute | solution.py:21
  35.0 22.6 %collective-permute-start.7 = (bf16[2,384,256]{2,1,0:T(8,128)(2,1)S(1)}, bf16[2,384,256]{2,1,0:T(8,128)(2,1)S(1)}, u32[]{:S(2)}, u32[]{:S(2)}) collective-permute-start(bf16[2,384,256]{2,1,0:T(8,128)(2,1)S(1)} %choose.5), channel_id=1, source_target_pairs={{0,2},{1,3},{2,0},{3,1},{4,6},{5,7},{6,4},{7,5},{8,10},{9,11},{10,... | collective-permute-start | bytes 1179656 | tf_op jit(solution)/shard_map/ppermute | solution.py:21
  43.4 18.0 %collective-permute-start.9 = (bf16[2,384,256]{2,1,0:T(8,128)(2,1)S(1)}, bf16[2,384,256]{2,1,0:T(8,128)(2,1)S(1)}, u32[]{:S(2)}, u32[]{:S(2)}) collective-permute-start(bf16[2,384,256]{2,1,0:T(8,128)(2,1)S(1)} %choose.6), channel_id=1, source_target_pairs={{0,2},{1,3},{2,0},{3,1},{4,6},{5,7},{6,4},{7,5},{8,10},{9,11},{10,... | collective-permute-start | bytes 1179656 | tf_op jit(solution)/shard_map/ppermute | solution.py:21
  44.7 21.1 %collective-permute-start.13 = (bf16[2,384,256]{2,1,0:T(8,128)(2,1)S(1)}, bf16[2,384,256]{2,1,0:T(8,128)(2,1)S(1)}, u32[]{:S(2)}, u32[]{:S(2)}) collective-permute-start(bf16[2,384,256]{2,1,0:T(8,128)(2,1)S(1)} %choose.7), channel_id=1, source_target_pairs={{0,2},{1,3},{2,0},{3,1},{4,6},{5,7},{6,4},{7,5},{8,10},{9,11},{10,... | collective-permute-start | bytes 1179656 | tf_op jit(solution)/shard_map/ppermute | solution.py:21
  49.0 12.4 %collective-permute-start.11 = (bf16[2,128,512]{2,1,0:T(8,128)(2,1)S(1)}, bf16[2,128,512]{2,1,0:T(8,128)(2,1)S(1)}, u32[]{:S(2)}, u32[]{:S(2)}) collective-permute-start(bf16[2,128,512]{2,1,0:T(8,128)(2,1)S(1)} %collective-permute-done.10.rest_4_), channel_id=1, source_target_pairs={{0,4},{1,5},{2,6},{3,7},{4,8},{5,9},{6,10},{7,11},{8,12},{9,13},{1... | collective-permute-start | bytes 786440 | tf_op jit(solution)/shard_map/ppermute | solution.py:21
  56.0 13.7 %collective-permute-start.14 = (bf16[256,512]{1,0:T(8,128)(2,1)S(1)}, bf16[256,512]{1,0:T(8,128)(2,1)S(1)}, u32[]{:S(2)}, u32[]{:S(2)}) collective-permute-start(bf16[256,512]{1,0:T(8,128)(2,1)S(1)} %get-tuple-element.37), channel_id=1, source_target_pairs={{0,1},{1,0},{2,3},{3,2},{4,5},{5,4},{6,7},{7,6},{8,9},{9,8},{10,11... | collective-permute-start | bytes 786440 | tf_op jit(solution)/shard_map/ppermute | solution.py:21
  61.3 8.3 %collective-permute-start.15 = (bf16[256,512]{1,0:T(8,128)(2,1)S(1)}, bf16[256,512]{1,0:T(8,128)(2,1)S(1)}, u32[]{:S(2)}, u32[]{:S(2)}) collective-permute-start(bf16[256,512]{1,0:T(8,128)(2,1)S(1)} %get-tuple-element.38), channel_id=1, source_target_pairs={{0,1},{1,0},{2,3},{3,2},{4,5},{5,4},{6,7},{7,6},{8,9},{9,8},{10,11... | collective-permute-start | bytes 786440 | tf_op jit(solution)/shard_map/ppermute | solution.py:21
  65.3 4.4 %collective-permute-start.16 = (bf16[256,512]{1,0:T(8,128)(2,1)S(1)}, bf16[256,512]{1,0:T(8,128)(2,1)S(1)}, u32[]{:S(2)}, u32[]{:S(2)}) collective-permute-start(bf16[256,512]{1,0:T(8,128)(2,1)S(1)} %get-tuple-element.39), channel_id=1, source_target_pairs={{0,1},{1,0},{2,3},{3,2},{4,5},{5,4},{6,7},{7,6},{8,9},{9,8},{10,11... | collective-permute-start | bytes 786440 | tf_op jit(solution)/shard_map/ppermute | solution.py:21
  69.5 1.6 %collective-permute-start.17 = (bf16[256,512]{1,0:T(8,128)(2,1)S(1)}, bf16[256,512]{1,0:T(8,128)(2,1)S(1)}, u32[]{:S(2)}, u32[]{:S(2)}) collective-permute-start(bf16[256,512]{1,0:T(8,128)(2,1)S(1)} %get-tuple-element.40), channel_id=1, source_target_pairs={{0,1},{1,0},{2,3},{3,2},{4,5},{5,4},{6,7},{7,6},{8,9},{9,8},{10,11... | collective-permute-start | bytes 786440 | tf_op jit(solution)/shard_map/ppermute | solution.py:21

commit v2 on v1

--- a/solution.py
+++ b/solution.py
@@ -13,6 +13,7 @@
 BLK = 128
 CORES = 2
 SLOTS = 4
+LIMIT = 58 << 20
 PART = 16
 SCALE = 144.0 ** (-0.5)
 
@@ -38,15 +39,20 @@
     q_buf[pl.ds(mine, rows)] = q_near[0, :, q_cols]
     q_buf[pl.ds(other, rows)] = q_far[0, :, q_cols]
 
-    def bring(piece, at, col):
-        k_buf[at : at + piece.shape[1]] = piece[0, :, col : col + heads * DH]
-        v_buf[at : at + piece.shape[1]] = piece[1, :, col : col + heads * DH]
-
-    for piece, (at, col, side) in zip(pieces, spots):
-        if side is None:
-            bring(piece, at, col)
+    def bring(piece, at, low, high, col):
+        to = slice(at, at + high - low)
+        k_buf[to] = piece[0, low:high, col : col + heads * DH]
+        v_buf[to] = piece[1, low:high, col : col + heads * DH]
+
+    tests = {"side": chip % 2, "core": core}
+    for piece, (at, low, high, col, test) in zip(pieces, spots):
+        if test is None:
+            bring(piece, at, low, high, col)
         else:
-            pl.when(chip % 2 == side)(functools.partial(bring, piece, at, col))
+            name, wanted = test
+            pl.when(tests[name] == wanted)(
+                functools.partial(bring, piece, at, low, high, col)
+            )
 
     units = chip_rows // BLK
     factor = SCALE * math.log2(math.e)
@@ -181,15 +187,17 @@
     )(*nears, *fars)
 
 
-def split_kernel(arrays, widths, *refs):
-    sources, far, near, sems = refs[:arrays], *refs[arrays:]
+def split_kernel(arrays, width, early, *refs):
+    sources, outs, sems = refs[:arrays], refs[arrays:-1], refs[-1]
     core = lax.axis_index("seq") % CORES
     copies = []
-    for which, target in ((1 - core, far), (core, near)):
+    for out, which, count in zip(
+        outs, (1 - core, core, core, 1 - core), (width, width, early, early)
+    ):
         for i in range(arrays):
-            col = pl.multiple_of(which * widths, DH)
+            col = pl.multiple_of(which * width, DH)
             copy = pltpu.make_async_copy(
-                sources[i].at[:, pl.ds(col, widths)], target.at[i], sems.at[len(copies)]
+                sources[i].at[:, pl.ds(col, count)], out.at[i], sems.at[len(copies)]
             )
             copy.start()
             copies.append(copy)
@@ -197,18 +205,20 @@
         copy.wait()
 
 
-def split(*arrays):
+def split(early, limit, *arrays):
     rows, columns = arrays[0].shape
     width = columns // CORES
-    shape = pltpu.VMEM((len(arrays), rows, width), arrays[0].dtype)
+    counts = [width] * 2 + [early] * (2 if early else 0)
     anywhere = pl.BlockSpec(memory_space=pl.ANY)
     return pl.pallas_call(
-        functools.partial(split_kernel, len(arrays), width),
-        out_shape=(shape, shape),
+        functools.partial(split_kernel, len(arrays), width, early),
+        out_shape=tuple(
+            pltpu.VMEM((len(arrays), rows, count), arrays[0].dtype) for count in counts
+        ),
         in_specs=[pl.BlockSpec(memory_space=pltpu.HBM)] * len(arrays),
-        out_specs=(anywhere, anywhere),
-        scratch_shapes=[pltpu.SemaphoreType.DMA((CORES * len(arrays),))],
-        compiler_params=pltpu.CompilerParams(vmem_limit_bytes=1 << 20),
+        out_specs=(anywhere,) * len(counts),
+        scratch_shapes=[pltpu.SemaphoreType.DMA((len(counts) * len(arrays),))],
+        compiler_params=pltpu.CompilerParams(vmem_limit_bytes=limit),
         name="split",
     )(*arrays)
 
@@ -247,8 +257,11 @@
     )(near, far)
 
 
-def choose_kernel(own, came, out):
-    row = lax.axis_index("seq") // CORES % 2
+def choose_kernel(own, *refs):
+    came, out = refs[:-1], refs[-1]
+    me = lax.axis_index("seq")
+    core = me % CORES
+    row = me // CORES % 2
 
     @pl.when(row == 0)
     def _():
@@ -256,24 +269,31 @@
 
     @pl.when(row == 1)
     def _():
-        out[...] = came[...]
-
-
-def choose(own, came):
+        if len(came) == 1:
+            out[...] = came[0][...]
+        else:
+            rows = came[0].shape[1]
+            out[:, pl.ds(pl.multiple_of(core * rows, rows), rows)] = came[0][...]
+            out[:, pl.ds(pl.multiple_of((1 - core) * rows, rows), rows)] = came[1][...]
+
+
+def choose(own, *came):
     near_by = pl.BlockSpec(memory_space=pltpu.VMEM)
     return pl.pallas_call(
         choose_kernel,
         out_shape=pltpu.VMEM(own.shape, own.dtype),
-        in_specs=[near_by, near_by],
+        in_specs=[near_by] * (1 + len(came)),
         out_specs=near_by,
         compiler_params=pltpu.CompilerParams(vmem_limit_bytes=6 << 20),
         name="choose",
-    )(own, came)
+    )(own, *came)
 
 
 def chunk_heads(half):
-    sizes = [2] * (half // 2)
-    return sizes + [1] * (half % 2)
+    sizes = []
+    while sum(sizes) + 2 < half:
+        sizes.append(2)
+    return sizes + [1] * (half - sum(sizes))
 
 
 def on_device(queries, keys, values, doc_blocks):
@@ -293,52 +313,71 @@
     next_pair = [(i, i + 2 * CORES) for i in range(devices - 2 * CORES)]
     across = [(i, i ^ CORES) for i in range(devices)]
 
-    kv_send, kv_near = split(keys, values)
-    kv_far = shift(kv_send, partner)
-    q_send, q_near = split(queries)
-    q_far = shift(q_send, partner)
-
     sizes = chunk_heads(half)
     firsts = [sum(sizes[:i]) for i in range(len(sizes))]
-
     base = spans * chip_rows
     lead = base - (window - 1) * BLK
     paired = spans == 2 and chips % 2 == 0 and 0 < lead <= rows
     width = half * DH
-    kept = lead if paired else 0
-    shapes = [
-        (kept, first * DH, chip_rows - kept, heads * DH) for first, heads in zip(firsts, sizes)
-    ]
-    leads, lead_near, lead_far = [], [], []
-    parts = 2 if paired else 0
-    shapes += [(0, part * width // parts, lead, width // parts) for part in range(parts)]
+    crossed = [(i, (i + 2 * CORES) ^ 1) for i in range(devices - 2 * CORES)]
+    early = sizes[0] * DH if paired else 0
+    kv_send, kv_near, *firstly = split(early, LIMIT, keys, values)
+    kv_far = shift(kv_send, partner)
+    if paired:
+        straight = shift(firstly[0], next_pair)
+        cross = shift(firstly[1], crossed)
+    q_send, q_near = split(0, 1 << 20, queries)
+    q_far = shift(q_send, partner)
+
+    shapes = []
+    for i, (first, heads) in enumerate(zip(firsts, sizes)):
+        low = lead if paired and i > 0 else 0
+        shapes.append((low, first * DH, chip_rows - low, heads * DH))
+    if paired:
+        shapes.append((0, early, lead, width - early))
     merged = merge(shapes, kv_near, kv_far)
-    own, leads = merged[: len(sizes)], merged[len(sizes) :]
-    for part, block in enumerate(leads):
-        lead_near.append(shift(block, across))
-        lead_far.append(shift(lead_near[part], next_pair))
+    own = merged[: len(sizes)]
+    if paired:
+        lead_near = shift(merged[-1], across)
+        lead_far = shift(lead_near, next_pair)
 
     nears, fars = [], []
     for i, (first, heads) in enumerate(zip(firsts, sizes)):
         if paired:
-            two_back = shift(own[i], next_pair)
-            one_back = shift(choose(own[i], two_back), across)
-            part = first * DH * parts // width
-            col = first * DH - part * width // parts
-            pieces = [own[i], one_back, two_back, leads[part], lead_near[part], lead_far[part]]
-            spots = (
-                (base + lead, 0, None),
-                (base - chip_rows + lead, 0, None),
-                (base - 2 * chip_rows + lead, 0, None),
-                (base, col, None),
-                (base - chip_rows, col, 1),
-                (base - chip_rows, col, 0),
-            )
+            if i == 0:
+                two_back = (straight, cross)
+            else:
+                two_back = (shift(own[i], next_pair),)
+            chosen = choose(own[i], *two_back)
+            one_back = shift(chosen, across)
+            low = shapes[i][0]
+            count = chip_rows - low
+            one, two = base - chip_rows, base - 2 * chip_rows
+            pieces = [own[i], one_back]
+            spots = ((base + low, 0, count, 0, None), (one + low, 0, count, 0, None))
+            if i == 0:
+                for core, (same, other) in enumerate(((two, two + rows), (two + rows, two))):
+                    pieces += [straight, cross]
+                    spots += (
+                        (same, 0, rows, 0, ("core", core)),
+                        (other, 0, rows, 0, ("core", core)),
+                    )
+            else:
+                pieces += [*two_back, merged[-1], lead_near, lead_far]
+                col = first * DH - early
+                spots += (
+                    (two + low, 0, count, 0, None),
+                    (base, 0, lead, col, None),
+                    (one, 0, lead, col, ("side", 1)),
+                    (one, 0, lead, col, ("side", 0)),
+                )
         else:
             pieces = [own[i]]
             for _ in range(spans):
                 pieces.append(shift(pieces[-1], next_chip))
-            spots = tuple((base - back * chip_rows, 0, None) for back in range(spans + 1))
+            spots = tuple(
+                (base - back * chip_rows, 0, chip_rows, 0, None) for back in range(spans + 1)
+            )
         plan = (first, heads, half, ratio, window, spans)
         out_near, out_far = attend(plan, spots, doc_blocks, q_near, q_far, pieces)
         nears.append(out_near)

time: 73.9 us -> 76.7 us (1.038); the launches traced: 72.7 us -> 76.3 us
  starting transfers between devices: 26.9 us -> 36.2 us
  waiting for transfers between devices: 25.8 us -> 19.9 us
  Pallas kernels: 17.1 us -> 19.8 us
  local copies, waits for them, and re-layouts: 2.61 us -> 0.01 us
    ppermute x18 -> x20, starting transfers between devices: 26.9 us -> 36.2 us  [shift(): return lax.ppermute(block, 'seq', pairs)]
    ppermute x18 -> x20, waiting for transfers between devices: 25.8 us -> 19.9 us  [shift(): return lax.ppermute(block, 'seq', pairs)]
    unnamed x8 -> x4, local copies, waits for them, and re-layouts: 2.61 us -> 0.01 us
    pallas_call x2, Pallas kernels: 0.48 us -> 2.12 us  [split(): pl.pallas_call(functools.partial(split_kernel, len(arrays), width, early)...]
    pallas_call x4 -> x5, Pallas kernels: 15 us -> 15.9 us  [attend(): pl.pallas_call(functools.partial(attend_kernel, plan, spots), out_shape=(...]
  transfers between devices with their start and end apart: 18 -> 20, of which waited for: 7 -> 7; matrix products, arithmetic and copies ran while one was open for 0% -> 0% of each run, Pallas kernels for 21% -> 22%
where the time goes in v2:
time: 76.7 us; the launch traced here: 76.3 us
  starting transfers between devices  36.2 us (47%)
  waiting for transfers between devices  19.9 us (26%)
  Pallas kernels  19.8 us (26%)
    ppermute x20, starting transfers between devices, shift(): return lax.ppermute(block, 'seq', pairs)  36.2 us
    ppermute x20, waiting for transfers between devices, shift(): return lax.ppermute(block, 'seq', pairs)  19.9 us
    pallas_call x5, Pallas kernels, attend(): pl.pallas_call(functools.partial(attend_kernel, plan, spots), out_shape=(...  15.9 us
    pallas_call x2, Pallas kernels, split(): pl.pallas_call(functools.partial(split_kernel, len(arrays), width, early)...  2.12 us
  transfers between devices with their start and end apart: 20, of which 7 were waited for; matrix products, arithmetic and copies ran while one was open for 0% of the time, Pallas kernels for 22%

profile of v2, /device:TPU:11, one launch (start us, length us, event | category | flops | bytes accessed | tf_op | source)
XLA Modules:
  0.0 76.3 jit_solution(13127569432594751060)
XLA Ops:
  0.0 1.9 %split.3 = (bf16[2,256,1024]{2,1,0:T(8,128)(2,1)S(1)}, bf16[2,256,1024]{2,1,0:T(8,128)(2,1)S(1)}, bf16[2,256,256]{2,1,0:T(8,128)(2,1)S(1)}, bf16[2,256,256]{2,1,0:T(8,128)(2,1)S(1)}) custom-call(bf16[256,2048]{1,0:T(8,128)(2,1)} %refs_0_.3, bf16[256,2048]{1,0:T(8,128)(2,1)} %refs_1_.1), custom_call_target="tpu_custom_call" | custom-call | tf_op jit(solution)/shard_map/split/pallas_call | solution.py:213
  1.9 0.7 collective-permute-start.1
  2.6 0.2 split.2
  2.9 0.5 collective-permute-start
  3.4 3.2 %collective-permute-start.2 = (bf16[2,256,256]{2,1,0:T(8,128)(2,1)S(1)}, bf16[2,256,256]{2,1,0:T(8,128)(2,1)S(1)}, u32[]{:S(2)}, u32[]{:S(2)}) collective-permute-start(bf16[2,256,256]{2,1,0:T(8,128)(2,1)S(1)} %get-tuple-element.32), channel_id=1, source_target_pairs={{0,4},{1,5},{2,6},{3,7},{4,8},{5,9},{6,10},{7,11},{8,12},{9,13},{1... | collective-permute-start | bytes 786440 | tf_op jit(solution)/shard_map/ppermute | solution.py:22
  6.6 3.5 %collective-permute-start.3 = (bf16[2,256,256]{2,1,0:T(8,128)(2,1)S(1)}, bf16[2,256,256]{2,1,0:T(8,128)(2,1)S(1)}, u32[]{:S(2)}, u32[]{:S(2)}) collective-permute-start(bf16[2,256,256]{2,1,0:T(8,128)(2,1)S(1)} %get-tuple-element.33), channel_id=1, source_target_pairs={{0,5},{1,4},{2,7},{3,6},{4,9},{5,8},{6,11},{7,10},{8,13},{9,12},{1... | collective-permute-start | bytes 786440 | tf_op jit(solution)/shard_map/ppermute | solution.py:22
  10.0 0.0 collective-permute-done.1.far
  10.0 0.2 merge.1
  10.3 1.9 %collective-permute-start.5 = (bf16[2,384,256]{2,1,0:T(8,128)(2,1)S(1)}, bf16[2,384,256]{2,1,0:T(8,128)(2,1)S(1)}, u32[]{:S(2)}, u32[]{:S(2)}) collective-permute-start(bf16[2,384,256]{2,1,0:T(8,128)(2,1)S(1)} %get-tuple-element.35.own.rest_0_), channel_id=1, source_target_pairs={{0,4},{1,5},{2,6},{3,7},{4,8},{5,9},{6,10},{7,11},{8,12},{9,13},{1... | collective-permute-start | bytes 1179656 | tf_op jit(solution)/shard_map/ppermute | solution.py:22
  12.2 1.9 %collective-permute-start.11 = (bf16[2,384,128]{2,1,0:T(8,128)(2,1)S(1)}, bf16[2,384,128]{2,1,0:T(8,128)(2,1)S(1)}, u32[]{:S(2)}, u32[]{:S(2)}) collective-permute-start(bf16[2,384,128]{2,1,0:T(8,128)(2,1)S(1)} %get-tuple-element.40.own.rest_0_), channel_id=1, source_target_pairs={{0,4},{1,5},{2,6},{3,7},{4,8},{5,9},{6,10},{7,11},{8,12},{9,13},{1... | collective-permute-start | bytes 589832 | tf_op jit(solution)/shard_map/ppermute | solution.py:22
  14.1 0.0 collective-permute-done.2.refs_0_.rest_2_.rest_4_
  14.1 1.3 %collective-permute-start.7 = (bf16[2,128,768]{2,1,0:T(8,128)(2,1)S(1)}, bf16[2,128,768]{2,1,0:T(8,128)(2,1)S(1)}, u32[]{:S(2)}, u32[]{:S(2)}) collective-permute-start(bf16[2,128,768]{2,1,0:T(8,128)(2,1)S(1)} %get-tuple-element.36.rest_3_), channel_id=1, source_target_pairs={{0,2},{1,3},{2,0},{3,1},{4,6},{5,7},{6,4},{7,5},{8,10},{9,11},{10,... | collective-permute-start | bytes 1179656 | tf_op jit(solution)/shard_map/ppermute | solution.py:22
  15.4 4.3 %collective-permute-done.3.refs_1_.rest_3_.rest_5_ = bf16[2,256,256]{2,1,0:T(8,128)(2,1)S(1)} collective-permute-done((bf16[2,256,256]{2,1,0:T(8,128)(2,1)S(1)}, bf16[2,256,256]{2,1,0:T(8,128)(2,1)S(1)}, u32[]{:S(2)}, u32[]{:S(2)}) %collective-permute-start.3) | collective-permute-done | bytes 262176 | tf_op jit(solution)/shard_map/ppermute | solution.py:22
  19.7 3.2 %collective-permute-start.9 = (bf16[2,384,256]{2,1,0:T(8,128)(2,1)S(1)}, bf16[2,384,256]{2,1,0:T(8,128)(2,1)S(1)}, u32[]{:S(2)}, u32[]{:S(2)}) collective-permute-start(bf16[2,384,256]{2,1,0:T(8,128)(2,1)S(1)} %get-tuple-element.38.own.rest_0_), channel_id=1, source_target_pairs={{0,4},{1,5},{2,6},{3,7},{4,8},{5,9},{6,10},{7,11},{8,12},{9,13},{1... | collective-permute-start | bytes 1179656 | tf_op jit(solution)/shard_map/ppermute | solution.py:22
  22.9 0.1 choose.5
  23.0 0.0 copy-start.1
  23.0 8.3 %collective-permute-done.11.refs_0_.rest_2_ = bf16[2,384,128]{2,1,0:T(8,128)(2,1)S(1)} collective-permute-done((bf16[2,384,128]{2,1,0:T(8,128)(2,1)S(1)}, bf16[2,384,128]{2,1,0:T(8,128)(2,1)S(1)}, u32[]{:S(2)}, u32[]{:S(2)}) %collective-permute-start.11) | collective-permute-done | bytes 196640 | tf_op jit(solution)/shard_map/ppermute | solution.py:22
  31.3 1.2 %collective-permute-start.4 = (bf16[2,512,256]{2,1,0:T(8,128)(2,1)S(1)}, bf16[2,512,256]{2,1,0:T(8,128)(2,1)S(1)}, u32[]{:S(2)}, u32[]{:S(2)}) collective-permute-start(bf16[2,512,256]{2,1,0:T(8,128)(2,1)S(1)} %choose.5), channel_id=1, source_target_pairs={{0,2},{1,3},{2,0},{3,1},{4,6},{5,7},{6,4},{7,5},{8,10},{9,11},{10,... | collective-permute-start | bytes 1572872 | tf_op jit(solution)/shard_map/ppermute | solution.py:22
  32.5 0.0 collective-permute-done.5.refs_0_.rest_2_
  32.5 3.2 %collective-permute-start.13 = (bf16[2,384,128]{2,1,0:T(8,128)(2,1)S(1)}, bf16[2,384,128]{2,1,0:T(8,128)(2,1)S(1)}, u32[]{:S(2)}, u32[]{:S(2)}) collective-permute-start(bf16[2,384,128]{2,1,0:T(8,128)(2,1)S(1)} %get-tuple-element.42.own.rest_0_), channel_id=1, source_target_pairs={{0,4},{1,5},{2,6},{3,7},{4,8},{5,9},{6,10},{7,11},{8,12},{9,13},{1... | collective-permute-start | bytes 589832 | tf_op jit(solution)/shard_map/ppermute | solution.py:22
  35.7 0.1 choose.6
  35.8 0.0 collective-permute-done.7.rest_4_
  35.8 0.3 collective-permute-start.6
  36.1 3.6 %collective-permute-done.9.refs_0_.rest_2_ = bf16[2,384,256]{2,1,0:T(8,128)(2,1)S(1)} collective-permute-done((bf16[2,384,256]{2,1,0:T(8,128)(2,1)S(1)}, bf16[2,384,256]{2,1,0:T(8,128)(2,1)S(1)}, u32[]{:S(2)}, u32[]{:S(2)}) %collective-permute-start.9) | collective-permute-done | bytes 393248 | tf_op jit(solution)/shard_map/ppermute | solution.py:22
  39.7 3.2 %collective-permute-start.8 = (bf16[2,128,768]{2,1,0:T(8,128)(2,1)S(1)}, bf16[2,128,768]{2,1,0:T(8,128)(2,1)S(1)}, u32[]{:S(2)}, u32[]{:S(2)}) collective-permute-start(bf16[2,128,768]{2,1,0:T(8,128)(2,1)S(1)} %collective-permute-done.7.rest_4_), channel_id=1, source_target_pairs={{0,4},{1,5},{2,6},{3,7},{4,8},{5,9},{6,10},{7,11},{8,12},{9,13},{1... | collective-permute-start | bytes 1179656 | tf_op jit(solution)/shard_map/ppermute | solution.py:22
  42.9 0.1 choose.7
  43.0 1.0 %collective-permute-done.13.refs_0_.rest_2_ = bf16[2,384,128]{2,1,0:T(8,128)(2,1)S(1)} collective-permute-done((bf16[2,384,128]{2,1,0:T(8,128)(2,1)S(1)}, bf16[2,384,128]{2,1,0:T(8,128)(2,1)S(1)}, u32[]{:S(2)}, u32[]{:S(2)}) %collective-permute-start.13) | collective-permute-done | bytes 196640 | tf_op jit(solution)/shard_map/ppermute | solution.py:22
  43.9 1.2 %collective-permute-start.10 = (bf16[2,384,256]{2,1,0:T(8,128)(2,1)S(1)}, bf16[2,384,256]{2,1,0:T(8,128)(2,1)S(1)}, u32[]{:S(2)}, u32[]{:S(2)}) collective-permute-start(bf16[2,384,256]{2,1,0:T(8,128)(2,1)S(1)} %choose.7), channel_id=1, source_target_pairs={{0,2},{1,3},{2,0},{3,1},{4,6},{5,7},{6,4},{7,5},{8,10},{9,11},{10,... | collective-permute-start | bytes 1179656 | tf_op jit(solution)/shard_map/ppermute | solution.py:22
  45.3 0.3 collective-permute-start.12
  45.6 1.2 %collective-permute-start.14 = (bf16[2,384,128]{2,1,0:T(8,128)(2,1)S(1)}, bf16[2,384,128]{2,1,0:T(8,128)(2,1)S(1)}, u32[]{:S(2)}, u32[]{:S(2)}) collective-permute-start(bf16[2,384,128]{2,1,0:T(8,128)(2,1)S(1)} %choose.9), channel_id=1, source_target_pairs={{0,2},{1,3},{2,0},{3,1},{4,6},{5,7},{6,4},{7,5},{8,10},{9,11},{10,... | collective-permute-start | bytes 589832 | tf_op jit(solution)/shard_map/ppermute | solution.py:22
  46.8 3.7 %shard_map.46 = (bf16[256,512]{1,0:T(8,128)(2,1)S(1)}, bf16[256,512]{1,0:T(8,128)(2,1)S(1)}) custom-call(s32[8]{0:T(128)S(1)} %copy-done.1, bf16[1,256,2048]{2,1,0:T(8,128)(2,1)S(1)} %get-tuple-element.27.q_near, bf16[1,256,2048]{2,1,0:T(8,128)(2,1)S(1)} %collective-permute-done.q_far, bf16[2,512,256]{2,1,0:T(8,128)(2,1)S(1)} %get-tuple-element.31.own.rest_0_, ...), custom_call_target="tpu_custom_call" | custom-call | flops 1073741824 | bytes 2621440 | tf_op jit(solution)/shard_map/pallas_call | solution.py:138
  50.5 1.2 %collective-permute-done.6.rest_1_ = bf16[2,384,256]{2,1,0:T(8,128)(2,1)S(1)} collective-permute-done((bf16[2,384,256]{2,1,0:T(8,128)(2,1)S(1)}, bf16[2,384,256]{2,1,0:T(8,128)(2,1)S(1)}, u32[]{:S(2)}, u32[]{:S(2)}) %collective-permute-start.6) | collective-permute-done | bytes 393248 | tf_op jit(solution)/shard_map/ppermute | solution.py:22
  51.7 4.3 %collective-permute-start.15 = (bf16[256,512]{1,0:T(8,128)(2,1)S(1)}, bf16[256,512]{1,0:T(8,128)(2,1)S(1)}, u32[]{:S(2)}, u32[]{:S(2)}) collective-permute-start(bf16[256,512]{1,0:T(8,128)(2,1)S(1)} %get-tuple-element.44), channel_id=1, source_target_pairs={{0,1},{1,0},{2,3},{3,2},{4,5},{5,4},{6,7},{7,6},{8,9},{9,8},{10,11... | collective-permute-start | bytes 786440 | tf_op jit(solution)/shard_map/ppermute | solution.py:22
  56.0 3.7 %shard_map.47 = (bf16[256,512]{1,0:T(8,128)(2,1)S(1)}, bf16[256,512]{1,0:T(8,128)(2,1)S(1)}) custom-call(s32[8]{0:T(128)S(1)} %copy-done.1, bf16[1,256,2048]{2,1,0:T(8,128)(2,1)S(1)} %get-tuple-element.27.q_near, bf16[1,256,2048]{2,1,0:T(8,128)(2,1)S(1)} %collective-permute-done.q_far, bf16[2,384,256]{2,1,0:T(8,128)(2,1)S(1)} %get-tuple-element.35.own.rest_0_, ...), custom_call_target="tpu_custom_call" | custom-call | flops 1073741824 | bytes 2621440 | tf_op jit(solution)/shard_map/pallas_call | solution.py:138
  59.7 0.1 collective-permute-start.16
  59.8 0.4 collective-permute-done.10.rest_1_
  60.2 3.9 %shard_map.48 = (bf16[256,512]{1,0:T(8,128)(2,1)S(1)}, bf16[256,512]{1,0:T(8,128)(2,1)S(1)}) custom-call(s32[8]{0:T(128)S(1)} %copy-done.1, bf16[1,256,2048]{2,1,0:T(8,128)(2,1)S(1)} %get-tuple-element.27.q_near, bf16[1,256,2048]{2,1,0:T(8,128)(2,1)S(1)} %collective-permute-done.q_far, bf16[2,384,256]{2,1,0:T(8,128)(2,1)S(1)} %get-tuple-element.38.own.rest_0_, ...), custom_call_target="tpu_custom_call" | custom-call | flops 1073741824 | bytes 2621440 | tf_op jit(solution)/shard_map/pallas_call | solution.py:138
  64.0 4.3 %collective-permute-start.17 = (bf16[256,512]{1,0:T(8,128)(2,1)S(1)}, bf16[256,512]{1,0:T(8,128)(2,1)S(1)}, u32[]{:S(2)}, u32[]{:S(2)}) collective-permute-start(bf16[256,512]{1,0:T(8,128)(2,1)S(1)} %get-tuple-element.46), channel_id=1, source_target_pairs={{0,1},{1,0},{2,3},{3,2},{4,5},{5,4},{6,7},{7,6},{8,9},{9,8},{10,11... | collective-permute-start | bytes 786440 | tf_op jit(solution)/shard_map/ppermute | solution.py:22
  68.4 2.3 %shard_map.49 = (bf16[256,256]{1,0:T(8,128)(2,1)S(1)}, bf16[256,256]{1,0:T(8,128)(2,1)S(1)}) custom-call(s32[8]{0:T(128)S(1)} %copy-done.1, bf16[1,256,2048]{2,1,0:T(8,128)(2,1)S(1)} %get-tuple-element.27.q_near, bf16[1,256,2048]{2,1,0:T(8,128)(2,1)S(1)} %collective-permute-done.q_far, bf16[2,384,128]{2,1,0:T(8,128)(2,1)S(1)} %get-tuple-element.40.own.rest_0_, ...), custom_call_target="tpu_custom_call" | custom-call | flops 536870912 | bytes 1310720 | tf_op jit(solution)/shard_map/pallas_call | solution.py:138
  70.7 0.3 collective-permute-start.18
  71.0 0.0 collective-permute-done.14.rest_1_
  71.0 2.3 %shard_map.50 = (bf16[256,256]{1,0:T(8,128)(2,1)S(1)}, bf16[256,256]{1,0:T(8,128)(2,1)S(1)}) custom-call(s32[8]{0:T(128)S(1)} %copy-done.1, bf16[1,256,2048]{2,1,0:T(8,128)(2,1)S(1)} %get-tuple-element.27.q_near, bf16[1,256,2048]{2,1,0:T(8,128)(2,1)S(1)} %collective-permute-done.q_far, bf16[2,384,128]{2,1,0:T(8,128)(2,1)S(1)} %get-tuple-element.42.own.rest_0_, ...), custom_call_target="tpu_custom_call" | custom-call | flops 536870912 | bytes 1310720 | tf_op jit(solution)/shard_map/pallas_call | solution.py:138
  73.3 0.3 collective-permute-start.19
  73.6 0.0 collective-permute-done.18.refs_8_
  73.6 1.1 %collective-permute-done.19.refs_9_ = bf16[256,256]{1,0:T(8,128)(2,1)S(1)} collective-permute-done((bf16[256,256]{1,0:T(8,128)(2,1)S(1)}, bf16[256,256]{1,0:T(8,128)(2,1)S(1)}, u32[]{:S(2)}, u32[]{:S(2)}) %collective-permute-start.19) | collective-permute-done | bytes 131104 | tf_op jit(solution)/shard_map/ppermute | solution.py:22
  74.7 0.0 collective-permute-done.16.refs_6_
  74.7 0.0 collective-permute-done.17.refs_7_
  74.7 1.4 %place.1 = bf16[256,4096]{1,0:T(8,128)(2,1)} custom-call(bf16[256,512]{1,0:T(8,128)(2,1)S(1)} %get-tuple-element.34.refs_0_, bf16[256,512]{1,0:T(8,128)(2,1)S(1)} %get-tuple-element.37.refs_1_, bf16[256,512]{1,0:T(8,128)(2,1)S(1)} %get-tuple-element.39.refs_2_, bf16[256,256]{1,0:T(8,128)(2,1)S(1)} %get-tuple-element.41.refs_3_, ...), custom_call_target="tpu_custom_call" | custom-call | tf_op jit(solution)/shard_map/place/pallas_call | solution.py:179
  (10 shorter events, 0.1 us)
Async XLA Ops:
  0.0 2.6 %copy-start = (bf16[256,4096]{1,0:T(8,128)(2,1)S(1)}, bf16[256,4096]{1,0:T(8,128)(2,1)}, u32[]{:S(2)}) copy-start(bf16[256,4096]{1,0:T(8,128)(2,1)} %refs_0_.2) | copy-start | bytes 6291460
  1.9 8.2 %collective-permute-start.1 = (bf16[2,256,1024]{2,1,0:T(8,128)(2,1)S(1)}, bf16[2,256,1024]{2,1,0:T(8,128)(2,1)S(1)}, u32[]{:S(2)}, u32[]{:S(2)}) collective-permute-start(bf16[2,256,1024]{2,1,0:T(8,128)(2,1)S(1)} %get-tuple-element.30), channel_id=1, source_target_pairs={{0,1},{1,0},{2,3},{3,2},{4,5},{5,4},{6,7},{7,6},{8,9},{9,8},{10,11... | collective-permute-start | bytes 3145736 | tf_op jit(solution)/shard_map/ppermute | solution.py:22
  2.9 42.4 %collective-permute-start = (bf16[1,256,2048]{2,1,0:T(8,128)(2,1)S(1)}, bf16[1,256,2048]{2,1,0:T(8,128)(2,1)S(1)}, u32[]{:S(2)}, u32[]{:S(2)}) collective-permute-start(bf16[1,256,2048]{2,1,0:T(8,128)(2,1)S(1)} %get-tuple-element.28), channel_id=1, source_target_pairs={{0,1},{1,0},{2,3},{3,2},{4,5},{5,4},{6,7},{7,6},{8,9},{9,8},{10,11... | collective-permute-start | bytes 3145736 | tf_op jit(solution)/shard_map/ppermute | solution.py:22
  3.4 10.8 %collective-permute-start.2 = (bf16[2,256,256]{2,1,0:T(8,128)(2,1)S(1)}, bf16[2,256,256]{2,1,0:T(8,128)(2,1)S(1)}, u32[]{:S(2)}, u32[]{:S(2)}) collective-permute-start(bf16[2,256,256]{2,1,0:T(8,128)(2,1)S(1)} %get-tuple-element.32), channel_id=1, source_target_pairs={{0,4},{1,5},{2,6},{3,7},{4,8},{5,9},{6,10},{7,11},{8,12},{9,13},{1... | collective-permute-start | bytes 786440 | tf_op jit(solution)/shard_map/ppermute | solution.py:22
  6.6 13.2 %collective-permute-start.3 = (bf16[2,256,256]{2,1,0:T(8,128)(2,1)S(1)}, bf16[2,256,256]{2,1,0:T(8,128)(2,1)S(1)}, u32[]{:S(2)}, u32[]{:S(2)}) collective-permute-start(bf16[2,256,256]{2,1,0:T(8,128)(2,1)S(1)} %get-tuple-element.33), channel_id=1, source_target_pairs={{0,5},{1,4},{2,7},{3,6},{4,9},{5,8},{6,11},{7,10},{8,13},{9,12},{1... | collective-permute-start | bytes 786440 | tf_op jit(solution)/shard_map/ppermute | solution.py:22
  10.3 22.3 %collective-permute-start.5 = (bf16[2,384,256]{2,1,0:T(8,128)(2,1)S(1)}, bf16[2,384,256]{2,1,0:T(8,128)(2,1)S(1)}, u32[]{:S(2)}, u32[]{:S(2)}) collective-permute-start(bf16[2,384,256]{2,1,0:T(8,128)(2,1)S(1)} %get-tuple-element.35.own.rest_0_), channel_id=1, source_target_pairs={{0,4},{1,5},{2,6},{3,7},{4,8},{5,9},{6,10},{7,11},{8,12},{9,13},{1... | collective-permute-start | bytes 1179656 | tf_op jit(solution)/shard_map/ppermute | solution.py:22
  12.2 19.1 %collective-permute-start.11 = (bf16[2,384,128]{2,1,0:T(8,128)(2,1)S(1)}, bf16[2,384,128]{2,1,0:T(8,128)(2,1)S(1)}, u32[]{:S(2)}, u32[]{:S(2)}) collective-permute-start(bf16[2,384,128]{2,1,0:T(8,128)(2,1)S(1)} %get-tuple-element.40.own.rest_0_), channel_id=1, source_target_pairs={{0,4},{1,5},{2,6},{3,7},{4,8},{5,9},{6,10},{7,11},{8,12},{9,13},{1... | collective-permute-start | bytes 589832 | tf_op jit(solution)/shard_map/ppermute | solution.py:22
  14.1 21.7 %collective-permute-start.7 = (bf16[2,128,768]{2,1,0:T(8,128)(2,1)S(1)}, bf16[2,128,768]{2,1,0:T(8,128)(2,1)S(1)}, u32[]{:S(2)}, u32[]{:S(2)}) collective-permute-start(bf16[2,128,768]{2,1,0:T(8,128)(2,1)S(1)} %get-tuple-element.36.rest_3_), channel_id=1, source_target_pairs={{0,2},{1,3},{2,0},{3,1},{4,6},{5,7},{6,4},{7,5},{8,10},{9,11},{10,... | collective-permute-start | bytes 1179656 | tf_op jit(solution)/shard_map/ppermute | solution.py:22
  19.7 20.0 %collective-permute-start.9 = (bf16[2,384,256]{2,1,0:T(8,128)(2,1)S(1)}, bf16[2,384,256]{2,1,0:T(8,128)(2,1)S(1)}, u32[]{:S(2)}, u32[]{:S(2)}) collective-permute-start(bf16[2,384,256]{2,1,0:T(8,128)(2,1)S(1)} %get-tuple-element.38.own.rest_0_), channel_id=1, source_target_pairs={{0,4},{1,5},{2,6},{3,7},{4,8},{5,9},{6,10},{7,11},{8,12},{9,13},{1... | collective-permute-start | bytes 1179656 | tf_op jit(solution)/shard_map/ppermute | solution.py:22
  23.0 23.8 %copy-start.1 = (s32[8]{0:T(128)S(1)}, s32[8]{0:T(128)}, u32[]{:S(2)}) copy-start(s32[8]{0:T(128)} %blocks.9) | copy-start | bytes 100
  31.3 14.2 %collective-permute-start.4 = (bf16[2,512,256]{2,1,0:T(8,128)(2,1)S(1)}, bf16[2,512,256]{2,1,0:T(8,128)(2,1)S(1)}, u32[]{:S(2)}, u32[]{:S(2)}) collective-permute-start(bf16[2,512,256]{2,1,0:T(8,128)(2,1)S(1)} %choose.5), channel_id=1, source_target_pairs={{0,2},{1,3},{2,0},{3,1},{4,6},{5,7},{6,4},{7,5},{8,10},{9,11},{10,... | collective-permute-start | bytes 1572872 | tf_op jit(solution)/shard_map/ppermute | solution.py:22
  32.5 11.4 %collective-permute-start.13 = (bf16[2,384,128]{2,1,0:T(8,128)(2,1)S(1)}, bf16[2,384,128]{2,1,0:T(8,128)(2,1)S(1)}, u32[]{:S(2)}, u32[]{:S(2)}) collective-permute-start(bf16[2,384,128]{2,1,0:T(8,128)(2,1)S(1)} %get-tuple-element.42.own.rest_0_), channel_id=1, source_target_pairs={{0,4},{1,5},{2,6},{3,7},{4,8},{5,9},{6,10},{7,11},{8,12},{9,13},{1... | collective-permute-start | bytes 589832 | tf_op jit(solution)/shard_map/ppermute | solution.py:22
  35.8 15.9 %collective-permute-start.6 = (bf16[2,384,256]{2,1,0:T(8,128)(2,1)S(1)}, bf16[2,384,256]{2,1,0:T(8,128)(2,1)S(1)}, u32[]{:S(2)}, u32[]{:S(2)}) collective-permute-start(bf16[2,384,256]{2,1,0:T(8,128)(2,1)S(1)} %choose.6), channel_id=1, source_target_pairs={{0,2},{1,3},{2,0},{3,1},{4,6},{5,7},{6,4},{7,5},{8,10},{9,11},{10,... | collective-permute-start | bytes 1179656 | tf_op jit(solution)/shard_map/ppermute | solution.py:22
  39.7 16.3 %collective-permute-start.8 = (bf16[2,128,768]{2,1,0:T(8,128)(2,1)S(1)}, bf16[2,128,768]{2,1,0:T(8,128)(2,1)S(1)}, u32[]{:S(2)}, u32[]{:S(2)}) collective-permute-start(bf16[2,128,768]{2,1,0:T(8,128)(2,1)S(1)} %collective-permute-done.7.rest_4_), channel_id=1, source_target_pairs={{0,4},{1,5},{2,6},{3,7},{4,8},{5,9},{6,10},{7,11},{8,12},{9,13},{1... | collective-permute-start | bytes 1179656 | tf_op jit(solution)/shard_map/ppermute | solution.py:22
  43.9 16.2 %collective-permute-start.10 = (bf16[2,384,256]{2,1,0:T(8,128)(2,1)S(1)}, bf16[2,384,256]{2,1,0:T(8,128)(2,1)S(1)}, u32[]{:S(2)}, u32[]{:S(2)}) collective-permute-start(bf16[2,384,256]{2,1,0:T(8,128)(2,1)S(1)} %choose.7), channel_id=1, source_target_pairs={{0,2},{1,3},{2,0},{3,1},{4,6},{5,7},{6,4},{7,5},{8,10},{9,11},{10,... | collective-permute-start | bytes 1179656 | tf_op jit(solution)/shard_map/ppermute | solution.py:22
  45.3 23.1 %collective-permute-start.12 = (bf16[2,384,128]{2,1,0:T(8,128)(2,1)S(1)}, bf16[2,384,128]{2,1,0:T(8,128)(2,1)S(1)}, u32[]{:S(2)}, u32[]{:S(2)}) collective-permute-start(bf16[2,384,128]{2,1,0:T(8,128)(2,1)S(1)} %choose.8), channel_id=1, source_target_pairs={{0,2},{1,3},{2,0},{3,1},{4,6},{5,7},{6,4},{7,5},{8,10},{9,11},{10,... | collective-permute-start | bytes 589832 | tf_op jit(solution)/shard_map/ppermute | solution.py:22
  45.6 25.4 %collective-permute-start.14 = (bf16[2,384,128]{2,1,0:T(8,128)(2,1)S(1)}, bf16[2,384,128]{2,1,0:T(8,128)(2,1)S(1)}, u32[]{:S(2)}, u32[]{:S(2)}) collective-permute-start(bf16[2,384,128]{2,1,0:T(8,128)(2,1)S(1)} %choose.9), channel_id=1, source_target_pairs={{0,2},{1,3},{2,0},{3,1},{4,6},{5,7},{6,4},{7,5},{8,10},{9,11},{10,... | collective-permute-start | bytes 589832 | tf_op jit(solution)/shard_map/ppermute | solution.py:22
  51.7 21.9 %collective-permute-start.15 = (bf16[256,512]{1,0:T(8,128)(2,1)S(1)}, bf16[256,512]{1,0:T(8,128)(2,1)S(1)}, u32[]{:S(2)}, u32[]{:S(2)}) collective-permute-start(bf16[256,512]{1,0:T(8,128)(2,1)S(1)} %get-tuple-element.44), channel_id=1, source_target_pairs={{0,1},{1,0},{2,3},{3,2},{4,5},{5,4},{6,7},{7,6},{8,9},{9,8},{10,11... | collective-permute-start | bytes 786440 | tf_op jit(solution)/shard_map/ppermute | solution.py:22
  59.7 15.0 %collective-permute-start.16 = (bf16[256,512]{1,0:T(8,128)(2,1)S(1)}, bf16[256,512]{1,0:T(8,128)(2,1)S(1)}, u32[]{:S(2)}, u32[]{:S(2)}) collective-permute-start(bf16[256,512]{1,0:T(8,128)(2,1)S(1)} %get-tuple-element.45), channel_id=1, source_target_pairs={{0,1},{1,0},{2,3},{3,2},{4,5},{5,4},{6,7},{7,6},{8,9},{9,8},{10,11... | collective-permute-start | bytes 786440 | tf_op jit(solution)/shard_map/ppermute | solution.py:22
  64.0 10.7 %collective-permute-start.17 = (bf16[256,512]{1,0:T(8,128)(2,1)S(1)}, bf16[256,512]{1,0:T(8,128)(2,1)S(1)}, u32[]{:S(2)}, u32[]{:S(2)}) collective-permute-start(bf16[256,512]{1,0:T(8,128)(2,1)S(1)} %get-tuple-element.46), channel_id=1, source_target_pairs={{0,1},{1,0},{2,3},{3,2},{4,5},{5,4},{6,7},{7,6},{8,9},{9,8},{10,11... | collective-permute-start | bytes 786440 | tf_op jit(solution)/shard_map/ppermute | solution.py:22
  70.7 2.9 %collective-permute-start.18 = (bf16[256,256]{1,0:T(8,128)(2,1)S(1)}, bf16[256,256]{1,0:T(8,128)(2,1)S(1)}, u32[]{:S(2)}, u32[]{:S(2)}) collective-permute-start(bf16[256,256]{1,0:T(8,128)(2,1)S(1)} %get-tuple-element.47), channel_id=1, source_target_pairs={{0,1},{1,0},{2,3},{3,2},{4,5},{5,4},{6,7},{7,6},{8,9},{9,8},{10,11... | collective-permute-start | bytes 393224 | tf_op jit(solution)/shard_map/ppermute | solution.py:22
  73.3 1.4 %collective-permute-start.19 = (bf16[256,256]{1,0:T(8,128)(2,1)S(1)}, bf16[256,256]{1,0:T(8,128)(2,1)S(1)}, u32[]{:S(2)}, u32[]{:S(2)}) collective-permute-start(bf16[256,256]{1,0:T(8,128)(2,1)S(1)} %get-tuple-element.48), channel_id=1, source_target_pairs={{0,1},{1,0},{2,3},{3,2},{4,5},{5,4},{6,7},{7,6},{8,9},{9,8},{10,11... | collective-permute-start | bytes 393224 | tf_op jit(solution)/shard_map/ppermute | solution.py:22

commit v3 on v2

--- a/solution.py
+++ b/solution.py
@@ -290,10 +290,9 @@
 
 
 def chunk_heads(half):
-    sizes = []
-    while sum(sizes) + 2 < half:
-        sizes.append(2)
-    return sizes + [1] * (half - sum(sizes))
+    if half < 4:
+        return [1] * half
+    return [1] + [2] * ((half - 2) // 2) + [1] * (half % 2 + 1)
 
 
 def on_device(queries, keys, values, doc_blocks):
@@ -310,7 +309,7 @@
 
     partner = [(i, i ^ 1) for i in range(devices)]
     next_chip = [(i, i + CORES) for i in range(devices - CORES)]
-    next_pair = [(i, i + 2 * CORES) for i in range(devices - 2 * CORES)]
+    next_pair = [(i, (i + 2 * CORES) % devices) for i in range(devices)]
     across = [(i, i ^ CORES) for i in range(devices)]
 
     sizes = chunk_heads(half)
@@ -318,8 +317,7 @@
     base = spans * chip_rows
     lead = base - (window - 1) * BLK
     paired = spans == 2 and chips % 2 == 0 and 0 < lead <= rows
-    width = half * DH
-    crossed = [(i, (i + 2 * CORES) ^ 1) for i in range(devices - 2 * CORES)]
+    crossed = [(i, (i + 2 * CORES) % devices ^ 1) for i in range(devices)]
     early = sizes[0] * DH if paired else 0
     kv_send, kv_near, *firstly = split(early, LIMIT, keys, values)
     kv_far = shift(kv_send, partner)
@@ -333,13 +331,18 @@
     for i, (first, heads) in enumerate(zip(firsts, sizes)):
         low = lead if paired and i > 0 else 0
         shapes.append((low, first * DH, chip_rows - low, heads * DH))
+    groups = ()
     if paired:
-        shapes.append((0, early, lead, width - early))
+        middle = 1 + len(sizes) // 2
+        ends = (firsts[1], firsts[middle], half)
+        groups = tuple(zip(ends, ends[1:]))
+        shapes += [(0, low * DH, lead, (high - low) * DH) for low, high in groups]
     merged = merge(shapes, kv_near, kv_far)
     own = merged[: len(sizes)]
-    if paired:
-        lead_near = shift(merged[-1], across)
-        lead_far = shift(lead_near, next_pair)
+    leads, leads_near, leads_far = merged[len(sizes) :], [], []
+    for g, block in enumerate(leads):
+        leads_near.append(shift(block, across))
+        leads_far.append(shift(leads_near[g], next_pair))
 
     nears, fars = [], []
     for i, (first, heads) in enumerate(zip(firsts, sizes)):
@@ -363,8 +366,9 @@
                         (other, 0, rows, 0, ("core", core)),
                     )
             else:
-                pieces += [*two_back, merged[-1], lead_near, lead_far]
-                col = first * DH - early
+                g = 0 if i < middle else 1
+                pieces += [*two_back, leads[g], leads_near[g], leads_far[g]]
+                col = (first - groups[g][0]) * DH
                 spots += (
                     (two + low, 0, count, 0, None),
                     (base, 0, lead, col, None),

time: 76.7 us -> 86.1 us (1.12)
  the two profiles are of different devices: /device:TPU:11 before, /device:TPU:0 now
where the time goes in v3:
time: 86.1 us; the launch traced here: 85.9 us
  waiting for transfers between devices  49.5 us (57%)
  Pallas kernels  19.6 us (23%)
  starting transfers between devices  16.5 us (19%)
    ppermute x22, waiting for transfers between devices, shift(): return lax.ppermute(block, 'seq', pairs)  49.5 us
    ppermute x22, starting transfers between devices, shift(): return lax.ppermute(block, 'seq', pairs)  16.5 us
    pallas_call x5, Pallas kernels, attend(): pl.pallas_call(functools.partial(attend_kernel, plan, spots), out_shape=(...  15.8 us
    pallas_call x2, Pallas kernels, split(): pl.pallas_call(functools.partial(split_kernel, len(arrays), width, early)...  2 us
  transfers between devices with their start and end apart: 22, of which 12 were waited for; matrix products, arithmetic and copies ran while one was open for 0% of the time, Pallas kernels for 19%

profile of v3, /device:TPU:0, one launch (start us, length us, event | category | flops | bytes accessed | tf_op | source)
XLA Modules:
  0.0 85.9 jit_solution(5853639217923783476)
XLA Ops:
  0.0 1.8 %split.3 = (bf16[2,256,1024]{2,1,0:T(8,128)(2,1)S(1)}, bf16[2,256,1024]{2,1,0:T(8,128)(2,1)S(1)}, bf16[2,256,128]{2,1,0:T(8,128)(2,1)S(1)}, bf16[2,256,128]{2,1,0:T(8,128)(2,1)S(1)}) custom-call(bf16[256,2048]{1,0:T(8,128)(2,1)} %refs_0_.3, bf16[256,2048]{1,0:T(8,128)(2,1)} %refs_1_.1), custom_call_target="tpu_custom_call" | custom-call | tf_op jit(solution)/shard_map/split/pallas_call | solution.py:213
  1.8 0.6 collective-permute-start.1
  2.3 0.2 split.2
  2.6 0.5 collective-permute-start
  3.1 1.5 %collective-permute-done.1.far = bf16[2,256,1024]{2,1,0:T(8,128)(2,1)S(1)} collective-permute-done((bf16[2,256,1024]{2,1,0:T(8,128)(2,1)S(1)}, bf16[2,256,1024]{2,1,0:T(8,128)(2,1)S(1)}, u32[]{:S(2)}, u32[]{:S(2)}) %collective-permute-start.1) | collective-permute-done | bytes 1048608 | tf_op jit(solution)/shard_map/ppermute | solution.py:22
  4.6 0.2 merge.1
  4.8 3.0 %collective-permute-start.11 = (bf16[2,384,256]{2,1,0:T(8,128)(2,1)S(1)}, bf16[2,384,256]{2,1,0:T(8,128)(2,1)S(1)}, u32[]{:S(2)}, u32[]{:S(2)}) collective-permute-start(bf16[2,384,256]{2,1,0:T(8,128)(2,1)S(1)} %get-tuple-element.41.own.rest_0_), channel_id=1, source_target_pairs={{0,4},{1,5},{2,6},{3,7},{4,8},{5,9},{6,10},{7,11},{8,12},{9,13},{1... | collective-permute-start | bytes 1179656 | tf_op jit(solution)/shard_map/ppermute | solution.py:22
  7.8 1.6 %collective-permute-start.9 = (bf16[2,384,256]{2,1,0:T(8,128)(2,1)S(1)}, bf16[2,384,256]{2,1,0:T(8,128)(2,1)S(1)}, u32[]{:S(2)}, u32[]{:S(2)}) collective-permute-start(bf16[2,384,256]{2,1,0:T(8,128)(2,1)S(1)} %get-tuple-element.39.own.rest_0_), channel_id=1, source_target_pairs={{0,4},{1,5},{2,6},{3,7},{4,8},{5,9},{6,10},{7,11},{8,12},{9,13},{1... | collective-permute-start | bytes 1179656 | tf_op jit(solution)/shard_map/ppermute | solution.py:22
  9.4 1.6 %collective-permute-start.2 = (bf16[2,256,128]{2,1,0:T(8,128)(2,1)S(1)}, bf16[2,256,128]{2,1,0:T(8,128)(2,1)S(1)}, u32[]{:S(2)}, u32[]{:S(2)}) collective-permute-start(bf16[2,256,128]{2,1,0:T(8,128)(2,1)S(1)} %get-tuple-element.33), channel_id=1, source_target_pairs={{0,4},{1,5},{2,6},{3,7},{4,8},{5,9},{6,10},{7,11},{8,12},{9,13},{1... | collective-permute-start | bytes 393224 | tf_op jit(solution)/shard_map/ppermute | solution.py:22
  10.9 20.1 %collective-permute-done.2.refs_0_.rest_2_.rest_4_ = bf16[2,256,128]{2,1,0:T(8,128)(2,1)S(1)} collective-permute-done((bf16[2,256,128]{2,1,0:T(8,128)(2,1)S(1)}, bf16[2,256,128]{2,1,0:T(8,128)(2,1)S(1)}, u32[]{:S(2)}, u32[]{:S(2)}) %collective-permute-start.2) | collective-permute-done | bytes 131104 | tf_op jit(solution)/shard_map/ppermute | solution.py:22
  31.0 0.0 collective-permute-start.5
  31.0 1.7 %collective-permute-done.3.refs_1_.rest_3_.rest_5_ = bf16[2,256,128]{2,1,0:T(8,128)(2,1)S(1)} collective-permute-done((bf16[2,256,128]{2,1,0:T(8,128)(2,1)S(1)}, bf16[2,256,128]{2,1,0:T(8,128)(2,1)S(1)}, u32[]{:S(2)}, u32[]{:S(2)}) %collective-permute-start.3) | collective-permute-done | bytes 131104 | tf_op jit(solution)/shard_map/ppermute | solution.py:22
  32.7 1.3 %collective-permute-start.13 = (bf16[2,128,384]{2,1,0:T(8,128)(2,1)S(1)}, bf16[2,128,384]{2,1,0:T(8,128)(2,1)S(1)}, u32[]{:S(2)}, u32[]{:S(2)}) collective-permute-start(bf16[2,128,384]{2,1,0:T(8,128)(2,1)S(1)} %get-tuple-element.42.rest_3_), channel_id=1, source_target_pairs={{0,2},{1,3},{2,0},{3,1},{4,6},{5,7},{6,4},{7,5},{8,10},{9,11},{10,... | collective-permute-start | bytes 589832 | tf_op jit(solution)/shard_map/ppermute | solution.py:22
  34.0 0.0 collective-permute-done.11.refs_0_.rest_2_
  34.0 0.7 collective-permute-start.7
  34.8 0.0 copy-start.1
  34.8 0.0 collective-permute-done.q_far
  34.8 1.4 %collective-permute-start.12 = (bf16[2,384,256]{2,1,0:T(8,128)(2,1)S(1)}, bf16[2,384,256]{2,1,0:T(8,128)(2,1)S(1)}, u32[]{:S(2)}, u32[]{:S(2)}) collective-permute-start(bf16[2,384,256]{2,1,0:T(8,128)(2,1)S(1)} %choose.8), channel_id=1, source_target_pairs={{0,2},{1,3},{2,0},{3,1},{4,6},{5,7},{6,4},{7,5},{8,10},{9,11},{10,... | collective-permute-start | bytes 1179656 | tf_op jit(solution)/shard_map/ppermute | solution.py:22
  36.2 0.0 collective-permute-done.9.refs_0_.rest_2_
  36.2 0.4 collective-permute-start.15
  36.6 3.9 %collective-permute-done.13.rest_4_ = bf16[2,128,384]{2,1,0:T(8,128)(2,1)S(1)} collective-permute-done((bf16[2,128,384]{2,1,0:T(8,128)(2,1)S(1)}, bf16[2,128,384]{2,1,0:T(8,128)(2,1)S(1)}, u32[]{:S(2)}, u32[]{:S(2)}) %collective-permute-start.13) | collective-permute-done | bytes 196640 | tf_op jit(solution)/shard_map/ppermute | solution.py:22
  40.5 1.3 %collective-permute-start.10 = (bf16[2,384,256]{2,1,0:T(8,128)(2,1)S(1)}, bf16[2,384,256]{2,1,0:T(8,128)(2,1)S(1)}, u32[]{:S(2)}, u32[]{:S(2)}) collective-permute-start(bf16[2,384,256]{2,1,0:T(8,128)(2,1)S(1)} %choose.7), channel_id=1, source_target_pairs={{0,2},{1,3},{2,0},{3,1},{4,6},{5,7},{6,4},{7,5},{8,10},{9,11},{10,... | collective-permute-start | bytes 1179656 | tf_op jit(solution)/shard_map/ppermute | solution.py:22
  41.8 3.0 %collective-permute-done.5.refs_0_.rest_2_ = bf16[2,384,256]{2,1,0:T(8,128)(2,1)S(1)} collective-permute-done((bf16[2,384,256]{2,1,0:T(8,128)(2,1)S(1)}, bf16[2,384,256]{2,1,0:T(8,128)(2,1)S(1)}, u32[]{:S(2)}, u32[]{:S(2)}) %collective-permute-start.5) | collective-permute-done | bytes 393248 | tf_op jit(solution)/shard_map/ppermute | solution.py:22
  44.8 0.0 collective-permute-start.14
  44.8 3.9 %collective-permute-done.15.refs_0_.rest_2_ = bf16[2,384,128]{2,1,0:T(8,128)(2,1)S(1)} collective-permute-done((bf16[2,384,128]{2,1,0:T(8,128)(2,1)S(1)}, bf16[2,384,128]{2,1,0:T(8,128)(2,1)S(1)}, u32[]{:S(2)}, u32[]{:S(2)}) %collective-permute-start.15) | collective-permute-done | bytes 196640 | tf_op jit(solution)/shard_map/ppermute | solution.py:22
  48.7 1.7 %collective-permute-start.6 = (bf16[2,384,256]{2,1,0:T(8,128)(2,1)S(1)}, bf16[2,384,256]{2,1,0:T(8,128)(2,1)S(1)}, u32[]{:S(2)}, u32[]{:S(2)}) collective-permute-start(bf16[2,384,256]{2,1,0:T(8,128)(2,1)S(1)} %choose.6), channel_id=1, source_target_pairs={{0,2},{1,3},{2,0},{3,1},{4,6},{5,7},{6,4},{7,5},{8,10},{9,11},{10,... | collective-permute-start | bytes 1179656 | tf_op jit(solution)/shard_map/ppermute | solution.py:22
  50.5 3.8 %collective-permute-done.14.rest_5_ = bf16[2,128,384]{2,1,0:T(8,128)(2,1)S(1)} collective-permute-done((bf16[2,128,384]{2,1,0:T(8,128)(2,1)S(1)}, bf16[2,128,384]{2,1,0:T(8,128)(2,1)S(1)}, u32[]{:S(2)}, u32[]{:S(2)}) %collective-permute-start.14) | collective-permute-done | bytes 196640 | tf_op jit(solution)/shard_map/ppermute | solution.py:22
  54.4 1.5 %collective-permute-start.4 = (bf16[2,512,128]{2,1,0:T(8,128)(2,1)S(1)}, bf16[2,512,128]{2,1,0:T(8,128)(2,1)S(1)}, u32[]{:S(2)}, u32[]{:S(2)}) collective-permute-start(bf16[2,512,128]{2,1,0:T(8,128)(2,1)S(1)} %choose.5), channel_id=1, source_target_pairs={{0,2},{1,3},{2,0},{3,1},{4,6},{5,7},{6,4},{7,5},{8,10},{9,11},{10,... | collective-permute-start | bytes 786440 | tf_op jit(solution)/shard_map/ppermute | solution.py:22
  55.8 0.0 collective-permute-done.12.rest_1_
  55.8 0.6 collective-permute-start.16
  56.4 3.7 %shard_map.49 = (bf16[256,512]{1,0:T(8,128)(2,1)S(1)}, bf16[256,512]{1,0:T(8,128)(2,1)S(1)}) custom-call(s32[8]{0:T(128)S(1)} %copy-done.1, bf16[1,256,2048]{2,1,0:T(8,128)(2,1)S(1)} %get-tuple-element.28.q_near, bf16[1,256,2048]{2,1,0:T(8,128)(2,1)S(1)} %collective-permute-done.q_far, bf16[2,384,256]{2,1,0:T(8,128)(2,1)S(1)} %get-tuple-element.41.own.rest_0_, ...), custom_call_target="tpu_custom_call" | custom-call | flops 1073741824 | bytes 2621440 | tf_op jit(solution)/shard_map/pallas_call | solution.py:138
  60.1 0.1 collective-permute-start.20
  60.2 2.8 %collective-permute-done.10.rest_1_ = bf16[2,384,256]{2,1,0:T(8,128)(2,1)S(1)} collective-permute-done((bf16[2,384,256]{2,1,0:T(8,128)(2,1)S(1)}, bf16[2,384,256]{2,1,0:T(8,128)(2,1)S(1)}, u32[]{:S(2)}, u32[]{:S(2)}) %collective-permute-start.10) | collective-permute-done | bytes 393248 | tf_op jit(solution)/shard_map/ppermute | solution.py:22
  63.0 3.7 %shard_map.48 = (bf16[256,512]{1,0:T(8,128)(2,1)S(1)}, bf16[256,512]{1,0:T(8,128)(2,1)S(1)}) custom-call(s32[8]{0:T(128)S(1)} %copy-done.1, bf16[1,256,2048]{2,1,0:T(8,128)(2,1)S(1)} %get-tuple-element.28.q_near, bf16[1,256,2048]{2,1,0:T(8,128)(2,1)S(1)} %collective-permute-done.q_far, bf16[2,384,256]{2,1,0:T(8,128)(2,1)S(1)} %get-tuple-element.39.own.rest_0_, ...), custom_call_target="tpu_custom_call" | custom-call | flops 1073741824 | bytes 2621440 | tf_op jit(solution)/shard_map/pallas_call | solution.py:138
  66.7 0.1 collective-permute-start.19
  66.7 4.7 %collective-permute-done.6.rest_1_ = bf16[2,384,256]{2,1,0:T(8,128)(2,1)S(1)} collective-permute-done((bf16[2,384,256]{2,1,0:T(8,128)(2,1)S(1)}, bf16[2,384,256]{2,1,0:T(8,128)(2,1)S(1)}, u32[]{:S(2)}, u32[]{:S(2)}) %collective-permute-start.6) | collective-permute-done | bytes 393248 | tf_op jit(solution)/shard_map/ppermute | solution.py:22
  71.4 3.9 %shard_map.47 = (bf16[256,512]{1,0:T(8,128)(2,1)S(1)}, bf16[256,512]{1,0:T(8,128)(2,1)S(1)}) custom-call(s32[8]{0:T(128)S(1)} %copy-done.1, bf16[1,256,2048]{2,1,0:T(8,128)(2,1)S(1)} %get-tuple-element.28.q_near, bf16[1,256,2048]{2,1,0:T(8,128)(2,1)S(1)} %collective-permute-done.q_far, bf16[2,384,256]{2,1,0:T(8,128)(2,1)S(1)} %get-tuple-element.36.own.rest_0_, ...), custom_call_target="tpu_custom_call" | custom-call | flops 1073741824 | bytes 2621440 | tf_op jit(solution)/shard_map/pallas_call | solution.py:138
  75.3 0.1 collective-permute-start.18
  75.3 1.7 %collective-permute-done.4.rest_1_ = bf16[2,512,128]{2,1,0:T(8,128)(2,1)S(1)} collective-permute-done((bf16[2,512,128]{2,1,0:T(8,128)(2,1)S(1)}, bf16[2,512,128]{2,1,0:T(8,128)(2,1)S(1)}, u32[]{:S(2)}, u32[]{:S(2)}) %collective-permute-start.4) | collective-permute-done | bytes 262176 | tf_op jit(solution)/shard_map/ppermute | solution.py:22
  77.0 2.3 %shard_map.46 = (bf16[256,256]{1,0:T(8,128)(2,1)S(1)}, bf16[256,256]{1,0:T(8,128)(2,1)S(1)}) custom-call(s32[8]{0:T(128)S(1)} %copy-done.1, bf16[1,256,2048]{2,1,0:T(8,128)(2,1)S(1)} %get-tuple-element.28.q_near, bf16[1,256,2048]{2,1,0:T(8,128)(2,1)S(1)} %collective-permute-done.q_far, bf16[2,512,128]{2,1,0:T(8,128)(2,1)S(1)} %get-tuple-element.32.own.rest_0_, ...), custom_call_target="tpu_custom_call" | custom-call | flops 536870912 | bytes 1310720 | tf_op jit(solution)/shard_map/pallas_call | solution.py:138
  79.3 0.1 collective-permute-start.17
  79.4 1.3 %collective-permute-done.16.rest_1_ = bf16[2,384,128]{2,1,0:T(8,128)(2,1)S(1)} collective-permute-done((bf16[2,384,128]{2,1,0:T(8,128)(2,1)S(1)}, bf16[2,384,128]{2,1,0:T(8,128)(2,1)S(1)}, u32[]{:S(2)}, u32[]{:S(2)}) %collective-permute-start.16) | collective-permute-done | bytes 196640 | tf_op jit(solution)/shard_map/ppermute | solution.py:22
  80.6 2.3 %shard_map.50 = (bf16[256,256]{1,0:T(8,128)(2,1)S(1)}, bf16[256,256]{1,0:T(8,128)(2,1)S(1)}) custom-call(s32[8]{0:T(128)S(1)} %copy-done.1, bf16[1,256,2048]{2,1,0:T(8,128)(2,1)S(1)} %get-tuple-element.28.q_near, bf16[1,256,2048]{2,1,0:T(8,128)(2,1)S(1)} %collective-permute-done.q_far, bf16[2,384,128]{2,1,0:T(8,128)(2,1)S(1)} %get-tuple-element.44.own.rest_0_, ...), custom_call_target="tpu_custom_call" | custom-call | flops 536870912 | bytes 1310720 | tf_op jit(solution)/shard_map/pallas_call | solution.py:138
  82.9 0.1 collective-permute-start.21
  83.0 0.0 collective-permute-done.17.refs_5_
  83.0 1.3 %collective-permute-done.21.refs_9_ = bf16[256,256]{1,0:T(8,128)(2,1)S(1)} collective-permute-done((bf16[256,256]{1,0:T(8,128)(2,1)S(1)}, bf16[256,256]{1,0:T(8,128)(2,1)S(1)}, u32[]{:S(2)}, u32[]{:S(2)}) %collective-permute-start.21) | collective-permute-done | bytes 131104 | tf_op jit(solution)/shard_map/ppermute | solution.py:22
  84.3 0.0 collective-permute-done.19.refs_7_
  84.3 1.4 %place.1 = bf16[256,4096]{1,0:T(8,128)(2,1)} custom-call(bf16[256,256]{1,0:T(8,128)(2,1)S(1)} %get-tuple-element.35.refs_0_, bf16[256,512]{1,0:T(8,128)(2,1)S(1)} %get-tuple-element.38.refs_1_, bf16[256,512]{1,0:T(8,128)(2,1)S(1)} %get-tuple-element.40.refs_2_, bf16[256,512]{1,0:T(8,128)(2,1)S(1)} %get-tuple-element.43.refs_3_, ...), custom_call_target="tpu_custom_call" | custom-call | tf_op jit(solution)/shard_map/place/pallas_call | solution.py:179
  (14 shorter events, 0.2 us)
Async XLA Ops:
  0.0 2.3 %copy-start = (bf16[256,4096]{1,0:T(8,128)(2,1)S(1)}, bf16[256,4096]{1,0:T(8,128)(2,1)}, u32[]{:S(2)}) copy-start(bf16[256,4096]{1,0:T(8,128)(2,1)} %refs_0_.2) | copy-start | bytes 6291460
  1.8 2.8 %collective-permute-start.1 = (bf16[2,256,1024]{2,1,0:T(8,128)(2,1)S(1)}, bf16[2,256,1024]{2,1,0:T(8,128)(2,1)S(1)}, u32[]{:S(2)}, u32[]{:S(2)}) collective-permute-start(bf16[2,256,1024]{2,1,0:T(8,128)(2,1)S(1)} %get-tuple-element.31), channel_id=1, source_target_pairs={{0,1},{1,0},{2,3},{3,2},{4,5},{5,4},{6,7},{7,6},{8,9},{9,8},{10,11... | collective-permute-start | bytes 3145736 | tf_op jit(solution)/shard_map/ppermute | solution.py:22
  2.6 32.2 %collective-permute-start = (bf16[1,256,2048]{2,1,0:T(8,128)(2,1)S(1)}, bf16[1,256,2048]{2,1,0:T(8,128)(2,1)S(1)}, u32[]{:S(2)}, u32[]{:S(2)}) collective-permute-start(bf16[1,256,2048]{2,1,0:T(8,128)(2,1)S(1)} %get-tuple-element.29), channel_id=1, source_target_pairs={{0,1},{1,0},{2,3},{3,2},{4,5},{5,4},{6,7},{7,6},{8,9},{9,8},{10,11... | collective-permute-start | bytes 3145736 | tf_op jit(solution)/shard_map/ppermute | solution.py:22
  4.8 29.2 %collective-permute-start.11 = (bf16[2,384,256]{2,1,0:T(8,128)(2,1)S(1)}, bf16[2,384,256]{2,1,0:T(8,128)(2,1)S(1)}, u32[]{:S(2)}, u32[]{:S(2)}) collective-permute-start(bf16[2,384,256]{2,1,0:T(8,128)(2,1)S(1)} %get-tuple-element.41.own.rest_0_), channel_id=1, source_target_pairs={{0,4},{1,5},{2,6},{3,7},{4,8},{5,9},{6,10},{7,11},{8,12},{9,13},{1... | collective-permute-start | bytes 1179656 | tf_op jit(solution)/shard_map/ppermute | solution.py:22
  7.8 28.4 %collective-permute-start.9 = (bf16[2,384,256]{2,1,0:T(8,128)(2,1)S(1)}, bf16[2,384,256]{2,1,0:T(8,128)(2,1)S(1)}, u32[]{:S(2)}, u32[]{:S(2)}) collective-permute-start(bf16[2,384,256]{2,1,0:T(8,128)(2,1)S(1)} %get-tuple-element.39.own.rest_0_), channel_id=1, source_target_pairs={{0,4},{1,5},{2,6},{3,7},{4,8},{5,9},{6,10},{7,11},{8,12},{9,13},{1... | collective-permute-start | bytes 1179656 | tf_op jit(solution)/shard_map/ppermute | solution.py:22
  9.4 21.6 %collective-permute-start.2 = (bf16[2,256,128]{2,1,0:T(8,128)(2,1)S(1)}, bf16[2,256,128]{2,1,0:T(8,128)(2,1)S(1)}, u32[]{:S(2)}, u32[]{:S(2)}) collective-permute-start(bf16[2,256,128]{2,1,0:T(8,128)(2,1)S(1)} %get-tuple-element.33), channel_id=1, source_target_pairs={{0,4},{1,5},{2,6},{3,7},{4,8},{5,9},{6,10},{7,11},{8,12},{9,13},{1... | collective-permute-start | bytes 393224 | tf_op jit(solution)/shard_map/ppermute | solution.py:22
  10.9 21.8 %collective-permute-start.3 = (bf16[2,256,128]{2,1,0:T(8,128)(2,1)S(1)}, bf16[2,256,128]{2,1,0:T(8,128)(2,1)S(1)}, u32[]{:S(2)}, u32[]{:S(2)}) collective-permute-start(bf16[2,256,128]{2,1,0:T(8,128)(2,1)S(1)} %get-tuple-element.34), channel_id=1, source_target_pairs={{0,5},{1,4},{2,7},{3,6},{4,9},{5,8},{6,11},{7,10},{8,13},{9,12},{1... | collective-permute-start | bytes 393224 | tf_op jit(solution)/shard_map/ppermute | solution.py:22
  31.0 13.8 %collective-permute-start.5 = (bf16[2,384,256]{2,1,0:T(8,128)(2,1)S(1)}, bf16[2,384,256]{2,1,0:T(8,128)(2,1)S(1)}, u32[]{:S(2)}, u32[]{:S(2)}) collective-permute-start(bf16[2,384,256]{2,1,0:T(8,128)(2,1)S(1)} %get-tuple-element.36.own.rest_0_), channel_id=1, source_target_pairs={{0,4},{1,5},{2,6},{3,7},{4,8},{5,9},{6,10},{7,11},{8,12},{9,13},{1... | collective-permute-start | bytes 1179656 | tf_op jit(solution)/shard_map/ppermute | solution.py:22
  32.7 7.8 %collective-permute-start.13 = (bf16[2,128,384]{2,1,0:T(8,128)(2,1)S(1)}, bf16[2,128,384]{2,1,0:T(8,128)(2,1)S(1)}, u32[]{:S(2)}, u32[]{:S(2)}) collective-permute-start(bf16[2,128,384]{2,1,0:T(8,128)(2,1)S(1)} %get-tuple-element.42.rest_3_), channel_id=1, source_target_pairs={{0,2},{1,3},{2,0},{3,1},{4,6},{5,7},{6,4},{7,5},{8,10},{9,11},{10,... | collective-permute-start | bytes 589832 | tf_op jit(solution)/shard_map/ppermute | solution.py:22
  34.0 16.4 %collective-permute-start.7 = (bf16[2,128,512]{2,1,0:T(8,128)(2,1)S(1)}, bf16[2,128,512]{2,1,0:T(8,128)(2,1)S(1)}, u32[]{:S(2)}, u32[]{:S(2)}) collective-permute-start(bf16[2,128,512]{2,1,0:T(8,128)(2,1)S(1)} %get-tuple-element.37.rest_3_), channel_id=1, source_target_pairs={{0,2},{1,3},{2,0},{3,1},{4,6},{5,7},{6,4},{7,5},{8,10},{9,11},{10,... | collective-permute-start | bytes 786440 | tf_op jit(solution)/shard_map/ppermute | solution.py:22
  34.8 21.6 %copy-start.1 = (s32[8]{0:T(128)S(1)}, s32[8]{0:T(128)}, u32[]{:S(2)}) copy-start(s32[8]{0:T(128)} %blocks.9) | copy-start | bytes 100
  34.8 21.0 %collective-permute-start.12 = (bf16[2,384,256]{2,1,0:T(8,128)(2,1)S(1)}, bf16[2,384,256]{2,1,0:T(8,128)(2,1)S(1)}, u32[]{:S(2)}, u32[]{:S(2)}) collective-permute-start(bf16[2,384,256]{2,1,0:T(8,128)(2,1)S(1)} %choose.8), channel_id=1, source_target_pairs={{0,2},{1,3},{2,0},{3,1},{4,6},{5,7},{6,4},{7,5},{8,10},{9,11},{10,... | collective-permute-start | bytes 1179656 | tf_op jit(solution)/shard_map/ppermute | solution.py:22
  36.2 12.6 %collective-permute-start.15 = (bf16[2,384,128]{2,1,0:T(8,128)(2,1)S(1)}, bf16[2,384,128]{2,1,0:T(8,128)(2,1)S(1)}, u32[]{:S(2)}, u32[]{:S(2)}) collective-permute-start(bf16[2,384,128]{2,1,0:T(8,128)(2,1)S(1)} %get-tuple-element.44.own.rest_0_), channel_id=1, source_target_pairs={{0,4},{1,5},{2,6},{3,7},{4,8},{5,9},{6,10},{7,11},{8,12},{9,13},{1... | collective-permute-start | bytes 589832 | tf_op jit(solution)/shard_map/ppermute | solution.py:22
  40.5 22.5 %collective-permute-start.10 = (bf16[2,384,256]{2,1,0:T(8,128)(2,1)S(1)}, bf16[2,384,256]{2,1,0:T(8,128)(2,1)S(1)}, u32[]{:S(2)}, u32[]{:S(2)}) collective-permute-start(bf16[2,384,256]{2,1,0:T(8,128)(2,1)S(1)} %choose.7), channel_id=1, source_target_pairs={{0,2},{1,3},{2,0},{3,1},{4,6},{5,7},{6,4},{7,5},{8,10},{9,11},{10,... | collective-permute-start | bytes 1179656 | tf_op jit(solution)/shard_map/ppermute | solution.py:22
  44.8 9.6 %collective-permute-start.14 = (bf16[2,128,384]{2,1,0:T(8,128)(2,1)S(1)}, bf16[2,128,384]{2,1,0:T(8,128)(2,1)S(1)}, u32[]{:S(2)}, u32[]{:S(2)}) collective-permute-start(bf16[2,128,384]{2,1,0:T(8,128)(2,1)S(1)} %collective-permute-done.13.rest_4_), channel_id=1, source_target_pairs={{0,4},{1,5},{2,6},{3,7},{4,8},{5,9},{6,10},{7,11},{8,12},{9,13},{1... | collective-permute-start | bytes 589832 | tf_op jit(solution)/shard_map/ppermute | solution.py:22
  48.7 22.7 %collective-permute-start.6 = (bf16[2,384,256]{2,1,0:T(8,128)(2,1)S(1)}, bf16[2,384,256]{2,1,0:T(8,128)(2,1)S(1)}, u32[]{:S(2)}, u32[]{:S(2)}) collective-permute-start(bf16[2,384,256]{2,1,0:T(8,128)(2,1)S(1)} %choose.6), channel_id=1, source_target_pairs={{0,2},{1,3},{2,0},{3,1},{4,6},{5,7},{6,4},{7,5},{8,10},{9,11},{10,... | collective-permute-start | bytes 1179656 | tf_op jit(solution)/shard_map/ppermute | solution.py:22
  50.5 9.6 %collective-permute-start.8 = (bf16[2,128,512]{2,1,0:T(8,128)(2,1)S(1)}, bf16[2,128,512]{2,1,0:T(8,128)(2,1)S(1)}, u32[]{:S(2)}, u32[]{:S(2)}) collective-permute-start(bf16[2,128,512]{2,1,0:T(8,128)(2,1)S(1)} %collective-permute-done.7.rest_4_), channel_id=1, source_target_pairs={{0,4},{1,5},{2,6},{3,7},{4,8},{5,9},{6,10},{7,11},{8,12},{9,13},{1... | collective-permute-start | bytes 786440 | tf_op jit(solution)/shard_map/ppermute | solution.py:22
  54.4 22.6 %collective-permute-start.4 = (bf16[2,512,128]{2,1,0:T(8,128)(2,1)S(1)}, bf16[2,512,128]{2,1,0:T(8,128)(2,1)S(1)}, u32[]{:S(2)}, u32[]{:S(2)}) collective-permute-start(bf16[2,512,128]{2,1,0:T(8,128)(2,1)S(1)} %choose.5), channel_id=1, source_target_pairs={{0,2},{1,3},{2,0},{3,1},{4,6},{5,7},{6,4},{7,5},{8,10},{9,11},{10,... | collective-permute-start | bytes 786440 | tf_op jit(solution)/shard_map/ppermute | solution.py:22
  55.8 24.8 %collective-permute-start.16 = (bf16[2,384,128]{2,1,0:T(8,128)(2,1)S(1)}, bf16[2,384,128]{2,1,0:T(8,128)(2,1)S(1)}, u32[]{:S(2)}, u32[]{:S(2)}) collective-permute-start(bf16[2,384,128]{2,1,0:T(8,128)(2,1)S(1)} %choose.9), channel_id=1, source_target_pairs={{0,2},{1,3},{2,0},{3,1},{4,6},{5,7},{6,4},{7,5},{8,10},{9,11},{10,... | collective-permute-start | bytes 589832 | tf_op jit(solution)/shard_map/ppermute | solution.py:22
  60.1 24.2 %collective-permute-start.20 = (bf16[256,512]{1,0:T(8,128)(2,1)S(1)}, bf16[256,512]{1,0:T(8,128)(2,1)S(1)}, u32[]{:S(2)}, u32[]{:S(2)}) collective-permute-start(bf16[256,512]{1,0:T(8,128)(2,1)S(1)} %get-tuple-element.49), channel_id=1, source_target_pairs={{0,1},{1,0},{2,3},{3,2},{4,5},{5,4},{6,7},{7,6},{8,9},{9,8},{10,11... | collective-permute-start | bytes 786440 | tf_op jit(solution)/shard_map/ppermute | solution.py:22
  66.7 17.7 %collective-permute-start.19 = (bf16[256,512]{1,0:T(8,128)(2,1)S(1)}, bf16[256,512]{1,0:T(8,128)(2,1)S(1)}, u32[]{:S(2)}, u32[]{:S(2)}) collective-permute-start(bf16[256,512]{1,0:T(8,128)(2,1)S(1)} %get-tuple-element.48), channel_id=1, source_target_pairs={{0,1},{1,0},{2,3},{3,2},{4,5},{5,4},{6,7},{7,6},{8,9},{9,8},{10,11... | collective-permute-start | bytes 786440 | tf_op jit(solution)/shard_map/ppermute | solution.py:22
  75.3 9.1 %collective-permute-start.18 = (bf16[256,512]{1,0:T(8,128)(2,1)S(1)}, bf16[256,512]{1,0:T(8,128)(2,1)S(1)}, u32[]{:S(2)}, u32[]{:S(2)}) collective-permute-start(bf16[256,512]{1,0:T(8,128)(2,1)S(1)} %get-tuple-element.47), channel_id=1, source_target_pairs={{0,1},{1,0},{2,3},{3,2},{4,5},{5,4},{6,7},{7,6},{8,9},{9,8},{10,11... | collective-permute-start | bytes 786440 | tf_op jit(solution)/shard_map/ppermute | solution.py:22
  79.3 3.7 %collective-permute-start.17 = (bf16[256,256]{1,0:T(8,128)(2,1)S(1)}, bf16[256,256]{1,0:T(8,128)(2,1)S(1)}, u32[]{:S(2)}, u32[]{:S(2)}) collective-permute-start(bf16[256,256]{1,0:T(8,128)(2,1)S(1)} %get-tuple-element.46), channel_id=1, source_target_pairs={{0,1},{1,0},{2,3},{3,2},{4,5},{5,4},{6,7},{7,6},{8,9},{9,8},{10,11... | collective-permute-start | bytes 393224 | tf_op jit(solution)/shard_map/ppermute | solution.py:22
  82.9 1.4 %collective-permute-start.21 = (bf16[256,256]{1,0:T(8,128)(2,1)S(1)}, bf16[256,256]{1,0:T(8,128)(2,1)S(1)}, u32[]{:S(2)}, u32[]{:S(2)}) collective-permute-start(bf16[256,256]{1,0:T(8,128)(2,1)S(1)} %get-tuple-element.50), channel_id=1, source_target_pairs={{0,1},{1,0},{2,3},{3,2},{4,5},{5,4},{6,7},{7,6},{8,9},{9,8},{10,11... | collective-permute-start | bytes 393224 | tf_op jit(solution)/shard_map/ppermute | solution.py:22

commit v4 on v3

--- a/solution.py
+++ b/solution.py
@@ -13,6 +13,7 @@
 BLK = 128
 CORES = 2
 SLOTS = 4
+WHOLE = 2
 LIMIT = 58 << 20
 PART = 16
 SCALE = 144.0 ** (-0.5)
@@ -290,9 +291,9 @@
 
 
 def chunk_heads(half):
-    if half < 4:
+    if half < 6:
         return [1] * half
-    return [1] + [2] * ((half - 2) // 2) + [1] * (half % 2 + 1)
+    return [1, 1] + [2] * ((half - 4) // 2) + [1] * (half % 2 + 2)
 
 
 def on_device(queries, keys, values, doc_blocks):
@@ -316,7 +317,7 @@
     firsts = [sum(sizes[:i]) for i in range(len(sizes))]
     base = spans * chip_rows
     lead = base - (window - 1) * BLK
-    paired = spans == 2 and chips % 2 == 0 and 0 < lead <= rows
+    paired = spans == 2 and chips % 2 == 0 and 0 < lead <= rows and len(sizes) > WHOLE + 1
     crossed = [(i, (i + 2 * CORES) % devices ^ 1) for i in range(devices)]
     early = sizes[0] * DH if paired else 0
     kv_send, kv_near, *firstly = split(early, LIMIT, keys, values)
@@ -329,12 +330,12 @@
 
     shapes = []
     for i, (first, heads) in enumerate(zip(firsts, sizes)):
-        low = lead if paired and i > 0 else 0
+        low = lead if paired and i >= WHOLE else 0
         shapes.append((low, first * DH, chip_rows - low, heads * DH))
     groups = ()
     if paired:
-        middle = 1 + len(sizes) // 2
-        ends = (firsts[1], firsts[middle], half)
+        middle = len(sizes) // 2 + 1
+        ends = (firsts[WHOLE], firsts[middle], half)
         groups = tuple(zip(ends, ends[1:]))
         shapes += [(0, low * DH, lead, (high - low) * DH) for low, high in groups]
     merged = merge(shapes, kv_near, kv_far)
@@ -366,11 +367,13 @@
                         (other, 0, rows, 0, ("core", core)),
                     )
             else:
+                pieces += [*two_back]
+                spots += ((two + low, 0, count, 0, None),)
+            if i >= WHOLE:
                 g = 0 if i < middle else 1
-                pieces += [*two_back, leads[g], leads_near[g], leads_far[g]]
+                pieces += [leads[g], leads_near[g], leads_far[g]]
                 col = (first - groups[g][0]) * DH
                 spots += (
-                    (two + low, 0, count, 0, None),
                     (base, 0, lead, col, None),
                     (one, 0, lead, col, ("side", 1)),
                     (one, 0, lead, col, ("side", 0)),

time: 86.1 us -> 92.2 us (1.071)
  the two profiles are of different devices: /device:TPU:0 before, /device:TPU:11 now
where the time goes in v4:
time: 92.2 us; the launch traced here: 91.1 us
  waiting for transfers between devices  48.7 us (53%)
  starting transfers between devices  21.5 us (23%)
  Pallas kernels  20.5 us (22%)
    ppermute x25, waiting for transfers between devices, shift(): return lax.ppermute(block, 'seq', pairs)  48.7 us
    ppermute x25, starting transfers between devices, shift(): return lax.ppermute(block, 'seq', pairs)  21.5 us
    pallas_call x6, Pallas kernels, attend(): pl.pallas_call(functools.partial(attend_kernel, plan, spots), out_shape=(...  16.7 us
    pallas_call x2, Pallas kernels, split(): pl.pallas_call(functools.partial(split_kernel, len(arrays), width, early)...  2 us
  transfers between devices with their start and end apart: 25, of which 7 were waited for; matrix products, arithmetic and copies ran while one was open for 0% of the time, Pallas kernels for 19%

profile of v4, /device:TPU:11, one launch (start us, length us, event | category | flops | bytes accessed | tf_op | source)
XLA Modules:
  0.0 91.1 jit_solution(11075051337526185820)
XLA Ops:
  0.0 1.8 %split.3 = (bf16[2,256,1024]{2,1,0:T(8,128)(2,1)S(1)}, bf16[2,256,1024]{2,1,0:T(8,128)(2,1)S(1)}, bf16[2,256,128]{2,1,0:T(8,128)(2,1)S(1)}, bf16[2,256,128]{2,1,0:T(8,128)(2,1)S(1)}) custom-call(bf16[256,2048]{1,0:T(8,128)(2,1)} %refs_0_.3, bf16[256,2048]{1,0:T(8,128)(2,1)} %refs_1_.1), custom_call_target="tpu_custom_call" | custom-call | tf_op jit(solution)/shard_map/split/pallas_call | solution.py:214
  1.8 0.7 collective-permute-start.1
  2.5 0.2 split.2
  2.8 0.5 collective-permute-start
  3.3 1.5 %collective-permute-done.1.far = bf16[2,256,1024]{2,1,0:T(8,128)(2,1)S(1)} collective-permute-done((bf16[2,256,1024]{2,1,0:T(8,128)(2,1)S(1)}, bf16[2,256,1024]{2,1,0:T(8,128)(2,1)S(1)}, u32[]{:S(2)}, u32[]{:S(2)}) %collective-permute-start.1) | collective-permute-done | bytes 1048608 | tf_op jit(solution)/shard_map/ppermute | solution.py:23
  4.8 0.2 merge.1
  5.0 1.3 %collective-permute-start.11 = (bf16[2,384,256]{2,1,0:T(8,128)(2,1)S(1)}, bf16[2,384,256]{2,1,0:T(8,128)(2,1)S(1)}, u32[]{:S(2)}, u32[]{:S(2)}) collective-permute-start(bf16[2,384,256]{2,1,0:T(8,128)(2,1)S(1)} %get-tuple-element.44.own.rest_0_), channel_id=1, source_target_pairs={{0,4},{1,5},{2,6},{3,7},{4,8},{5,9},{6,10},{7,11},{8,12},{9,13},{1... | collective-permute-start | bytes 1179656 | tf_op jit(solution)/shard_map/ppermute | solution.py:23
  6.4 1.3 %collective-permute-start.2 = (bf16[2,256,128]{2,1,0:T(8,128)(2,1)S(1)}, bf16[2,256,128]{2,1,0:T(8,128)(2,1)S(1)}, u32[]{:S(2)}, u32[]{:S(2)}) collective-permute-start(bf16[2,256,128]{2,1,0:T(8,128)(2,1)S(1)} %get-tuple-element.36), channel_id=1, source_target_pairs={{0,4},{1,5},{2,6},{3,7},{4,8},{5,9},{6,10},{7,11},{8,12},{9,13},{1... | collective-permute-start | bytes 393224 | tf_op jit(solution)/shard_map/ppermute | solution.py:23
  7.7 0.1 collective-permute-start.7
  7.8 2.3 %collective-permute-start.3 = (bf16[2,256,128]{2,1,0:T(8,128)(2,1)S(1)}, bf16[2,256,128]{2,1,0:T(8,128)(2,1)S(1)}, u32[]{:S(2)}, u32[]{:S(2)}) collective-permute-start(bf16[2,256,128]{2,1,0:T(8,128)(2,1)S(1)} %get-tuple-element.37), channel_id=1, source_target_pairs={{0,5},{1,4},{2,7},{3,6},{4,9},{5,8},{6,11},{7,10},{8,13},{9,12},{1... | collective-permute-start | bytes 393224 | tf_op jit(solution)/shard_map/ppermute | solution.py:23
  10.0 8.2 %collective-permute-done.2.refs_0_.rest_2_.rest_4_ = bf16[2,256,128]{2,1,0:T(8,128)(2,1)S(1)} collective-permute-done((bf16[2,256,128]{2,1,0:T(8,128)(2,1)S(1)}, bf16[2,256,128]{2,1,0:T(8,128)(2,1)S(1)}, u32[]{:S(2)}, u32[]{:S(2)}) %collective-permute-start.2) | collective-permute-done | bytes 131104 | tf_op jit(solution)/shard_map/ppermute | solution.py:23
  18.2 1.3 %collective-permute-start.17 = (bf16[2,384,128]{2,1,0:T(8,128)(2,1)S(1)}, bf16[2,384,128]{2,1,0:T(8,128)(2,1)S(1)}, u32[]{:S(2)}, u32[]{:S(2)}) collective-permute-start(bf16[2,384,128]{2,1,0:T(8,128)(2,1)S(1)} %get-tuple-element.49.own.rest_0_), channel_id=1, source_target_pairs={{0,4},{1,5},{2,6},{3,7},{4,8},{5,9},{6,10},{7,11},{8,12},{9,13},{1... | collective-permute-start | bytes 589832 | tf_op jit(solution)/shard_map/ppermute | solution.py:23
  19.5 11.3 %collective-permute-done.3.refs_1_.rest_3_.rest_5_ = bf16[2,256,128]{2,1,0:T(8,128)(2,1)S(1)} collective-permute-done((bf16[2,256,128]{2,1,0:T(8,128)(2,1)S(1)}, bf16[2,256,128]{2,1,0:T(8,128)(2,1)S(1)}, u32[]{:S(2)}, u32[]{:S(2)}) %collective-permute-start.3) | collective-permute-done | bytes 131104 | tf_op jit(solution)/shard_map/ppermute | solution.py:23
  30.8 1.2 %collective-permute-start.9 = (bf16[2,128,512]{2,1,0:T(8,128)(2,1)S(1)}, bf16[2,128,512]{2,1,0:T(8,128)(2,1)S(1)}, u32[]{:S(2)}, u32[]{:S(2)}) collective-permute-start(bf16[2,128,512]{2,1,0:T(8,128)(2,1)S(1)} %get-tuple-element.42.rest_3_), channel_id=1, source_target_pairs={{0,2},{1,3},{2,0},{3,1},{4,6},{5,7},{6,4},{7,5},{8,10},{9,11},{10,... | collective-permute-start | bytes 786440 | tf_op jit(solution)/shard_map/ppermute | solution.py:23
  32.1 0.0 collective-permute-done.q_far
  32.1 1.3 %collective-permute-start.13 = (bf16[2,384,128]{2,1,0:T(8,128)(2,1)S(1)}, bf16[2,384,128]{2,1,0:T(8,128)(2,1)S(1)}, u32[]{:S(2)}, u32[]{:S(2)}) collective-permute-start(bf16[2,384,128]{2,1,0:T(8,128)(2,1)S(1)} %get-tuple-element.46.own.rest_0_), channel_id=1, source_target_pairs={{0,4},{1,5},{2,6},{3,7},{4,8},{5,9},{6,10},{7,11},{8,12},{9,13},{1... | collective-permute-start | bytes 589832 | tf_op jit(solution)/shard_map/ppermute | solution.py:23
  33.4 1.3 %collective-permute-start.5 = (bf16[2,512,128]{2,1,0:T(8,128)(2,1)S(1)}, bf16[2,512,128]{2,1,0:T(8,128)(2,1)S(1)}, u32[]{:S(2)}, u32[]{:S(2)}) collective-permute-start(bf16[2,512,128]{2,1,0:T(8,128)(2,1)S(1)} %get-tuple-element.39.own.rest_0_), channel_id=1, source_target_pairs={{0,4},{1,5},{2,6},{3,7},{4,8},{5,9},{6,10},{7,11},{8,12},{9,13},{1... | collective-permute-start | bytes 786440 | tf_op jit(solution)/shard_map/ppermute | solution.py:23
  34.7 0.0 copy-start.1
  34.7 0.0 collective-permute-done.17.refs_0_.rest_2_
  34.7 0.3 collective-permute-start.12
  35.0 0.0 collective-permute-done.7.refs_0_.rest_2_
  35.0 1.3 %collective-permute-start.4 = (bf16[2,512,128]{2,1,0:T(8,128)(2,1)S(1)}, bf16[2,512,128]{2,1,0:T(8,128)(2,1)S(1)}, u32[]{:S(2)}, u32[]{:S(2)}) collective-permute-start(bf16[2,512,128]{2,1,0:T(8,128)(2,1)S(1)} %choose.6), channel_id=1, source_target_pairs={{0,2},{1,3},{2,0},{3,1},{4,6},{5,7},{6,4},{7,5},{8,10},{9,11},{10,... | collective-permute-start | bytes 786440 | tf_op jit(solution)/shard_map/ppermute | solution.py:23
  36.4 3.1 %collective-permute-done.13.refs_0_.rest_2_ = bf16[2,384,128]{2,1,0:T(8,128)(2,1)S(1)} collective-permute-done((bf16[2,384,128]{2,1,0:T(8,128)(2,1)S(1)}, bf16[2,384,128]{2,1,0:T(8,128)(2,1)S(1)}, u32[]{:S(2)}, u32[]{:S(2)}) %collective-permute-start.13) | collective-permute-done | bytes 196640 | tf_op jit(solution)/shard_map/ppermute | solution.py:23
  39.5 0.2 collective-permute-start.8
  39.7 0.8 collective-permute-start.10
  40.5 4.6 %collective-permute-done.5.refs_0_.rest_2_ = bf16[2,512,128]{2,1,0:T(8,128)(2,1)S(1)} collective-permute-done((bf16[2,512,128]{2,1,0:T(8,128)(2,1)S(1)}, bf16[2,512,128]{2,1,0:T(8,128)(2,1)S(1)}, u32[]{:S(2)}, u32[]{:S(2)}) %collective-permute-start.5) | collective-permute-done | bytes 262176 | tf_op jit(solution)/shard_map/ppermute | solution.py:23
  45.1 0.2 collective-permute-start.15
  45.4 18.7 %collective-permute-done.15.rest_4_ = bf16[2,128,256]{2,1,0:T(8,128)(2,1)S(1)} collective-permute-done((bf16[2,128,256]{2,1,0:T(8,128)(2,1)S(1)}, bf16[2,128,256]{2,1,0:T(8,128)(2,1)S(1)}, u32[]{:S(2)}, u32[]{:S(2)}) %collective-permute-start.15) | collective-permute-done | bytes 131104 | tf_op jit(solution)/shard_map/ppermute | solution.py:23
  64.2 1.3 %collective-permute-start.16 = (bf16[2,128,256]{2,1,0:T(8,128)(2,1)S(1)}, bf16[2,128,256]{2,1,0:T(8,128)(2,1)S(1)}, u32[]{:S(2)}, u32[]{:S(2)}) collective-permute-start(bf16[2,128,256]{2,1,0:T(8,128)(2,1)S(1)} %collective-permute-done.15.rest_4_), channel_id=1, source_target_pairs={{0,4},{1,5},{2,6},{3,7},{4,8},{5,9},{6,10},{7,11},{8,12},{9,13},{1... | collective-permute-start | bytes 393224 | tf_op jit(solution)/shard_map/ppermute | solution.py:23
  65.5 0.0 collective-permute-done.4.rest_1_
  65.5 1.2 %collective-permute-start.18 = (bf16[2,384,128]{2,1,0:T(8,128)(2,1)S(1)}, bf16[2,384,128]{2,1,0:T(8,128)(2,1)S(1)}, u32[]{:S(2)}, u32[]{:S(2)}) collective-permute-start(bf16[2,384,128]{2,1,0:T(8,128)(2,1)S(1)} %choose.11), channel_id=1, source_target_pairs={{0,2},{1,3},{2,0},{3,1},{4,6},{5,7},{6,4},{7,5},{8,10},{9,11},{10,... | collective-permute-start | bytes 589832 | tf_op jit(solution)/shard_map/ppermute | solution.py:23
  66.7 2.3 %shard_map.46 = (bf16[256,256]{1,0:T(8,128)(2,1)S(1)}, bf16[256,256]{1,0:T(8,128)(2,1)S(1)}) custom-call(s32[8]{0:T(128)S(1)} %copy-done.1, bf16[1,256,2048]{2,1,0:T(8,128)(2,1)S(1)} %get-tuple-element.31.q_near, bf16[1,256,2048]{2,1,0:T(8,128)(2,1)S(1)} %collective-permute-done.q_far, bf16[2,512,128]{2,1,0:T(8,128)(2,1)S(1)} %get-tuple-element.35.own.rest_0_, ...), custom_call_target="tpu_custom_call" | custom-call | flops 536870912 | bytes 1310720 | tf_op jit(solution)/shard_map/pallas_call | solution.py:139
  69.0 0.3 collective-permute-start.14
  69.3 0.0 collective-permute-done.12.rest_1_
  69.3 1.2 %collective-permute-start.6 = (bf16[2,512,128]{2,1,0:T(8,128)(2,1)S(1)}, bf16[2,512,128]{2,1,0:T(8,128)(2,1)S(1)}, u32[]{:S(2)}, u32[]{:S(2)}) collective-permute-start(bf16[2,512,128]{2,1,0:T(8,128)(2,1)S(1)} %choose.7), channel_id=1, source_target_pairs={{0,2},{1,3},{2,0},{3,1},{4,6},{5,7},{6,4},{7,5},{8,10},{9,11},{10,... | collective-permute-start | bytes 786440 | tf_op jit(solution)/shard_map/ppermute | solution.py:23
  70.6 3.7 %shard_map.49 = (bf16[256,512]{1,0:T(8,128)(2,1)S(1)}, bf16[256,512]{1,0:T(8,128)(2,1)S(1)}) custom-call(s32[8]{0:T(128)S(1)} %copy-done.1, bf16[1,256,2048]{2,1,0:T(8,128)(2,1)S(1)} %get-tuple-element.31.q_near, bf16[1,256,2048]{2,1,0:T(8,128)(2,1)S(1)} %collective-permute-done.q_far, bf16[2,384,256]{2,1,0:T(8,128)(2,1)S(1)} %get-tuple-element.44.own.rest_0_, ...), custom_call_target="tpu_custom_call" | custom-call | flops 1073741824 | bytes 2621440 | tf_op jit(solution)/shard_map/pallas_call | solution.py:139
  74.3 1.8 %collective-permute-start.19 = (bf16[256,256]{1,0:T(8,128)(2,1)S(1)}, bf16[256,256]{1,0:T(8,128)(2,1)S(1)}, u32[]{:S(2)}, u32[]{:S(2)}) collective-permute-start(bf16[256,256]{1,0:T(8,128)(2,1)S(1)} %get-tuple-element.51), channel_id=1, source_target_pairs={{0,1},{1,0},{2,3},{3,2},{4,5},{5,4},{6,7},{7,6},{8,9},{9,8},{10,11... | collective-permute-start | bytes 393224 | tf_op jit(solution)/shard_map/ppermute | solution.py:23
  76.1 3.7 %shard_map.48 = (bf16[256,512]{1,0:T(8,128)(2,1)S(1)}, bf16[256,512]{1,0:T(8,128)(2,1)S(1)}) custom-call(s32[8]{0:T(128)S(1)} %copy-done.1, bf16[1,256,2048]{2,1,0:T(8,128)(2,1)S(1)} %get-tuple-element.31.q_near, bf16[1,256,2048]{2,1,0:T(8,128)(2,1)S(1)} %collective-permute-done.q_far, bf16[2,384,256]{2,1,0:T(8,128)(2,1)S(1)} %get-tuple-element.41.own.rest_0_, ...), custom_call_target="tpu_custom_call" | custom-call | flops 1073741824 | bytes 2621440 | tf_op jit(solution)/shard_map/pallas_call | solution.py:139
  79.8 0.1 collective-permute-start.22
  79.9 0.5 collective-permute-start.21
  80.4 2.5 %shard_map.51 = (bf16[256,256]{1,0:T(8,128)(2,1)S(1)}, bf16[256,256]{1,0:T(8,128)(2,1)S(1)}) custom-call(s32[8]{0:T(128)S(1)} %copy-done.1, bf16[1,256,2048]{2,1,0:T(8,128)(2,1)S(1)} %get-tuple-element.31.q_near, bf16[1,256,2048]{2,1,0:T(8,128)(2,1)S(1)} %collective-permute-done.q_far, bf16[2,384,128]{2,1,0:T(8,128)(2,1)S(1)} %get-tuple-element.49.own.rest_0_, ...), custom_call_target="tpu_custom_call" | custom-call | flops 536870912 | bytes 1310720 | tf_op jit(solution)/shard_map/pallas_call | solution.py:139
  82.9 0.2 collective-permute-start.24
  83.0 2.3 %shard_map.50 = (bf16[256,256]{1,0:T(8,128)(2,1)S(1)}, bf16[256,256]{1,0:T(8,128)(2,1)S(1)}) custom-call(s32[8]{0:T(128)S(1)} %copy-done.1, bf16[1,256,2048]{2,1,0:T(8,128)(2,1)S(1)} %get-tuple-element.31.q_near, bf16[1,256,2048]{2,1,0:T(8,128)(2,1)S(1)} %collective-permute-done.q_far, bf16[2,384,128]{2,1,0:T(8,128)(2,1)S(1)} %get-tuple-element.46.own.rest_0_, ...), custom_call_target="tpu_custom_call" | custom-call | flops 536870912 | bytes 1310720 | tf_op jit(solution)/shard_map/pallas_call | solution.py:139
  85.3 0.5 collective-permute-start.23
  85.8 2.3 %shard_map.47 = (bf16[256,256]{1,0:T(8,128)(2,1)S(1)}, bf16[256,256]{1,0:T(8,128)(2,1)S(1)}) custom-call(s32[8]{0:T(128)S(1)} %copy-done.1, bf16[1,256,2048]{2,1,0:T(8,128)(2,1)S(1)} %get-tuple-element.31.q_near, bf16[1,256,2048]{2,1,0:T(8,128)(2,1)S(1)} %collective-permute-done.q_far, bf16[2,512,128]{2,1,0:T(8,128)(2,1)S(1)} %get-tuple-element.39.own.rest_0_, ...), custom_call_target="tpu_custom_call" | custom-call | flops 536870912 | bytes 1310720 | tf_op jit(solution)/shard_map/pallas_call | solution.py:139
  88.1 0.2 collective-permute-start.20
  88.2 1.3 %collective-permute-done.20.refs_7_ = bf16[256,256]{1,0:T(8,128)(2,1)S(1)} collective-permute-done((bf16[256,256]{1,0:T(8,128)(2,1)S(1)}, bf16[256,256]{1,0:T(8,128)(2,1)S(1)}, u32[]{:S(2)}, u32[]{:S(2)}) %collective-permute-start.20) | collective-permute-done | bytes 131104 | tf_op jit(solution)/shard_map/ppermute | solution.py:23
  89.5 1.4 %place.1 = bf16[256,4096]{1,0:T(8,128)(2,1)} custom-call(bf16[256,256]{1,0:T(8,128)(2,1)S(1)} %get-tuple-element.38.refs_0_, bf16[256,256]{1,0:T(8,128)(2,1)S(1)} %get-tuple-element.40.refs_1_, bf16[256,512]{1,0:T(8,128)(2,1)S(1)} %get-tuple-element.43.refs_2_, bf16[256,512]{1,0:T(8,128)(2,1)S(1)} %get-tuple-element.45.refs_3_, ...), custom_call_target="tpu_custom_call" | custom-call | tf_op jit(solution)/shard_map/place/pallas_call | solution.py:180
  (22 shorter events, 0.2 us)
Async XLA Ops:
  0.0 2.5 %copy-start = (bf16[256,4096]{1,0:T(8,128)(2,1)S(1)}, bf16[256,4096]{1,0:T(8,128)(2,1)}, u32[]{:S(2)}) copy-start(bf16[256,4096]{1,0:T(8,128)(2,1)} %refs_0_.2) | copy-start | bytes 6291460
  1.8 3.0 %collective-permute-start.1 = (bf16[2,256,1024]{2,1,0:T(8,128)(2,1)S(1)}, bf16[2,256,1024]{2,1,0:T(8,128)(2,1)S(1)}, u32[]{:S(2)}, u32[]{:S(2)}) collective-permute-start(bf16[2,256,1024]{2,1,0:T(8,128)(2,1)S(1)} %get-tuple-element.34), channel_id=1, source_target_pairs={{0,1},{1,0},{2,3},{3,2},{4,5},{5,4},{6,7},{7,6},{8,9},{9,8},{10,11... | collective-permute-start | bytes 3145736 | tf_op jit(solution)/shard_map/ppermute | solution.py:23
  2.8 29.3 %collective-permute-start = (bf16[1,256,2048]{2,1,0:T(8,128)(2,1)S(1)}, bf16[1,256,2048]{2,1,0:T(8,128)(2,1)S(1)}, u32[]{:S(2)}, u32[]{:S(2)}) collective-permute-start(bf16[1,256,2048]{2,1,0:T(8,128)(2,1)S(1)} %get-tuple-element.32), channel_id=1, source_target_pairs={{0,1},{1,0},{2,3},{3,2},{4,5},{5,4},{6,7},{7,6},{8,9},{9,8},{10,11... | collective-permute-start | bytes 3145736 | tf_op jit(solution)/shard_map/ppermute | solution.py:23
  5.0 28.3 %collective-permute-start.11 = (bf16[2,384,256]{2,1,0:T(8,128)(2,1)S(1)}, bf16[2,384,256]{2,1,0:T(8,128)(2,1)S(1)}, u32[]{:S(2)}, u32[]{:S(2)}) collective-permute-start(bf16[2,384,256]{2,1,0:T(8,128)(2,1)S(1)} %get-tuple-element.44.own.rest_0_), channel_id=1, source_target_pairs={{0,4},{1,5},{2,6},{3,7},{4,8},{5,9},{6,10},{7,11},{8,12},{9,13},{1... | collective-permute-start | bytes 1179656 | tf_op jit(solution)/shard_map/ppermute | solution.py:23
  6.4 11.8 %collective-permute-start.2 = (bf16[2,256,128]{2,1,0:T(8,128)(2,1)S(1)}, bf16[2,256,128]{2,1,0:T(8,128)(2,1)S(1)}, u32[]{:S(2)}, u32[]{:S(2)}) collective-permute-start(bf16[2,256,128]{2,1,0:T(8,128)(2,1)S(1)} %get-tuple-element.36), channel_id=1, source_target_pairs={{0,4},{1,5},{2,6},{3,7},{4,8},{5,9},{6,10},{7,11},{8,12},{9,13},{1... | collective-permute-start | bytes 393224 | tf_op jit(solution)/shard_map/ppermute | solution.py:23
  7.7 27.3 %collective-permute-start.7 = (bf16[2,384,256]{2,1,0:T(8,128)(2,1)S(1)}, bf16[2,384,256]{2,1,0:T(8,128)(2,1)S(1)}, u32[]{:S(2)}, u32[]{:S(2)}) collective-permute-start(bf16[2,384,256]{2,1,0:T(8,128)(2,1)S(1)} %get-tuple-element.41.own.rest_0_), channel_id=1, source_target_pairs={{0,4},{1,5},{2,6},{3,7},{4,8},{5,9},{6,10},{7,11},{8,12},{9,13},{1... | collective-permute-start | bytes 1179656 | tf_op jit(solution)/shard_map/ppermute | solution.py:23
  7.8 23.1 %collective-permute-start.3 = (bf16[2,256,128]{2,1,0:T(8,128)(2,1)S(1)}, bf16[2,256,128]{2,1,0:T(8,128)(2,1)S(1)}, u32[]{:S(2)}, u32[]{:S(2)}) collective-permute-start(bf16[2,256,128]{2,1,0:T(8,128)(2,1)S(1)} %get-tuple-element.37), channel_id=1, source_target_pairs={{0,5},{1,4},{2,7},{3,6},{4,9},{5,8},{6,11},{7,10},{8,13},{9,12},{1... | collective-permute-start | bytes 393224 | tf_op jit(solution)/shard_map/ppermute | solution.py:23
  18.2 16.5 %collective-permute-start.17 = (bf16[2,384,128]{2,1,0:T(8,128)(2,1)S(1)}, bf16[2,384,128]{2,1,0:T(8,128)(2,1)S(1)}, u32[]{:S(2)}, u32[]{:S(2)}) collective-permute-start(bf16[2,384,128]{2,1,0:T(8,128)(2,1)S(1)} %get-tuple-element.49.own.rest_0_), channel_id=1, source_target_pairs={{0,4},{1,5},{2,6},{3,7},{4,8},{5,9},{6,10},{7,11},{8,12},{9,13},{1... | collective-permute-start | bytes 589832 | tf_op jit(solution)/shard_map/ppermute | solution.py:23
  30.8 8.9 %collective-permute-start.9 = (bf16[2,128,512]{2,1,0:T(8,128)(2,1)S(1)}, bf16[2,128,512]{2,1,0:T(8,128)(2,1)S(1)}, u32[]{:S(2)}, u32[]{:S(2)}) collective-permute-start(bf16[2,128,512]{2,1,0:T(8,128)(2,1)S(1)} %get-tuple-element.42.rest_3_), channel_id=1, source_target_pairs={{0,2},{1,3},{2,0},{3,1},{4,6},{5,7},{6,4},{7,5},{8,10},{9,11},{10,... | collective-permute-start | bytes 786440 | tf_op jit(solution)/shard_map/ppermute | solution.py:23
  32.1 7.4 %collective-permute-start.13 = (bf16[2,384,128]{2,1,0:T(8,128)(2,1)S(1)}, bf16[2,384,128]{2,1,0:T(8,128)(2,1)S(1)}, u32[]{:S(2)}, u32[]{:S(2)}) collective-permute-start(bf16[2,384,128]{2,1,0:T(8,128)(2,1)S(1)} %get-tuple-element.46.own.rest_0_), channel_id=1, source_target_pairs={{0,4},{1,5},{2,6},{3,7},{4,8},{5,9},{6,10},{7,11},{8,12},{9,13},{1... | collective-permute-start | bytes 589832 | tf_op jit(solution)/shard_map/ppermute | solution.py:23
  33.4 11.7 %collective-permute-start.5 = (bf16[2,512,128]{2,1,0:T(8,128)(2,1)S(1)}, bf16[2,512,128]{2,1,0:T(8,128)(2,1)S(1)}, u32[]{:S(2)}, u32[]{:S(2)}) collective-permute-start(bf16[2,512,128]{2,1,0:T(8,128)(2,1)S(1)} %get-tuple-element.39.own.rest_0_), channel_id=1, source_target_pairs={{0,4},{1,5},{2,6},{3,7},{4,8},{5,9},{6,10},{7,11},{8,12},{9,13},{1... | collective-permute-start | bytes 786440 | tf_op jit(solution)/shard_map/ppermute | solution.py:23
  34.7 32.0 %copy-start.1 = (s32[8]{0:T(128)S(1)}, s32[8]{0:T(128)}, u32[]{:S(2)}) copy-start(s32[8]{0:T(128)} %blocks.11) | copy-start | bytes 100
  34.7 34.6 %collective-permute-start.12 = (bf16[2,384,256]{2,1,0:T(8,128)(2,1)S(1)}, bf16[2,384,256]{2,1,0:T(8,128)(2,1)S(1)}, u32[]{:S(2)}, u32[]{:S(2)}) collective-permute-start(bf16[2,384,256]{2,1,0:T(8,128)(2,1)S(1)} %choose.9), channel_id=1, source_target_pairs={{0,2},{1,3},{2,0},{3,1},{4,6},{5,7},{6,4},{7,5},{8,10},{9,11},{10,... | collective-permute-start | bytes 1179656 | tf_op jit(solution)/shard_map/ppermute | solution.py:23
  35.0 30.4 %collective-permute-start.4 = (bf16[2,512,128]{2,1,0:T(8,128)(2,1)S(1)}, bf16[2,512,128]{2,1,0:T(8,128)(2,1)S(1)}, u32[]{:S(2)}, u32[]{:S(2)}) collective-permute-start(bf16[2,512,128]{2,1,0:T(8,128)(2,1)S(1)} %choose.6), channel_id=1, source_target_pairs={{0,2},{1,3},{2,0},{3,1},{4,6},{5,7},{6,4},{7,5},{8,10},{9,11},{10,... | collective-permute-start | bytes 786440 | tf_op jit(solution)/shard_map/ppermute | solution.py:23
  39.5 34.8 %collective-permute-start.8 = (bf16[2,384,256]{2,1,0:T(8,128)(2,1)S(1)}, bf16[2,384,256]{2,1,0:T(8,128)(2,1)S(1)}, u32[]{:S(2)}, u32[]{:S(2)}) collective-permute-start(bf16[2,384,256]{2,1,0:T(8,128)(2,1)S(1)} %choose.8), channel_id=1, source_target_pairs={{0,2},{1,3},{2,0},{3,1},{4,6},{5,7},{6,4},{7,5},{8,10},{9,11},{10,... | collective-permute-start | bytes 1179656 | tf_op jit(solution)/shard_map/ppermute | solution.py:23
  39.7 29.3 %collective-permute-start.10 = (bf16[2,128,512]{2,1,0:T(8,128)(2,1)S(1)}, bf16[2,128,512]{2,1,0:T(8,128)(2,1)S(1)}, u32[]{:S(2)}, u32[]{:S(2)}) collective-permute-start(bf16[2,128,512]{2,1,0:T(8,128)(2,1)S(1)} %collective-permute-done.9.rest_4_), channel_id=1, source_target_pairs={{0,4},{1,5},{2,6},{3,7},{4,8},{5,9},{6,10},{7,11},{8,12},{9,13},{1... | collective-permute-start | bytes 786440 | tf_op jit(solution)/shard_map/ppermute | solution.py:23
  45.1 19.1 %collective-permute-start.15 = (bf16[2,128,256]{2,1,0:T(8,128)(2,1)S(1)}, bf16[2,128,256]{2,1,0:T(8,128)(2,1)S(1)}, u32[]{:S(2)}, u32[]{:S(2)}) collective-permute-start(bf16[2,128,256]{2,1,0:T(8,128)(2,1)S(1)} %get-tuple-element.47.rest_3_), channel_id=1, source_target_pairs={{0,2},{1,3},{2,0},{3,1},{4,6},{5,7},{6,4},{7,5},{8,10},{9,11},{10,... | collective-permute-start | bytes 393224 | tf_op jit(solution)/shard_map/ppermute | solution.py:23
  64.2 15.6 %collective-permute-start.16 = (bf16[2,128,256]{2,1,0:T(8,128)(2,1)S(1)}, bf16[2,128,256]{2,1,0:T(8,128)(2,1)S(1)}, u32[]{:S(2)}, u32[]{:S(2)}) collective-permute-start(bf16[2,128,256]{2,1,0:T(8,128)(2,1)S(1)} %collective-permute-done.15.rest_4_), channel_id=1, source_target_pairs={{0,4},{1,5},{2,6},{3,7},{4,8},{5,9},{6,10},{7,11},{8,12},{9,13},{1... | collective-permute-start | bytes 393224 | tf_op jit(solution)/shard_map/ppermute | solution.py:23
  65.5 14.4 %collective-permute-start.18 = (bf16[2,384,128]{2,1,0:T(8,128)(2,1)S(1)}, bf16[2,384,128]{2,1,0:T(8,128)(2,1)S(1)}, u32[]{:S(2)}, u32[]{:S(2)}) collective-permute-start(bf16[2,384,128]{2,1,0:T(8,128)(2,1)S(1)} %choose.11), channel_id=1, source_target_pairs={{0,2},{1,3},{2,0},{3,1},{4,6},{5,7},{6,4},{7,5},{8,10},{9,11},{10,... | collective-permute-start | bytes 589832 | tf_op jit(solution)/shard_map/ppermute | solution.py:23
  69.0 13.8 %collective-permute-start.14 = (bf16[2,384,128]{2,1,0:T(8,128)(2,1)S(1)}, bf16[2,384,128]{2,1,0:T(8,128)(2,1)S(1)}, u32[]{:S(2)}, u32[]{:S(2)}) collective-permute-start(bf16[2,384,128]{2,1,0:T(8,128)(2,1)S(1)} %choose.10), channel_id=1, source_target_pairs={{0,2},{1,3},{2,0},{3,1},{4,6},{5,7},{6,4},{7,5},{8,10},{9,11},{10,... | collective-permute-start | bytes 589832 | tf_op jit(solution)/shard_map/ppermute | solution.py:23
  69.3 16.0 %collective-permute-start.6 = (bf16[2,512,128]{2,1,0:T(8,128)(2,1)S(1)}, bf16[2,512,128]{2,1,0:T(8,128)(2,1)S(1)}, u32[]{:S(2)}, u32[]{:S(2)}) collective-permute-start(bf16[2,512,128]{2,1,0:T(8,128)(2,1)S(1)} %choose.7), channel_id=1, source_target_pairs={{0,2},{1,3},{2,0},{3,1},{4,6},{5,7},{6,4},{7,5},{8,10},{9,11},{10,... | collective-permute-start | bytes 786440 | tf_op jit(solution)/shard_map/ppermute | solution.py:23
  74.3 13.8 %collective-permute-start.19 = (bf16[256,256]{1,0:T(8,128)(2,1)S(1)}, bf16[256,256]{1,0:T(8,128)(2,1)S(1)}, u32[]{:S(2)}, u32[]{:S(2)}) collective-permute-start(bf16[256,256]{1,0:T(8,128)(2,1)S(1)} %get-tuple-element.51), channel_id=1, source_target_pairs={{0,1},{1,0},{2,3},{3,2},{4,5},{5,4},{6,7},{7,6},{8,9},{9,8},{10,11... | collective-permute-start | bytes 393224 | tf_op jit(solution)/shard_map/ppermute | solution.py:23
  79.8 9.7 %collective-permute-start.22 = (bf16[256,512]{1,0:T(8,128)(2,1)S(1)}, bf16[256,512]{1,0:T(8,128)(2,1)S(1)}, u32[]{:S(2)}, u32[]{:S(2)}) collective-permute-start(bf16[256,512]{1,0:T(8,128)(2,1)S(1)} %get-tuple-element.54), channel_id=1, source_target_pairs={{0,1},{1,0},{2,3},{3,2},{4,5},{5,4},{6,7},{7,6},{8,9},{9,8},{10,11... | collective-permute-start | bytes 786440 | tf_op jit(solution)/shard_map/ppermute | solution.py:23
  79.9 9.6 %collective-permute-start.21 = (bf16[256,512]{1,0:T(8,128)(2,1)S(1)}, bf16[256,512]{1,0:T(8,128)(2,1)S(1)}, u32[]{:S(2)}, u32[]{:S(2)}) collective-permute-start(bf16[256,512]{1,0:T(8,128)(2,1)S(1)} %get-tuple-element.53), channel_id=1, source_target_pairs={{0,1},{1,0},{2,3},{3,2},{4,5},{5,4},{6,7},{7,6},{8,9},{9,8},{10,11... | collective-permute-start | bytes 786440 | tf_op jit(solution)/shard_map/ppermute | solution.py:23
  82.9 5.4 %collective-permute-start.24 = (bf16[256,256]{1,0:T(8,128)(2,1)S(1)}, bf16[256,256]{1,0:T(8,128)(2,1)S(1)}, u32[]{:S(2)}, u32[]{:S(2)}) collective-permute-start(bf16[256,256]{1,0:T(8,128)(2,1)S(1)} %get-tuple-element.56), channel_id=1, source_target_pairs={{0,1},{1,0},{2,3},{3,2},{4,5},{5,4},{6,7},{7,6},{8,9},{9,8},{10,11... | collective-permute-start | bytes 393224 | tf_op jit(solution)/shard_map/ppermute | solution.py:23
  85.3 2.9 %collective-permute-start.23 = (bf16[256,256]{1,0:T(8,128)(2,1)S(1)}, bf16[256,256]{1,0:T(8,128)(2,1)S(1)}, u32[]{:S(2)}, u32[]{:S(2)}) collective-permute-start(bf16[256,256]{1,0:T(8,128)(2,1)S(1)} %get-tuple-element.55), channel_id=1, source_target_pairs={{0,1},{1,0},{2,3},{3,2},{4,5},{5,4},{6,7},{7,6},{8,9},{9,8},{10,11... | collective-permute-start | bytes 393224 | tf_op jit(solution)/shard_map/ppermute | solution.py:23
  88.1 1.4 %collective-permute-start.20 = (bf16[256,256]{1,0:T(8,128)(2,1)S(1)}, bf16[256,256]{1,0:T(8,128)(2,1)S(1)}, u32[]{:S(2)}, u32[]{:S(2)}) collective-permute-start(bf16[256,256]{1,0:T(8,128)(2,1)S(1)} %get-tuple-element.52), channel_id=1, source_target_pairs={{0,1},{1,0},{2,3},{3,2},{4,5},{5,4},{6,7},{7,6},{8,9},{9,8},{10,11... | collective-permute-start | bytes 393224 | tf_op jit(solution)/shard_map/ppermute | solution.py:23

commit v5 on v4

--- a/solution.py
+++ b/solution.py
@@ -23,10 +23,31 @@
     return lax.ppermute(block, "seq", pairs)
 
 
-def attend_kernel(plan, spots, blocks, q_near, q_far, *rest):
-    first, heads, _, ratio, window, spans = plan
+def store_pieces(puts, pieces, out, half, ratio, sems):
+    core = lax.axis_index("seq") % CORES
+    stores = []
+    for (swapped, first), piece in zip(puts, pieces):
+        which = 1 - core if swapped else core
+        col = pl.multiple_of((which * half + first) * ratio * DH, DH)
+        store = pltpu.make_async_copy(
+            piece, out.at[:, pl.ds(col, piece.shape[1])], sems.at[len(stores)]
+        )
+        store.start()
+        stores.append(store)
+    return stores
+
+
+def attend_kernel(plan, spots, puts, blocks, q_near, q_far, *rest):
+    first, heads, half, ratio, window, spans = plan
     pieces = rest[: len(spots)]
-    out_near, out_far, q_buf, k_buf, v_buf, o_buf, s_buf, w_buf = rest[len(spots) :]
+    rest = rest[len(spots) :]
+    stores = []
+    if puts:
+        placed, rest = rest[: len(puts)], rest[len(puts) :]
+        out, sems = rest[2], rest[-1]
+        rest = rest[:2] + rest[3:-1]
+        stores = store_pieces(puts, placed, out, half, ratio, sems)
+    out_near, out_far, q_buf, k_buf, v_buf, o_buf, s_buf, w_buf = rest
     rows = q_near.shape[-2]
     chip_rows = rows * CORES
     me = lax.axis_index("seq")
@@ -123,9 +144,11 @@
             blend(*tiles[step - 2])
     out_near[...] = o_buf[pl.ds(mine, rows)]
     out_far[...] = o_buf[pl.ds(other, rows)]
-
-
-def attend(plan, spots, blocks, q_near, q_far, pieces):
+    for store in stores:
+        store.wait()
+
+
+def attend(plan, spots, blocks, q_near, q_far, pieces, puts=(), placed=(), columns=0):
     _, heads, _, ratio, window, spans = plan
     rows = q_near.shape[-2]
     chip_rows = rows * CORES
@@ -136,11 +159,15 @@
     scratch_bytes = (chip_rows * q_width + held * kv_width) * 4 + SLOTS * ratio * BLK * window * BLK * 6
     near_by = pl.BlockSpec(memory_space=pltpu.VMEM)
     shape = pltpu.VMEM((rows, q_width), q_near.dtype)
+    anywhere = pl.BlockSpec(memory_space=pl.ANY)
+    whole = (pltpu.HBM((rows, columns), q_near.dtype),) if puts else ()
     return pl.pallas_call(
-        functools.partial(attend_kernel, plan, spots),
-        out_shape=(shape, shape),
-        in_specs=[pl.BlockSpec(memory_space=pltpu.SMEM)] + [near_by] * (2 + len(pieces)),
-        out_specs=(near_by, near_by),
+        functools.partial(attend_kernel, plan, spots, puts),
+        out_shape=(shape, shape) + whole,
+        in_specs=[pl.BlockSpec(memory_space=pltpu.SMEM)]
+        + [near_by] * (2 + len(pieces))
+        + [anywhere] * len(puts),
+        out_specs=(near_by, near_by) + (anywhere,) * len(whole),
         scratch_shapes=[
             pltpu.VMEM((chip_rows, q_width), jnp.bfloat16),
             pltpu.VMEM((held, kv_width), jnp.bfloat16),
@@ -148,44 +175,35 @@
             pltpu.VMEM((chip_rows, q_width), jnp.bfloat16),
             pltpu.VMEM((SLOTS, ratio * BLK, window * BLK), jnp.float32),
             pltpu.VMEM((SLOTS, ratio * BLK, window * BLK), jnp.bfloat16),
-        ],
+        ]
+        + [pltpu.SemaphoreType.DMA((len(puts),))] * len(whole),
         cost_estimate=pl.CostEstimate(
             flops=4 * scores * DH,
             bytes_accessed=2 * (chip_rows * q_width * 2 + held * kv_width * 2),
             transcendentals=scores,
         ),
         compiler_params=pltpu.CompilerParams(vmem_limit_bytes=scratch_bytes + (6 << 20)),
-    )(blocks, q_near, q_far, *pieces)
-
-
-def place_kernel(firsts, half, ratio, *refs):
-    count = len(firsts)
-    out, sems = refs[2 * count :]
-    core = lax.axis_index("seq") % CORES
-    stores = []
-    for i, first in enumerate(firsts):
-        for which, piece in ((core, refs[i]), (1 - core, refs[count + i])):
-            col = pl.multiple_of((which * half + first) * ratio * DH, DH)
-            store = pltpu.make_async_copy(
-                piece, out.at[:, pl.ds(col, piece.shape[1])], sems.at[len(stores)]
-            )
-            store.start()
-            stores.append(store)
-    for store in stores:
+    )(blocks, q_near, q_far, *pieces, *placed)
+
+
+def place_kernel(puts, half, ratio, *refs):
+    pieces, out, sems = refs[: len(puts)], refs[-2], refs[-1]
+    for store in store_pieces(puts, pieces, out, half, ratio, sems):
         store.wait()
 
 
-def place(firsts, half, ratio, nears, fars, width):
+def place(puts, half, ratio, pieces, out):
     anywhere = pl.BlockSpec(memory_space=pl.ANY)
     return pl.pallas_call(
-        functools.partial(place_kernel, firsts, half, ratio),
-        out_shape=pltpu.HBM((nears[0].shape[0], width), nears[0].dtype),
-        in_specs=[anywhere] * (2 * len(firsts)),
+        functools.partial(place_kernel, puts, half, ratio),
+        out_shape=pltpu.HBM(out.shape, out.dtype),
+        in_specs=[anywhere] * (len(puts) + 1),
         out_specs=anywhere,
-        scratch_shapes=[pltpu.SemaphoreType.DMA((2 * len(firsts),))],
+        scratch_shapes=[pltpu.SemaphoreType.DMA((len(puts),))],
+        input_output_aliases={len(puts): 0},
         compiler_params=pltpu.CompilerParams(vmem_limit_bytes=1 << 20),
         name="place",
-    )(*nears, *fars)
+    )(*pieces, out)
 
 
 def split_kernel(arrays, width, early, *refs):
@@ -386,10 +404,20 @@
                 (base - back * chip_rows, 0, chip_rows, 0, None) for back in range(spans + 1)
             )
         plan = (first, heads, half, ratio, window, spans)
-        out_near, out_far = attend(plan, spots, doc_blocks, q_near, q_far, pieces)
+        done, puts = (), ()
+        if i == len(sizes) - 1:
+            early_far = max(i - 1, 0)
+            done = (*nears, *fars[:early_far])
+            puts = tuple((0, f) for f in firsts[:i])
+            puts += tuple((1, f) for f in firsts[:early_far])
+        out_near, out_far, *out = attend(
+            plan, spots, doc_blocks, q_near, q_far, pieces, puts, done, queries.shape[1]
+        )
         nears.append(out_near)
         fars.append(shift(out_far, partner))
-    return place(firsts, half, ratio, nears, fars, queries.shape[1])
+    left = (nears[-1], *fars[early_far:])
+    puts = ((0, firsts[-1]), *((1, f) for f in firsts[early_far:]))
+    return place(puts, half, ratio, left, out[0])
 
 
 def solution(mesh):

time: 92.2 us -> 79.7 us (0.86)
  the two profiles are of different devices: /device:TPU:11 before, /device:TPU:0 now
where the time goes in v5:
time: 79.7 us; the launch traced here: 79.6 us
  waiting for transfers between devices  38.1 us (48%)
  starting transfers between devices  21.2 us (27%)
  Pallas kernels  19.9 us (25%)
    ppermute x25, waiting for transfers between devices, shift(): return lax.ppermute(block, 'seq', pairs)  38.1 us
    ppermute x25, starting transfers between devices, shift(): return lax.ppermute(block, 'seq', pairs)  21.2 us
    pallas_call x6, Pallas kernels, attend(): pl.pallas_call(functools.partial(attend_kernel, plan, spots, puts), out_s...  16.8 us
    pallas_call x2, Pallas kernels, split(): pl.pallas_call(functools.partial(split_kernel, len(arrays), width, early)...  2 us
  transfers between devices with their start and end apart: 25, of which 7 were waited for; matrix products, arithmetic and copies ran while one was open for 0% of the time, Pallas kernels for 22%

profile of v5, /device:TPU:0, one launch (start us, length us, event | category | flops | bytes accessed | tf_op | source)
XLA Modules:
  0.0 79.6 jit_solution(13776639035320237728)
XLA Ops:
  0.0 1.8 %split.3 = (bf16[2,256,1024]{2,1,0:T(8,128)(2,1)S(1)}, bf16[2,256,1024]{2,1,0:T(8,128)(2,1)S(1)}, bf16[2,256,128]{2,1,0:T(8,128)(2,1)S(1)}, bf16[2,256,128]{2,1,0:T(8,128)(2,1)S(1)}) custom-call(bf16[256,2048]{1,0:T(8,128)(2,1)} %refs_0_.3, bf16[256,2048]{1,0:T(8,128)(2,1)} %refs_1_.1), custom_call_target="tpu_custom_call" | custom-call | tf_op jit(solution)/shard_map/split/pallas_call | solution.py:232
  1.8 0.6 collective-permute-start.1
  2.3 0.2 split.2
  2.6 0.5 collective-permute-start
  3.1 1.5 %collective-permute-done.1.far = bf16[2,256,1024]{2,1,0:T(8,128)(2,1)S(1)} collective-permute-done((bf16[2,256,1024]{2,1,0:T(8,128)(2,1)S(1)}, bf16[2,256,1024]{2,1,0:T(8,128)(2,1)S(1)}, u32[]{:S(2)}, u32[]{:S(2)}) %collective-permute-start.1) | collective-permute-done | bytes 1048608 | tf_op jit(solution)/shard_map/ppermute | solution.py:23
  4.6 0.2 merge.1
  4.9 3.0 %collective-permute-start.11 = (bf16[2,384,256]{2,1,0:T(8,128)(2,1)S(1)}, bf16[2,384,256]{2,1,0:T(8,128)(2,1)S(1)}, u32[]{:S(2)}, u32[]{:S(2)}) collective-permute-start(bf16[2,384,256]{2,1,0:T(8,128)(2,1)S(1)} %get-tuple-element.44.own.rest_0_), channel_id=1, source_target_pairs={{0,4},{1,5},{2,6},{3,7},{4,8},{5,9},{6,10},{7,11},{8,12},{9,13},{1... | collective-permute-start | bytes 1179656 | tf_op jit(solution)/shard_map/ppermute | solution.py:23
  7.8 1.6 %collective-permute-start.15 = (bf16[2,384,256]{2,1,0:T(8,128)(2,1)S(1)}, bf16[2,384,256]{2,1,0:T(8,128)(2,1)S(1)}, u32[]{:S(2)}, u32[]{:S(2)}) collective-permute-start(bf16[2,384,256]{2,1,0:T(8,128)(2,1)S(1)} %get-tuple-element.47.own.rest_0_), channel_id=1, source_target_pairs={{0,4},{1,5},{2,6},{3,7},{4,8},{5,9},{6,10},{7,11},{8,12},{9,13},{1... | collective-permute-start | bytes 1179656 | tf_op jit(solution)/shard_map/ppermute | solution.py:23
  9.4 1.5 %collective-permute-start.13 = (bf16[2,128,512]{2,1,0:T(8,128)(2,1)S(1)}, bf16[2,128,512]{2,1,0:T(8,128)(2,1)S(1)}, u32[]{:S(2)}, u32[]{:S(2)}) collective-permute-start(bf16[2,128,512]{2,1,0:T(8,128)(2,1)S(1)} %get-tuple-element.45.rest_3_), channel_id=1, source_target_pairs={{0,2},{1,3},{2,0},{3,1},{4,6},{5,7},{6,4},{7,5},{8,10},{9,11},{10,... | collective-permute-start | bytes 786440 | tf_op jit(solution)/shard_map/ppermute | solution.py:23
  10.9 1.6 %collective-permute-start.6 = (bf16[2,256,128]{2,1,0:T(8,128)(2,1)S(1)}, bf16[2,256,128]{2,1,0:T(8,128)(2,1)S(1)}, u32[]{:S(2)}, u32[]{:S(2)}) collective-permute-start(bf16[2,256,128]{2,1,0:T(8,128)(2,1)S(1)} %get-tuple-element.39), channel_id=1, source_target_pairs={{0,4},{1,5},{2,6},{3,7},{4,8},{5,9},{6,10},{7,11},{8,12},{9,13},{1... | collective-permute-start | bytes 393224 | tf_op jit(solution)/shard_map/ppermute | solution.py:23
  12.5 7.3 %collective-permute-done.11.refs_0_.rest_2_ = bf16[2,384,256]{2,1,0:T(8,128)(2,1)S(1)} collective-permute-done((bf16[2,384,256]{2,1,0:T(8,128)(2,1)S(1)}, bf16[2,384,256]{2,1,0:T(8,128)(2,1)S(1)}, u32[]{:S(2)}, u32[]{:S(2)}) %collective-permute-start.11) | collective-permute-done | bytes 393248 | tf_op jit(solution)/shard_map/ppermute | solution.py:23
  19.9 11.2 %collective-permute-done.6.refs_0_.rest_2_.rest_4_ = bf16[2,256,128]{2,1,0:T(8,128)(2,1)S(1)} collective-permute-done((bf16[2,256,128]{2,1,0:T(8,128)(2,1)S(1)}, bf16[2,256,128]{2,1,0:T(8,128)(2,1)S(1)}, u32[]{:S(2)}, u32[]{:S(2)}) %collective-permute-start.6) | collective-permute-done | bytes 131104 | tf_op jit(solution)/shard_map/ppermute | solution.py:23
  31.1 1.7 %collective-permute-start.12 = (bf16[2,384,256]{2,1,0:T(8,128)(2,1)S(1)}, bf16[2,384,256]{2,1,0:T(8,128)(2,1)S(1)}, u32[]{:S(2)}, u32[]{:S(2)}) collective-permute-start(bf16[2,384,256]{2,1,0:T(8,128)(2,1)S(1)} %choose.9), channel_id=1, source_target_pairs={{0,2},{1,3},{2,0},{3,1},{4,6},{5,7},{6,4},{7,5},{8,10},{9,11},{10,... | collective-permute-start | bytes 1179656 | tf_op jit(solution)/shard_map/ppermute | solution.py:23
  32.8 0.0 collective-permute-done.7.refs_1_.rest_3_.rest_5_
  32.8 1.3 %collective-permute-start.4 = (bf16[2,128,256]{2,1,0:T(8,128)(2,1)S(1)}, bf16[2,128,256]{2,1,0:T(8,128)(2,1)S(1)}, u32[]{:S(2)}, u32[]{:S(2)}) collective-permute-start(bf16[2,128,256]{2,1,0:T(8,128)(2,1)S(1)} %get-tuple-element.37.rest_3_), channel_id=1, source_target_pairs={{0,2},{1,3},{2,0},{3,1},{4,6},{5,7},{6,4},{7,5},{8,10},{9,11},{10,... | collective-permute-start | bytes 393224 | tf_op jit(solution)/shard_map/ppermute | solution.py:23
  34.1 0.0 collective-permute-done.15.refs_0_.rest_2_
  34.1 0.8 %collective-permute-start.16 = (bf16[2,384,256]{2,1,0:T(8,128)(2,1)S(1)}, bf16[2,384,256]{2,1,0:T(8,128)(2,1)S(1)}, u32[]{:S(2)}, u32[]{:S(2)}) collective-permute-start(bf16[2,384,256]{2,1,0:T(8,128)(2,1)S(1)} %choose.10), channel_id=1, source_target_pairs={{0,2},{1,3},{2,0},{3,1},{4,6},{5,7},{6,4},{7,5},{8,10},{9,11},{10,... | collective-permute-start | bytes 1179656 | tf_op jit(solution)/shard_map/ppermute | solution.py:23
  35.0 1.3 %collective-permute-start.14 = (bf16[2,128,512]{2,1,0:T(8,128)(2,1)S(1)}, bf16[2,128,512]{2,1,0:T(8,128)(2,1)S(1)}, u32[]{:S(2)}, u32[]{:S(2)}) collective-permute-start(bf16[2,128,512]{2,1,0:T(8,128)(2,1)S(1)} %collective-permute-done.13.rest_4_), channel_id=1, source_target_pairs={{0,4},{1,5},{2,6},{3,7},{4,8},{5,9},{6,10},{7,11},{8,12},{9,13},{1... | collective-permute-start | bytes 786440 | tf_op jit(solution)/shard_map/ppermute | solution.py:23
  36.3 9.6 %collective-permute-done.4.rest_4_ = bf16[2,128,256]{2,1,0:T(8,128)(2,1)S(1)} collective-permute-done((bf16[2,128,256]{2,1,0:T(8,128)(2,1)S(1)}, bf16[2,128,256]{2,1,0:T(8,128)(2,1)S(1)}, u32[]{:S(2)}, u32[]{:S(2)}) %collective-permute-start.4) | collective-permute-done | bytes 131104 | tf_op jit(solution)/shard_map/ppermute | solution.py:23
  45.9 0.0 collective-permute-start.17
  45.9 0.0 collective-permute-done.9.refs_0_.rest_2_
  45.9 1.8 %collective-permute-start.8 = (bf16[2,512,128]{2,1,0:T(8,128)(2,1)S(1)}, bf16[2,512,128]{2,1,0:T(8,128)(2,1)S(1)}, u32[]{:S(2)}, u32[]{:S(2)}) collective-permute-start(bf16[2,512,128]{2,1,0:T(8,128)(2,1)S(1)} %choose.7), channel_id=1, source_target_pairs={{0,2},{1,3},{2,0},{3,1},{4,6},{5,7},{6,4},{7,5},{8,10},{9,11},{10,... | collective-permute-start | bytes 786440 | tf_op jit(solution)/shard_map/ppermute | solution.py:23
  47.7 6.5 %collective-permute-done.17.refs_0_.rest_2_ = bf16[2,384,128]{2,1,0:T(8,128)(2,1)S(1)} collective-permute-done((bf16[2,384,128]{2,1,0:T(8,128)(2,1)S(1)}, bf16[2,384,128]{2,1,0:T(8,128)(2,1)S(1)}, u32[]{:S(2)}, u32[]{:S(2)}) %collective-permute-start.17) | collective-permute-done | bytes 196640 | tf_op jit(solution)/shard_map/ppermute | solution.py:23
  54.2 0.8 %collective-permute-start.10 = (bf16[2,512,128]{2,1,0:T(8,128)(2,1)S(1)}, bf16[2,512,128]{2,1,0:T(8,128)(2,1)S(1)}, u32[]{:S(2)}, u32[]{:S(2)}) collective-permute-start(bf16[2,512,128]{2,1,0:T(8,128)(2,1)S(1)} %choose.8), channel_id=1, source_target_pairs={{0,2},{1,3},{2,0},{3,1},{4,6},{5,7},{6,4},{7,5},{8,10},{9,11},{10,... | collective-permute-start | bytes 786440 | tf_op jit(solution)/shard_map/ppermute | solution.py:23
  55.1 0.0 collective-permute-done.14.rest_5_
  55.1 0.1 collective-permute-start.2
  55.2 0.0 collective-permute-done.12.rest_1_
  55.2 0.1 collective-permute-start.5
  55.3 3.7 %shard_map.48 = (bf16[256,512]{1,0:T(8,128)(2,1)S(1)}, bf16[256,512]{1,0:T(8,128)(2,1)S(1)}) custom-call(s32[8]{0:T(128)S(1)} %copy-done.1, bf16[1,256,2048]{2,1,0:T(8,128)(2,1)S(1)} %get-tuple-element.32.q_near, bf16[1,256,2048]{2,1,0:T(8,128)(2,1)S(1)} %collective-permute-done.q_far, bf16[2,384,256]{2,1,0:T(8,128)(2,1)S(1)} %get-tuple-element.44.own.rest_0_, ...), custom_call_target="tpu_custom_call" | custom-call | flops 1073741824 | bytes 2621440 | tf_op jit(solution)/shard_map/pallas_call | solution.py:164
  59.0 0.0 collective-permute-done.16.rest_1_
  59.0 1.3 %collective-permute-start.18 = (bf16[2,384,128]{2,1,0:T(8,128)(2,1)S(1)}, bf16[2,384,128]{2,1,0:T(8,128)(2,1)S(1)}, u32[]{:S(2)}, u32[]{:S(2)}) collective-permute-start(bf16[2,384,128]{2,1,0:T(8,128)(2,1)S(1)} %choose.11), channel_id=1, source_target_pairs={{0,2},{1,3},{2,0},{3,1},{4,6},{5,7},{6,4},{7,5},{8,10},{9,11},{10,... | collective-permute-start | bytes 589832 | tf_op jit(solution)/shard_map/ppermute | solution.py:23
  60.2 3.7 %shard_map.49 = (bf16[256,512]{1,0:T(8,128)(2,1)S(1)}, bf16[256,512]{1,0:T(8,128)(2,1)S(1)}) custom-call(s32[8]{0:T(128)S(1)} %copy-done.1, bf16[1,256,2048]{2,1,0:T(8,128)(2,1)S(1)} %get-tuple-element.32.q_near, bf16[1,256,2048]{2,1,0:T(8,128)(2,1)S(1)} %collective-permute-done.q_far, bf16[2,384,256]{2,1,0:T(8,128)(2,1)S(1)} %get-tuple-element.47.own.rest_0_, ...), custom_call_target="tpu_custom_call" | custom-call | flops 1073741824 | bytes 2621440 | tf_op jit(solution)/shard_map/pallas_call | solution.py:164
  63.9 0.0 collective-permute-done.2.refs_0_.rest_2_
  64.0 0.1 collective-permute-start.21
  64.0 0.0 collective-permute-done.8.rest_1_
  64.0 0.5 collective-permute-start.22
  64.6 1.0 %collective-permute-done.10.rest_1_ = bf16[2,512,128]{2,1,0:T(8,128)(2,1)S(1)} collective-permute-done((bf16[2,512,128]{2,1,0:T(8,128)(2,1)S(1)}, bf16[2,512,128]{2,1,0:T(8,128)(2,1)S(1)}, u32[]{:S(2)}, u32[]{:S(2)}) %collective-permute-start.10) | collective-permute-done | bytes 262176 | tf_op jit(solution)/shard_map/ppermute | solution.py:23
  65.5 1.4 %collective-permute-start.3 = (bf16[2,384,128]{2,1,0:T(8,128)(2,1)S(1)}, bf16[2,384,128]{2,1,0:T(8,128)(2,1)S(1)}, u32[]{:S(2)}, u32[]{:S(2)}) collective-permute-start(bf16[2,384,128]{2,1,0:T(8,128)(2,1)S(1)} %choose.6), channel_id=1, source_target_pairs={{0,2},{1,3},{2,0},{3,1},{4,6},{5,7},{6,4},{7,5},{8,10},{9,11},{10,... | collective-permute-start | bytes 589832 | tf_op jit(solution)/shard_map/ppermute | solution.py:23
  67.0 2.5 %shard_map.46 = (bf16[256,256]{1,0:T(8,128)(2,1)S(1)}, bf16[256,256]{1,0:T(8,128)(2,1)S(1)}) custom-call(s32[8]{0:T(128)S(1)} %copy-done.1, bf16[1,256,2048]{2,1,0:T(8,128)(2,1)S(1)} %get-tuple-element.32.q_near, bf16[1,256,2048]{2,1,0:T(8,128)(2,1)S(1)} %collective-permute-done.q_far, bf16[2,512,128]{2,1,0:T(8,128)(2,1)S(1)} %get-tuple-element.38.own.rest_0_, ...), custom_call_target="tpu_custom_call" | custom-call | flops 536870912 | bytes 1310720 | tf_op jit(solution)/shard_map/pallas_call | solution.py:164
  69.4 2.3 %shard_map.47 = (bf16[256,256]{1,0:T(8,128)(2,1)S(1)}, bf16[256,256]{1,0:T(8,128)(2,1)S(1)}) custom-call(s32[8]{0:T(128)S(1)} %copy-done.1, bf16[1,256,2048]{2,1,0:T(8,128)(2,1)S(1)} %get-tuple-element.32.q_near, bf16[1,256,2048]{2,1,0:T(8,128)(2,1)S(1)} %collective-permute-done.q_far, bf16[2,512,128]{2,1,0:T(8,128)(2,1)S(1)} %get-tuple-element.42.own.rest_0_, ...), custom_call_target="tpu_custom_call" | custom-call | flops 536870912 | bytes 1310720 | tf_op jit(solution)/shard_map/pallas_call | solution.py:164
  71.7 0.1 collective-permute-start.19
  71.8 0.5 collective-permute-start.20
  72.3 2.3 %shard_map.50 = (bf16[256,256]{1,0:T(8,128)(2,1)S(1)}, bf16[256,256]{1,0:T(8,128)(2,1)S(1)}) custom-call(s32[8]{0:T(128)S(1)} %copy-done.1, bf16[1,256,2048]{2,1,0:T(8,128)(2,1)S(1)} %get-tuple-element.32.q_near, bf16[1,256,2048]{2,1,0:T(8,128)(2,1)S(1)} %collective-permute-done.q_far, bf16[2,384,128]{2,1,0:T(8,128)(2,1)S(1)} %get-tuple-element.49.own.rest_0_, ...), custom_call_target="tpu_custom_call" | custom-call | flops 536870912 | bytes 1310720 | tf_op jit(solution)/shard_map/pallas_call | solution.py:164
  74.6 0.2 collective-permute-start.23
  74.8 2.4 %shard_map.51 = (bf16[256,256]{1,0:T(8,128)(2,1)S(1)}, bf16[256,256]{1,0:T(8,128)(2,1)S(1)}, bf16[256,4096]{1,0:T(8,128)(2,1)}) custom-call(s32[8]{0:T(128)S(1)} %copy-done.1, bf16[1,256,2048]{2,1,0:T(8,128)(2,1)S(1)} %get-tuple-element.32.q_near, bf16[1,256,2048]{2,1,0:T(8,128)(2,1)S(1)} %collective-permute-done.q_far, ...), custom_call_target="tpu_custom_call" | custom-call | flops 536870912 | bytes 1310720 | tf_op jit(solution)/shard_map/pallas_call | solution.py:164
  77.2 0.5 collective-permute-start.24
  77.7 1.0 %collective-permute-done.24.refs_2_ = bf16[256,256]{1,0:T(8,128)(2,1)S(1)} collective-permute-done((bf16[256,256]{1,0:T(8,128)(2,1)S(1)}, bf16[256,256]{1,0:T(8,128)(2,1)S(1)}, u32[]{:S(2)}, u32[]{:S(2)}) %collective-permute-start.24) | collective-permute-done | bytes 131104 | tf_op jit(solution)/shard_map/ppermute | solution.py:23
  78.7 0.8 place.1
  (22 shorter events, 0.2 us)
Async XLA Ops:
  0.0 2.3 %copy-start = (bf16[256,4096]{1,0:T(8,128)(2,1)S(1)}, bf16[256,4096]{1,0:T(8,128)(2,1)}, u32[]{:S(2)}) copy-start(bf16[256,4096]{1,0:T(8,128)(2,1)} %refs_0_.2) | copy-start | bytes 6291460
  1.8 2.8 %collective-permute-start.1 = (bf16[2,256,1024]{2,1,0:T(8,128)(2,1)S(1)}, bf16[2,256,1024]{2,1,0:T(8,128)(2,1)S(1)}, u32[]{:S(2)}, u32[]{:S(2)}) collective-permute-start(bf16[2,256,1024]{2,1,0:T(8,128)(2,1)S(1)} %get-tuple-element.35), channel_id=1, source_target_pairs={{0,1},{1,0},{2,3},{3,2},{4,5},{5,4},{6,7},{7,6},{8,9},{9,8},{10,11... | collective-permute-start | bytes 3145736 | tf_op jit(solution)/shard_map/ppermute | solution.py:23
  2.6 31.5 %collective-permute-start = (bf16[1,256,2048]{2,1,0:T(8,128)(2,1)S(1)}, bf16[1,256,2048]{2,1,0:T(8,128)(2,1)S(1)}, u32[]{:S(2)}, u32[]{:S(2)}) collective-permute-start(bf16[1,256,2048]{2,1,0:T(8,128)(2,1)S(1)} %get-tuple-element.33), channel_id=1, source_target_pairs={{0,1},{1,0},{2,3},{3,2},{4,5},{5,4},{6,7},{7,6},{8,9},{9,8},{10,11... | collective-permute-start | bytes 3145736 | tf_op jit(solution)/shard_map/ppermute | solution.py:23
  4.9 15.0 %collective-permute-start.11 = (bf16[2,384,256]{2,1,0:T(8,128)(2,1)S(1)}, bf16[2,384,256]{2,1,0:T(8,128)(2,1)S(1)}, u32[]{:S(2)}, u32[]{:S(2)}) collective-permute-start(bf16[2,384,256]{2,1,0:T(8,128)(2,1)S(1)} %get-tuple-element.44.own.rest_0_), channel_id=1, source_target_pairs={{0,4},{1,5},{2,6},{3,7},{4,8},{5,9},{6,10},{7,11},{8,12},{9,13},{1... | collective-permute-start | bytes 1179656 | tf_op jit(solution)/shard_map/ppermute | solution.py:23
  7.8 26.2 %collective-permute-start.15 = (bf16[2,384,256]{2,1,0:T(8,128)(2,1)S(1)}, bf16[2,384,256]{2,1,0:T(8,128)(2,1)S(1)}, u32[]{:S(2)}, u32[]{:S(2)}) collective-permute-start(bf16[2,384,256]{2,1,0:T(8,128)(2,1)S(1)} %get-tuple-element.47.own.rest_0_), channel_id=1, source_target_pairs={{0,4},{1,5},{2,6},{3,7},{4,8},{5,9},{6,10},{7,11},{8,12},{9,13},{1... | collective-permute-start | bytes 1179656 | tf_op jit(solution)/shard_map/ppermute | solution.py:23
  9.4 25.5 %collective-permute-start.13 = (bf16[2,128,512]{2,1,0:T(8,128)(2,1)S(1)}, bf16[2,128,512]{2,1,0:T(8,128)(2,1)S(1)}, u32[]{:S(2)}, u32[]{:S(2)}) collective-permute-start(bf16[2,128,512]{2,1,0:T(8,128)(2,1)S(1)} %get-tuple-element.45.rest_3_), channel_id=1, source_target_pairs={{0,2},{1,3},{2,0},{3,1},{4,6},{5,7},{6,4},{7,5},{8,10},{9,11},{10,... | collective-permute-start | bytes 786440 | tf_op jit(solution)/shard_map/ppermute | solution.py:23
  10.9 20.1 %collective-permute-start.6 = (bf16[2,256,128]{2,1,0:T(8,128)(2,1)S(1)}, bf16[2,256,128]{2,1,0:T(8,128)(2,1)S(1)}, u32[]{:S(2)}, u32[]{:S(2)}) collective-permute-start(bf16[2,256,128]{2,1,0:T(8,128)(2,1)S(1)} %get-tuple-element.39), channel_id=1, source_target_pairs={{0,4},{1,5},{2,6},{3,7},{4,8},{5,9},{6,10},{7,11},{8,12},{9,13},{1... | collective-permute-start | bytes 393224 | tf_op jit(solution)/shard_map/ppermute | solution.py:23
  19.8 35.4 %copy-start.1 = (s32[8]{0:T(128)S(1)}, s32[8]{0:T(128)}, u32[]{:S(2)}) copy-start(s32[8]{0:T(128)} %blocks.11) | copy-start | bytes 100
  19.8 13.0 %collective-permute-start.7 = (bf16[2,256,128]{2,1,0:T(8,128)(2,1)S(1)}, bf16[2,256,128]{2,1,0:T(8,128)(2,1)S(1)}, u32[]{:S(2)}, u32[]{:S(2)}) collective-permute-start(bf16[2,256,128]{2,1,0:T(8,128)(2,1)S(1)} %get-tuple-element.40), channel_id=1, source_target_pairs={{0,5},{1,4},{2,7},{3,6},{4,9},{5,8},{6,11},{7,10},{8,13},{9,12},{1... | collective-permute-start | bytes 393224 | tf_op jit(solution)/shard_map/ppermute | solution.py:23
  31.1 24.1 %collective-permute-start.12 = (bf16[2,384,256]{2,1,0:T(8,128)(2,1)S(1)}, bf16[2,384,256]{2,1,0:T(8,128)(2,1)S(1)}, u32[]{:S(2)}, u32[]{:S(2)}) collective-permute-start(bf16[2,384,256]{2,1,0:T(8,128)(2,1)S(1)} %choose.9), channel_id=1, source_target_pairs={{0,2},{1,3},{2,0},{3,1},{4,6},{5,7},{6,4},{7,5},{8,10},{9,11},{10,... | collective-permute-start | bytes 1179656 | tf_op jit(solution)/shard_map/ppermute | solution.py:23
  32.8 13.1 %collective-permute-start.4 = (bf16[2,128,256]{2,1,0:T(8,128)(2,1)S(1)}, bf16[2,128,256]{2,1,0:T(8,128)(2,1)S(1)}, u32[]{:S(2)}, u32[]{:S(2)}) collective-permute-start(bf16[2,128,256]{2,1,0:T(8,128)(2,1)S(1)} %get-tuple-element.37.rest_3_), channel_id=1, source_target_pairs={{0,2},{1,3},{2,0},{3,1},{4,6},{5,7},{6,4},{7,5},{8,10},{9,11},{10,... | collective-permute-start | bytes 393224 | tf_op jit(solution)/shard_map/ppermute | solution.py:23
  34.1 11.8 %collective-permute-start.9 = (bf16[2,512,128]{2,1,0:T(8,128)(2,1)S(1)}, bf16[2,512,128]{2,1,0:T(8,128)(2,1)S(1)}, u32[]{:S(2)}, u32[]{:S(2)}) collective-permute-start(bf16[2,512,128]{2,1,0:T(8,128)(2,1)S(1)} %get-tuple-element.42.own.rest_0_), channel_id=1, source_target_pairs={{0,4},{1,5},{2,6},{3,7},{4,8},{5,9},{6,10},{7,11},{8,12},{9,13},{1... | collective-permute-start | bytes 786440 | tf_op jit(solution)/shard_map/ppermute | solution.py:23
  34.1 24.8 %collective-permute-start.16 = (bf16[2,384,256]{2,1,0:T(8,128)(2,1)S(1)}, bf16[2,384,256]{2,1,0:T(8,128)(2,1)S(1)}, u32[]{:S(2)}, u32[]{:S(2)}) collective-permute-start(bf16[2,384,256]{2,1,0:T(8,128)(2,1)S(1)} %choose.10), channel_id=1, source_target_pairs={{0,2},{1,3},{2,0},{3,1},{4,6},{5,7},{6,4},{7,5},{8,10},{9,11},{10,... | collective-permute-start | bytes 1179656 | tf_op jit(solution)/shard_map/ppermute | solution.py:23
  35.0 20.1 %collective-permute-start.14 = (bf16[2,128,512]{2,1,0:T(8,128)(2,1)S(1)}, bf16[2,128,512]{2,1,0:T(8,128)(2,1)S(1)}, u32[]{:S(2)}, u32[]{:S(2)}) collective-permute-start(bf16[2,128,512]{2,1,0:T(8,128)(2,1)S(1)} %collective-permute-done.13.rest_4_), channel_id=1, source_target_pairs={{0,4},{1,5},{2,6},{3,7},{4,8},{5,9},{6,10},{7,11},{8,12},{9,13},{1... | collective-permute-start | bytes 786440 | tf_op jit(solution)/shard_map/ppermute | solution.py:23
  45.9 8.4 %collective-permute-start.17 = (bf16[2,384,128]{2,1,0:T(8,128)(2,1)S(1)}, bf16[2,384,128]{2,1,0:T(8,128)(2,1)S(1)}, u32[]{:S(2)}, u32[]{:S(2)}) collective-permute-start(bf16[2,384,128]{2,1,0:T(8,128)(2,1)S(1)} %get-tuple-element.49.own.rest_0_), channel_id=1, source_target_pairs={{0,4},{1,5},{2,6},{3,7},{4,8},{5,9},{6,10},{7,11},{8,12},{9,13},{1... | collective-permute-start | bytes 589832 | tf_op jit(solution)/shard_map/ppermute | solution.py:23
  45.9 18.1 %collective-permute-start.8 = (bf16[2,512,128]{2,1,0:T(8,128)(2,1)S(1)}, bf16[2,512,128]{2,1,0:T(8,128)(2,1)S(1)}, u32[]{:S(2)}, u32[]{:S(2)}) collective-permute-start(bf16[2,512,128]{2,1,0:T(8,128)(2,1)S(1)} %choose.7), channel_id=1, source_target_pairs={{0,2},{1,3},{2,0},{3,1},{4,6},{5,7},{6,4},{7,5},{8,10},{9,11},{10,... | collective-permute-start | bytes 786440 | tf_op jit(solution)/shard_map/ppermute | solution.py:23
  54.2 11.3 %collective-permute-start.10 = (bf16[2,512,128]{2,1,0:T(8,128)(2,1)S(1)}, bf16[2,512,128]{2,1,0:T(8,128)(2,1)S(1)}, u32[]{:S(2)}, u32[]{:S(2)}) collective-permute-start(bf16[2,512,128]{2,1,0:T(8,128)(2,1)S(1)} %choose.8), channel_id=1, source_target_pairs={{0,2},{1,3},{2,0},{3,1},{4,6},{5,7},{6,4},{7,5},{8,10},{9,11},{10,... | collective-permute-start | bytes 786440 | tf_op jit(solution)/shard_map/ppermute | solution.py:23
  55.1 8.8 %collective-permute-start.2 = (bf16[2,384,128]{2,1,0:T(8,128)(2,1)S(1)}, bf16[2,384,128]{2,1,0:T(8,128)(2,1)S(1)}, u32[]{:S(2)}, u32[]{:S(2)}) collective-permute-start(bf16[2,384,128]{2,1,0:T(8,128)(2,1)S(1)} %get-tuple-element.36.own.rest_0_), channel_id=1, source_target_pairs={{0,4},{1,5},{2,6},{3,7},{4,8},{5,9},{6,10},{7,11},{8,12},{9,13},{1... | collective-permute-start | bytes 589832 | tf_op jit(solution)/shard_map/ppermute | solution.py:23
  55.2 16.5 %collective-permute-start.5 = (bf16[2,128,256]{2,1,0:T(8,128)(2,1)S(1)}, bf16[2,128,256]{2,1,0:T(8,128)(2,1)S(1)}, u32[]{:S(2)}, u32[]{:S(2)}) collective-permute-start(bf16[2,128,256]{2,1,0:T(8,128)(2,1)S(1)} %collective-permute-done.4.rest_4_), channel_id=1, source_target_pairs={{0,4},{1,5},{2,6},{3,7},{4,8},{5,9},{6,10},{7,11},{8,12},{9,13},{1... | collective-permute-start | bytes 393224 | tf_op jit(solution)/shard_map/ppermute | solution.py:23
  59.0 12.8 %collective-permute-start.18 = (bf16[2,384,128]{2,1,0:T(8,128)(2,1)S(1)}, bf16[2,384,128]{2,1,0:T(8,128)(2,1)S(1)}, u32[]{:S(2)}, u32[]{:S(2)}) collective-permute-start(bf16[2,384,128]{2,1,0:T(8,128)(2,1)S(1)} %choose.11), channel_id=1, source_target_pairs={{0,2},{1,3},{2,0},{3,1},{4,6},{5,7},{6,4},{7,5},{8,10},{9,11},{10,... | collective-permute-start | bytes 589832 | tf_op jit(solution)/shard_map/ppermute | solution.py:23
  64.0 10.8 %collective-permute-start.21 = (bf16[256,512]{1,0:T(8,128)(2,1)S(1)}, bf16[256,512]{1,0:T(8,128)(2,1)S(1)}, u32[]{:S(2)}, u32[]{:S(2)}) collective-permute-start(bf16[256,512]{1,0:T(8,128)(2,1)S(1)} %get-tuple-element.53), channel_id=1, source_target_pairs={{0,1},{1,0},{2,3},{3,2},{4,5},{5,4},{6,7},{7,6},{8,9},{9,8},{10,11... | collective-permute-start | bytes 786440 | tf_op jit(solution)/shard_map/ppermute | solution.py:23
  64.0 10.7 %collective-permute-start.22 = (bf16[256,512]{1,0:T(8,128)(2,1)S(1)}, bf16[256,512]{1,0:T(8,128)(2,1)S(1)}, u32[]{:S(2)}, u32[]{:S(2)}) collective-permute-start(bf16[256,512]{1,0:T(8,128)(2,1)S(1)} %get-tuple-element.54), channel_id=1, source_target_pairs={{0,1},{1,0},{2,3},{3,2},{4,5},{5,4},{6,7},{7,6},{8,9},{9,8},{10,11... | collective-permute-start | bytes 786440 | tf_op jit(solution)/shard_map/ppermute | solution.py:23
  65.5 9.0 %collective-permute-start.3 = (bf16[2,384,128]{2,1,0:T(8,128)(2,1)S(1)}, bf16[2,384,128]{2,1,0:T(8,128)(2,1)S(1)}, u32[]{:S(2)}, u32[]{:S(2)}) collective-permute-start(bf16[2,384,128]{2,1,0:T(8,128)(2,1)S(1)} %choose.6), channel_id=1, source_target_pairs={{0,2},{1,3},{2,0},{3,1},{4,6},{5,7},{6,4},{7,5},{8,10},{9,11},{10,... | collective-permute-start | bytes 589832 | tf_op jit(solution)/shard_map/ppermute | solution.py:23
  71.7 3.0 %collective-permute-start.19 = (bf16[256,256]{1,0:T(8,128)(2,1)S(1)}, bf16[256,256]{1,0:T(8,128)(2,1)S(1)}, u32[]{:S(2)}, u32[]{:S(2)}) collective-permute-start(bf16[256,256]{1,0:T(8,128)(2,1)S(1)} %get-tuple-element.51), channel_id=1, source_target_pairs={{0,1},{1,0},{2,3},{3,2},{4,5},{5,4},{6,7},{7,6},{8,9},{9,8},{10,11... | collective-permute-start | bytes 393224 | tf_op jit(solution)/shard_map/ppermute | solution.py:23
  71.8 2.9 %collective-permute-start.20 = (bf16[256,256]{1,0:T(8,128)(2,1)S(1)}, bf16[256,256]{1,0:T(8,128)(2,1)S(1)}, u32[]{:S(2)}, u32[]{:S(2)}) collective-permute-start(bf16[256,256]{1,0:T(8,128)(2,1)S(1)} %get-tuple-element.52), channel_id=1, source_target_pairs={{0,1},{1,0},{2,3},{3,2},{4,5},{5,4},{6,7},{7,6},{8,9},{9,8},{10,11... | collective-permute-start | bytes 393224 | tf_op jit(solution)/shard_map/ppermute | solution.py:23
  74.6 3.1 %collective-permute-start.23 = (bf16[256,256]{1,0:T(8,128)(2,1)S(1)}, bf16[256,256]{1,0:T(8,128)(2,1)S(1)}, u32[]{:S(2)}, u32[]{:S(2)}) collective-permute-start(bf16[256,256]{1,0:T(8,128)(2,1)S(1)} %get-tuple-element.56), channel_id=1, source_target_pairs={{0,1},{1,0},{2,3},{3,2},{4,5},{5,4},{6,7},{7,6},{8,9},{9,8},{10,11... | collective-permute-start | bytes 393224 | tf_op jit(solution)/shard_map/ppermute | solution.py:23
  77.2 1.5 %collective-permute-start.24 = (bf16[256,256]{1,0:T(8,128)(2,1)S(1)}, bf16[256,256]{1,0:T(8,128)(2,1)S(1)}, u32[]{:S(2)}, u32[]{:S(2)}) collective-permute-start(bf16[256,256]{1,0:T(8,128)(2,1)S(1)} %get-tuple-element.57), channel_id=1, source_target_pairs={{0,1},{1,0},{2,3},{3,2},{4,5},{5,4},{6,7},{7,6},{8,9},{9,8},{10,11... | collective-permute-start | bytes 393224 | tf_op jit(solution)/shard_map/ppermute | solution.py:23

commit v6 on v5

--- a/solution.py
+++ b/solution.py
@@ -14,7 +14,7 @@
 CORES = 2
 SLOTS = 4
 WHOLE = 2
-LIMIT = 58 << 20
+LIMIT = 54 << 20
 PART = 16
 SCALE = 144.0 ** (-0.5)
 
@@ -206,13 +206,12 @@
     )(*pieces, out)
 
 
-def split_kernel(arrays, width, early, *refs):
+def split_kernel(arrays, width, takes, *refs):
     sources, outs, sems = refs[:arrays], refs[arrays:-1], refs[-1]
     core = lax.axis_index("seq") % CORES
     copies = []
-    for out, which, count in zip(
-        outs, (1 - core, core, core, 1 - core), (width, width, early, early)
-    ):
+    for out, (swapped, count) in zip(outs, takes):
+        which = 1 - core if swapped else core
         for i in range(arrays):
             col = pl.multiple_of(which * width, DH)
             copy = pltpu.make_async_copy(
@@ -224,19 +223,19 @@
         copy.wait()
 
 
-def split(early, limit, *arrays):
+def split(takes, limit, *arrays):
     rows, columns = arrays[0].shape
     width = columns // CORES
-    counts = [width] * 2 + [early] * (2 if early else 0)
+    takes = tuple((swapped, count or width) for swapped, count in takes)
     anywhere = pl.BlockSpec(memory_space=pl.ANY)
     return pl.pallas_call(
-        functools.partial(split_kernel, len(arrays), width, early),
+        functools.partial(split_kernel, len(arrays), width, takes),
         out_shape=tuple(
-            pltpu.VMEM((len(arrays), rows, count), arrays[0].dtype) for count in counts
+            pltpu.VMEM((len(arrays), rows, count), arrays[0].dtype) for _, count in takes
         ),
         in_specs=[pl.BlockSpec(memory_space=pltpu.HBM)] * len(arrays),
-        out_specs=(anywhere,) * len(counts),
-        scratch_shapes=[pltpu.SemaphoreType.DMA((len(counts) * len(arrays),))],
+        out_specs=(anywhere,) * len(takes),
+        scratch_shapes=[pltpu.SemaphoreType.DMA((len(takes) * len(arrays),))],
         compiler_params=pltpu.CompilerParams(vmem_limit_bytes=limit),
         name="split",
     )(*arrays)
@@ -338,12 +337,14 @@
     paired = spans == 2 and chips % 2 == 0 and 0 < lead <= rows and len(sizes) > WHOLE + 1
     crossed = [(i, (i + 2 * CORES) % devices ^ 1) for i in range(devices)]
     early = sizes[0] * DH if paired else 0
-    kv_send, kv_near, *firstly = split(early, LIMIT, keys, values)
+    takes = ((0, early), (1, early)) if paired else ()
+    *firstly, kv_send = split((*takes, (1, 0)), LIMIT, keys, values)
     kv_far = shift(kv_send, partner)
     if paired:
         straight = shift(firstly[0], next_pair)
         cross = shift(firstly[1], crossed)
-    q_send, q_near = split(0, 1 << 20, queries)
+    (kv_near,) = split(((0, 0),), LIMIT, keys, values)
+    q_send, q_near = split(((1, 0), (0, 0)), 1 << 20, queries)
     q_far = shift(q_send, partner)
 
     shapes = []

time: 79.7 us -> 79.7 us (level)
  the two profiles are of different devices: /device:TPU:0 before, /device:TPU:11 now
where the time goes in v6:
time: 79.7 us; the launch traced here: 79.1 us
  starting transfers between devices  31.9 us (40%)
  waiting for transfers between devices  25.9 us (32%)
  Pallas kernels  21 us (26%)
    ppermute x25, starting transfers between devices, shift(): return lax.ppermute(block, 'seq', pairs)  31.9 us
    ppermute x25, waiting for transfers between devices, shift(): return lax.ppermute(block, 'seq', pairs)  25.9 us
    pallas_call x6, Pallas kernels, attend(): pl.pallas_call(functools.partial(attend_kernel, plan, spots, puts), out_s...  16.8 us
    pallas_call x3, Pallas kernels, split(): pl.pallas_call(functools.partial(split_kernel, len(arrays), width, takes)...  2.99 us
  transfers between devices with their start and end apart: 25, of which 8 were waited for; matrix products, arithmetic and copies ran while one was open for 0% of the time, Pallas kernels for 24%

profile of v6, /device:TPU:11, one launch (start us, length us, event | category | flops | bytes accessed | tf_op | source)
XLA Modules:
  0.0 79.1 jit_solution(14929205478777671300)
XLA Ops:
  0.0 1.5 %split.5 = (bf16[2,256,128]{2,1,0:T(8,128)(2,1)S(1)}, bf16[2,256,128]{2,1,0:T(8,128)(2,1)S(1)}, bf16[2,256,1024]{2,1,0:T(8,128)(2,1)S(1)}) custom-call(bf16[256,2048]{1,0:T(8,128)(2,1)} %refs_0_.5, bf16[256,2048]{1,0:T(8,128)(2,1)} %refs_1_.3), custom_call_target="tpu_custom_call" | custom-call | tf_op jit(solution)/shard_map/split/pallas_call | solution.py:231
  1.5 0.7 collective-permute-start.1
  2.3 0.2 split.3
  2.5 0.5 collective-permute-start
  3.0 1.2 %split.4.near = bf16[2,256,1024]{2,1,0:T(8,128)(2,1)S(1)} custom-call(bf16[256,2048]{1,0:T(8,128)(2,1)} %refs_0_.5, bf16[256,2048]{1,0:T(8,128)(2,1)} %refs_1_.3), custom_call_target="tpu_custom_call" | custom-call | tf_op jit(solution)/shard_map/split/pallas_call | solution.py:231
  4.3 0.3 collective-permute-done.1.far
  4.6 0.2 merge.1
  4.8 1.3 %collective-permute-start.15 = (bf16[2,384,256]{2,1,0:T(8,128)(2,1)S(1)}, bf16[2,384,256]{2,1,0:T(8,128)(2,1)S(1)}, u32[]{:S(2)}, u32[]{:S(2)}) collective-permute-start(bf16[2,384,256]{2,1,0:T(8,128)(2,1)S(1)} %get-tuple-element.45.own.rest_0_), channel_id=1, source_target_pairs={{0,4},{1,5},{2,6},{3,7},{4,8},{5,9},{6,10},{7,11},{8,12},{9,13},{1... | collective-permute-start | bytes 1179656 | tf_op jit(solution)/shard_map/ppermute | solution.py:23
  6.2 1.3 %collective-permute-start.11 = (bf16[2,384,256]{2,1,0:T(8,128)(2,1)S(1)}, bf16[2,384,256]{2,1,0:T(8,128)(2,1)S(1)}, u32[]{:S(2)}, u32[]{:S(2)}) collective-permute-start(bf16[2,384,256]{2,1,0:T(8,128)(2,1)S(1)} %get-tuple-element.42.own.rest_0_), channel_id=1, source_target_pairs={{0,4},{1,5},{2,6},{3,7},{4,8},{5,9},{6,10},{7,11},{8,12},{9,13},{1... | collective-permute-start | bytes 1179656 | tf_op jit(solution)/shard_map/ppermute | solution.py:23
  7.5 1.2 %collective-permute-start.13 = (bf16[2,128,512]{2,1,0:T(8,128)(2,1)S(1)}, bf16[2,128,512]{2,1,0:T(8,128)(2,1)S(1)}, u32[]{:S(2)}, u32[]{:S(2)}) collective-permute-start(bf16[2,128,512]{2,1,0:T(8,128)(2,1)S(1)} %get-tuple-element.43.rest_3_), channel_id=1, source_target_pairs={{0,2},{1,3},{2,0},{3,1},{4,6},{5,7},{6,4},{7,5},{8,10},{9,11},{10,... | collective-permute-start | bytes 786440 | tf_op jit(solution)/shard_map/ppermute | solution.py:23
  8.7 0.1 collective-permute-start.6
  8.8 6.4 %collective-permute-done.15.refs_0_.rest_2_ = bf16[2,384,256]{2,1,0:T(8,128)(2,1)S(1)} collective-permute-done((bf16[2,384,256]{2,1,0:T(8,128)(2,1)S(1)}, bf16[2,384,256]{2,1,0:T(8,128)(2,1)S(1)}, u32[]{:S(2)}, u32[]{:S(2)}) %collective-permute-start.15) | collective-permute-done | bytes 393248 | tf_op jit(solution)/shard_map/ppermute | solution.py:23
  15.2 3.2 %collective-permute-start.7 = (bf16[2,256,128]{2,1,0:T(8,128)(2,1)S(1)}, bf16[2,256,128]{2,1,0:T(8,128)(2,1)S(1)}, u32[]{:S(2)}, u32[]{:S(2)}) collective-permute-start(bf16[2,256,128]{2,1,0:T(8,128)(2,1)S(1)} %get-tuple-element.38), channel_id=1, source_target_pairs={{0,5},{1,4},{2,7},{3,6},{4,9},{5,8},{6,11},{7,10},{8,13},{9,12},{1... | collective-permute-start | bytes 393224 | tf_op jit(solution)/shard_map/ppermute | solution.py:23
  18.5 7.9 %collective-permute-done.6.refs_0_.rest_2_.rest_4_ = bf16[2,256,128]{2,1,0:T(8,128)(2,1)S(1)} collective-permute-done((bf16[2,256,128]{2,1,0:T(8,128)(2,1)S(1)}, bf16[2,256,128]{2,1,0:T(8,128)(2,1)S(1)}, u32[]{:S(2)}, u32[]{:S(2)}) %collective-permute-start.6) | collective-permute-done | bytes 131104 | tf_op jit(solution)/shard_map/ppermute | solution.py:23
  26.4 1.2 %collective-permute-start.16 = (bf16[2,384,256]{2,1,0:T(8,128)(2,1)S(1)}, bf16[2,384,256]{2,1,0:T(8,128)(2,1)S(1)}, u32[]{:S(2)}, u32[]{:S(2)}) collective-permute-start(bf16[2,384,256]{2,1,0:T(8,128)(2,1)S(1)} %choose.10), channel_id=1, source_target_pairs={{0,2},{1,3},{2,0},{3,1},{4,6},{5,7},{6,4},{7,5},{8,10},{9,11},{10,... | collective-permute-start | bytes 1179656 | tf_op jit(solution)/shard_map/ppermute | solution.py:23
  27.6 2.1 %collective-permute-done.7.refs_1_.rest_3_.rest_5_ = bf16[2,256,128]{2,1,0:T(8,128)(2,1)S(1)} collective-permute-done((bf16[2,256,128]{2,1,0:T(8,128)(2,1)S(1)}, bf16[2,256,128]{2,1,0:T(8,128)(2,1)S(1)}, u32[]{:S(2)}, u32[]{:S(2)}) %collective-permute-start.7) | collective-permute-done | bytes 131104 | tf_op jit(solution)/shard_map/ppermute | solution.py:23
  29.8 1.3 %collective-permute-start.17 = (bf16[2,384,128]{2,1,0:T(8,128)(2,1)S(1)}, bf16[2,384,128]{2,1,0:T(8,128)(2,1)S(1)}, u32[]{:S(2)}, u32[]{:S(2)}) collective-permute-start(bf16[2,384,128]{2,1,0:T(8,128)(2,1)S(1)} %get-tuple-element.47.own.rest_0_), channel_id=1, source_target_pairs={{0,4},{1,5},{2,6},{3,7},{4,8},{5,9},{6,10},{7,11},{8,12},{9,13},{1... | collective-permute-start | bytes 589832 | tf_op jit(solution)/shard_map/ppermute | solution.py:23
  31.1 0.0 collective-permute-done.11.refs_0_.rest_2_
  31.1 1.3 %collective-permute-start.9 = (bf16[2,512,128]{2,1,0:T(8,128)(2,1)S(1)}, bf16[2,512,128]{2,1,0:T(8,128)(2,1)S(1)}, u32[]{:S(2)}, u32[]{:S(2)}) collective-permute-start(bf16[2,512,128]{2,1,0:T(8,128)(2,1)S(1)} %get-tuple-element.40.own.rest_0_), channel_id=1, source_target_pairs={{0,4},{1,5},{2,6},{3,7},{4,8},{5,9},{6,10},{7,11},{8,12},{9,13},{1... | collective-permute-start | bytes 786440 | tf_op jit(solution)/shard_map/ppermute | solution.py:23
  32.4 0.0 collective-permute-done.q_far
  32.4 1.3 %collective-permute-start.12 = (bf16[2,384,256]{2,1,0:T(8,128)(2,1)S(1)}, bf16[2,384,256]{2,1,0:T(8,128)(2,1)S(1)}, u32[]{:S(2)}, u32[]{:S(2)}) collective-permute-start(bf16[2,384,256]{2,1,0:T(8,128)(2,1)S(1)} %choose.9), channel_id=1, source_target_pairs={{0,2},{1,3},{2,0},{3,1},{4,6},{5,7},{6,4},{7,5},{8,10},{9,11},{10,... | collective-permute-start | bytes 1179656 | tf_op jit(solution)/shard_map/ppermute | solution.py:23
  33.7 0.0 collective-permute-done.13.rest_4_
  33.7 1.8 %collective-permute-start.14 = (bf16[2,128,512]{2,1,0:T(8,128)(2,1)S(1)}, bf16[2,128,512]{2,1,0:T(8,128)(2,1)S(1)}, u32[]{:S(2)}, u32[]{:S(2)}) collective-permute-start(bf16[2,128,512]{2,1,0:T(8,128)(2,1)S(1)} %collective-permute-done.13.rest_4_), channel_id=1, source_target_pairs={{0,4},{1,5},{2,6},{3,7},{4,8},{5,9},{6,10},{7,11},{8,12},{9,13},{1... | collective-permute-start | bytes 786440 | tf_op jit(solution)/shard_map/ppermute | solution.py:23
  35.5 1.4 %collective-permute-done.17.refs_0_.rest_2_ = bf16[2,384,128]{2,1,0:T(8,128)(2,1)S(1)} collective-permute-done((bf16[2,384,128]{2,1,0:T(8,128)(2,1)S(1)}, bf16[2,384,128]{2,1,0:T(8,128)(2,1)S(1)}, u32[]{:S(2)}, u32[]{:S(2)}) %collective-permute-start.17) | collective-permute-done | bytes 196640 | tf_op jit(solution)/shard_map/ppermute | solution.py:23
  36.9 1.5 %collective-permute-start.4 = (bf16[2,128,256]{2,1,0:T(8,128)(2,1)S(1)}, bf16[2,128,256]{2,1,0:T(8,128)(2,1)S(1)}, u32[]{:S(2)}, u32[]{:S(2)}) collective-permute-start(bf16[2,128,256]{2,1,0:T(8,128)(2,1)S(1)} %get-tuple-element.35.rest_3_), channel_id=1, source_target_pairs={{0,2},{1,3},{2,0},{3,1},{4,6},{5,7},{6,4},{7,5},{8,10},{9,11},{10,... | collective-permute-start | bytes 393224 | tf_op jit(solution)/shard_map/ppermute | solution.py:23
  38.4 4.1 %collective-permute-done.9.refs_0_.rest_2_ = bf16[2,512,128]{2,1,0:T(8,128)(2,1)S(1)} collective-permute-done((bf16[2,512,128]{2,1,0:T(8,128)(2,1)S(1)}, bf16[2,512,128]{2,1,0:T(8,128)(2,1)S(1)}, u32[]{:S(2)}, u32[]{:S(2)}) %collective-permute-start.9) | collective-permute-done | bytes 262176 | tf_op jit(solution)/shard_map/ppermute | solution.py:23
  42.5 1.5 %collective-permute-start.8 = (bf16[2,512,128]{2,1,0:T(8,128)(2,1)S(1)}, bf16[2,512,128]{2,1,0:T(8,128)(2,1)S(1)}, u32[]{:S(2)}, u32[]{:S(2)}) collective-permute-start(bf16[2,512,128]{2,1,0:T(8,128)(2,1)S(1)} %choose.7), channel_id=1, source_target_pairs={{0,2},{1,3},{2,0},{3,1},{4,6},{5,7},{6,4},{7,5},{8,10},{9,11},{10,... | collective-permute-start | bytes 786440 | tf_op jit(solution)/shard_map/ppermute | solution.py:23
  44.1 2.3 %collective-permute-done.4.rest_4_ = bf16[2,128,256]{2,1,0:T(8,128)(2,1)S(1)} collective-permute-done((bf16[2,128,256]{2,1,0:T(8,128)(2,1)S(1)}, bf16[2,128,256]{2,1,0:T(8,128)(2,1)S(1)}, u32[]{:S(2)}, u32[]{:S(2)}) %collective-permute-start.4) | collective-permute-done | bytes 131104 | tf_op jit(solution)/shard_map/ppermute | solution.py:23
  46.4 1.8 %collective-permute-start.2 = (bf16[2,384,128]{2,1,0:T(8,128)(2,1)S(1)}, bf16[2,384,128]{2,1,0:T(8,128)(2,1)S(1)}, u32[]{:S(2)}, u32[]{:S(2)}) collective-permute-start(bf16[2,384,128]{2,1,0:T(8,128)(2,1)S(1)} %get-tuple-element.34.own.rest_0_), channel_id=1, source_target_pairs={{0,4},{1,5},{2,6},{3,7},{4,8},{5,9},{6,10},{7,11},{8,12},{9,13},{1... | collective-permute-start | bytes 589832 | tf_op jit(solution)/shard_map/ppermute | solution.py:23
  48.2 0.0 collective-permute-done.14.rest_5_
  48.2 0.6 collective-permute-start.5
  48.8 1.3 %collective-permute-start.10 = (bf16[2,512,128]{2,1,0:T(8,128)(2,1)S(1)}, bf16[2,512,128]{2,1,0:T(8,128)(2,1)S(1)}, u32[]{:S(2)}, u32[]{:S(2)}) collective-permute-start(bf16[2,512,128]{2,1,0:T(8,128)(2,1)S(1)} %choose.8), channel_id=1, source_target_pairs={{0,2},{1,3},{2,0},{3,1},{4,6},{5,7},{6,4},{7,5},{8,10},{9,11},{10,... | collective-permute-start | bytes 786440 | tf_op jit(solution)/shard_map/ppermute | solution.py:23
  50.1 3.7 %shard_map.49 = (bf16[256,512]{1,0:T(8,128)(2,1)S(1)}, bf16[256,512]{1,0:T(8,128)(2,1)S(1)}) custom-call(s32[8]{0:T(128)S(1)} %copy-done.1, bf16[1,256,2048]{2,1,0:T(8,128)(2,1)S(1)} %get-tuple-element.31.q_near, bf16[1,256,2048]{2,1,0:T(8,128)(2,1)S(1)} %collective-permute-done.q_far, bf16[2,384,256]{2,1,0:T(8,128)(2,1)S(1)} %get-tuple-element.45.own.rest_0_, ...), custom_call_target="tpu_custom_call" | custom-call | flops 1073741824 | bytes 2621440 | tf_op jit(solution)/shard_map/pallas_call | solution.py:164
  53.9 0.2 collective-permute-start.18
  54.1 3.7 %shard_map.48 = (bf16[256,512]{1,0:T(8,128)(2,1)S(1)}, bf16[256,512]{1,0:T(8,128)(2,1)S(1)}) custom-call(s32[8]{0:T(128)S(1)} %copy-done.1, bf16[1,256,2048]{2,1,0:T(8,128)(2,1)S(1)} %get-tuple-element.31.q_near, bf16[1,256,2048]{2,1,0:T(8,128)(2,1)S(1)} %collective-permute-done.q_far, bf16[2,384,256]{2,1,0:T(8,128)(2,1)S(1)} %get-tuple-element.42.own.rest_0_, ...), custom_call_target="tpu_custom_call" | custom-call | flops 1073741824 | bytes 2621440 | tf_op jit(solution)/shard_map/pallas_call | solution.py:164
  57.8 6.6 %collective-permute-start.22 = (bf16[256,512]{1,0:T(8,128)(2,1)S(1)}, bf16[256,512]{1,0:T(8,128)(2,1)S(1)}, u32[]{:S(2)}, u32[]{:S(2)}) collective-permute-start(bf16[256,512]{1,0:T(8,128)(2,1)S(1)} %get-tuple-element.52), channel_id=1, source_target_pairs={{0,1},{1,0},{2,3},{3,2},{4,5},{5,4},{6,7},{7,6},{8,9},{9,8},{10,11... | collective-permute-start | bytes 786440 | tf_op jit(solution)/shard_map/ppermute | solution.py:23
  64.4 0.1 collective-permute-start.21
  64.6 1.3 %collective-permute-start.3 = (bf16[2,384,128]{2,1,0:T(8,128)(2,1)S(1)}, bf16[2,384,128]{2,1,0:T(8,128)(2,1)S(1)}, u32[]{:S(2)}, u32[]{:S(2)}) collective-permute-start(bf16[2,384,128]{2,1,0:T(8,128)(2,1)S(1)} %choose.6), channel_id=1, source_target_pairs={{0,2},{1,3},{2,0},{3,1},{4,6},{5,7},{6,4},{7,5},{8,10},{9,11},{10,... | collective-permute-start | bytes 589832 | tf_op jit(solution)/shard_map/ppermute | solution.py:23
  65.9 2.5 %shard_map.46 = (bf16[256,256]{1,0:T(8,128)(2,1)S(1)}, bf16[256,256]{1,0:T(8,128)(2,1)S(1)}) custom-call(s32[8]{0:T(128)S(1)} %copy-done.1, bf16[1,256,2048]{2,1,0:T(8,128)(2,1)S(1)} %get-tuple-element.31.q_near, bf16[1,256,2048]{2,1,0:T(8,128)(2,1)S(1)} %collective-permute-done.q_far, bf16[2,512,128]{2,1,0:T(8,128)(2,1)S(1)} %get-tuple-element.36.own.rest_0_, ...), custom_call_target="tpu_custom_call" | custom-call | flops 536870912 | bytes 1310720 | tf_op jit(solution)/shard_map/pallas_call | solution.py:164
  68.3 0.8 collective-permute-start.19
  69.1 2.3 %shard_map.47 = (bf16[256,256]{1,0:T(8,128)(2,1)S(1)}, bf16[256,256]{1,0:T(8,128)(2,1)S(1)}) custom-call(s32[8]{0:T(128)S(1)} %copy-done.1, bf16[1,256,2048]{2,1,0:T(8,128)(2,1)S(1)} %get-tuple-element.31.q_near, bf16[1,256,2048]{2,1,0:T(8,128)(2,1)S(1)} %collective-permute-done.q_far, bf16[2,512,128]{2,1,0:T(8,128)(2,1)S(1)} %get-tuple-element.40.own.rest_0_, ...), custom_call_target="tpu_custom_call" | custom-call | flops 536870912 | bytes 1310720 | tf_op jit(solution)/shard_map/pallas_call | solution.py:164
  71.4 0.1 collective-permute-start.20
  71.5 2.3 %shard_map.50 = (bf16[256,256]{1,0:T(8,128)(2,1)S(1)}, bf16[256,256]{1,0:T(8,128)(2,1)S(1)}) custom-call(s32[8]{0:T(128)S(1)} %copy-done.1, bf16[1,256,2048]{2,1,0:T(8,128)(2,1)S(1)} %get-tuple-element.31.q_near, bf16[1,256,2048]{2,1,0:T(8,128)(2,1)S(1)} %collective-permute-done.q_far, bf16[2,384,128]{2,1,0:T(8,128)(2,1)S(1)} %get-tuple-element.47.own.rest_0_, ...), custom_call_target="tpu_custom_call" | custom-call | flops 536870912 | bytes 1310720 | tf_op jit(solution)/shard_map/pallas_call | solution.py:164
  73.8 0.6 collective-permute-start.23
  74.3 2.4 %shard_map.51 = (bf16[256,256]{1,0:T(8,128)(2,1)S(1)}, bf16[256,256]{1,0:T(8,128)(2,1)S(1)}, bf16[256,4096]{1,0:T(8,128)(2,1)}) custom-call(s32[8]{0:T(128)S(1)} %copy-done.1, bf16[1,256,2048]{2,1,0:T(8,128)(2,1)S(1)} %get-tuple-element.31.q_near, bf16[1,256,2048]{2,1,0:T(8,128)(2,1)S(1)} %collective-permute-done.q_far, ...), custom_call_target="tpu_custom_call" | custom-call | flops 536870912 | bytes 1310720 | tf_op jit(solution)/shard_map/pallas_call | solution.py:164
  76.8 0.1 collective-permute-start.24
  76.9 1.3 %collective-permute-done.24.refs_2_ = bf16[256,256]{1,0:T(8,128)(2,1)S(1)} collective-permute-done((bf16[256,256]{1,0:T(8,128)(2,1)S(1)}, bf16[256,256]{1,0:T(8,128)(2,1)S(1)}, u32[]{:S(2)}, u32[]{:S(2)}) %collective-permute-start.24) | collective-permute-done | bytes 131104 | tf_op jit(solution)/shard_map/ppermute | solution.py:23
  78.2 0.8 place.1
  (23 shorter events, 0.2 us)
Async XLA Ops:
  0.0 2.3 %copy-start = (bf16[256,4096]{1,0:T(8,128)(2,1)S(1)}, bf16[256,4096]{1,0:T(8,128)(2,1)}, u32[]{:S(2)}) copy-start(bf16[256,4096]{1,0:T(8,128)(2,1)} %refs_0_.3) | copy-start | bytes 6291460
  1.5 3.0 %collective-permute-start.1 = (bf16[2,256,1024]{2,1,0:T(8,128)(2,1)S(1)}, bf16[2,256,1024]{2,1,0:T(8,128)(2,1)S(1)}, u32[]{:S(2)}, u32[]{:S(2)}) collective-permute-start(bf16[2,256,1024]{2,1,0:T(8,128)(2,1)S(1)} %get-tuple-element.33), channel_id=1, source_target_pairs={{0,1},{1,0},{2,3},{3,2},{4,5},{5,4},{6,7},{7,6},{8,9},{9,8},{10,11... | collective-permute-start | bytes 3145736 | tf_op jit(solution)/shard_map/ppermute | solution.py:23
  2.5 29.9 %collective-permute-start = (bf16[1,256,2048]{2,1,0:T(8,128)(2,1)S(1)}, bf16[1,256,2048]{2,1,0:T(8,128)(2,1)S(1)}, u32[]{:S(2)}, u32[]{:S(2)}) collective-permute-start(bf16[1,256,2048]{2,1,0:T(8,128)(2,1)S(1)} %get-tuple-element.32), channel_id=1, source_target_pairs={{0,1},{1,0},{2,3},{3,2},{4,5},{5,4},{6,7},{7,6},{8,9},{9,8},{10,11... | collective-permute-start | bytes 3145736 | tf_op jit(solution)/shard_map/ppermute | solution.py:23
  4.8 10.3 %collective-permute-start.15 = (bf16[2,384,256]{2,1,0:T(8,128)(2,1)S(1)}, bf16[2,384,256]{2,1,0:T(8,128)(2,1)S(1)}, u32[]{:S(2)}, u32[]{:S(2)}) collective-permute-start(bf16[2,384,256]{2,1,0:T(8,128)(2,1)S(1)} %get-tuple-element.45.own.rest_0_), channel_id=1, source_target_pairs={{0,4},{1,5},{2,6},{3,7},{4,8},{5,9},{6,10},{7,11},{8,12},{9,13},{1... | collective-permute-start | bytes 1179656 | tf_op jit(solution)/shard_map/ppermute | solution.py:23
  6.2 24.9 %collective-permute-start.11 = (bf16[2,384,256]{2,1,0:T(8,128)(2,1)S(1)}, bf16[2,384,256]{2,1,0:T(8,128)(2,1)S(1)}, u32[]{:S(2)}, u32[]{:S(2)}) collective-permute-start(bf16[2,384,256]{2,1,0:T(8,128)(2,1)S(1)} %get-tuple-element.42.own.rest_0_), channel_id=1, source_target_pairs={{0,4},{1,5},{2,6},{3,7},{4,8},{5,9},{6,10},{7,11},{8,12},{9,13},{1... | collective-permute-start | bytes 1179656 | tf_op jit(solution)/shard_map/ppermute | solution.py:23
  7.5 26.2 %collective-permute-start.13 = (bf16[2,128,512]{2,1,0:T(8,128)(2,1)S(1)}, bf16[2,128,512]{2,1,0:T(8,128)(2,1)S(1)}, u32[]{:S(2)}, u32[]{:S(2)}) collective-permute-start(bf16[2,128,512]{2,1,0:T(8,128)(2,1)S(1)} %get-tuple-element.43.rest_3_), channel_id=1, source_target_pairs={{0,2},{1,3},{2,0},{3,1},{4,6},{5,7},{6,4},{7,5},{8,10},{9,11},{10,... | collective-permute-start | bytes 786440 | tf_op jit(solution)/shard_map/ppermute | solution.py:23
  8.7 17.7 %collective-permute-start.6 = (bf16[2,256,128]{2,1,0:T(8,128)(2,1)S(1)}, bf16[2,256,128]{2,1,0:T(8,128)(2,1)S(1)}, u32[]{:S(2)}, u32[]{:S(2)}) collective-permute-start(bf16[2,256,128]{2,1,0:T(8,128)(2,1)S(1)} %get-tuple-element.37), channel_id=1, source_target_pairs={{0,4},{1,5},{2,6},{3,7},{4,8},{5,9},{6,10},{7,11},{8,12},{9,13},{1... | collective-permute-start | bytes 393224 | tf_op jit(solution)/shard_map/ppermute | solution.py:23
  15.2 35.0 %copy-start.1 = (s32[8]{0:T(128)S(1)}, s32[8]{0:T(128)}, u32[]{:S(2)}) copy-start(s32[8]{0:T(128)} %blocks.11) | copy-start | bytes 100
  15.2 14.6 %collective-permute-start.7 = (bf16[2,256,128]{2,1,0:T(8,128)(2,1)S(1)}, bf16[2,256,128]{2,1,0:T(8,128)(2,1)S(1)}, u32[]{:S(2)}, u32[]{:S(2)}) collective-permute-start(bf16[2,256,128]{2,1,0:T(8,128)(2,1)S(1)} %get-tuple-element.38), channel_id=1, source_target_pairs={{0,5},{1,4},{2,7},{3,6},{4,9},{5,8},{6,11},{7,10},{8,13},{9,12},{1... | collective-permute-start | bytes 393224 | tf_op jit(solution)/shard_map/ppermute | solution.py:23
  26.4 22.4 %collective-permute-start.16 = (bf16[2,384,256]{2,1,0:T(8,128)(2,1)S(1)}, bf16[2,384,256]{2,1,0:T(8,128)(2,1)S(1)}, u32[]{:S(2)}, u32[]{:S(2)}) collective-permute-start(bf16[2,384,256]{2,1,0:T(8,128)(2,1)S(1)} %choose.10), channel_id=1, source_target_pairs={{0,2},{1,3},{2,0},{3,1},{4,6},{5,7},{6,4},{7,5},{8,10},{9,11},{10,... | collective-permute-start | bytes 1179656 | tf_op jit(solution)/shard_map/ppermute | solution.py:23
  29.8 7.1 %collective-permute-start.17 = (bf16[2,384,128]{2,1,0:T(8,128)(2,1)S(1)}, bf16[2,384,128]{2,1,0:T(8,128)(2,1)S(1)}, u32[]{:S(2)}, u32[]{:S(2)}) collective-permute-start(bf16[2,384,128]{2,1,0:T(8,128)(2,1)S(1)} %get-tuple-element.47.own.rest_0_), channel_id=1, source_target_pairs={{0,4},{1,5},{2,6},{3,7},{4,8},{5,9},{6,10},{7,11},{8,12},{9,13},{1... | collective-permute-start | bytes 589832 | tf_op jit(solution)/shard_map/ppermute | solution.py:23
  31.1 11.4 %collective-permute-start.9 = (bf16[2,512,128]{2,1,0:T(8,128)(2,1)S(1)}, bf16[2,512,128]{2,1,0:T(8,128)(2,1)S(1)}, u32[]{:S(2)}, u32[]{:S(2)}) collective-permute-start(bf16[2,512,128]{2,1,0:T(8,128)(2,1)S(1)} %get-tuple-element.40.own.rest_0_), channel_id=1, source_target_pairs={{0,4},{1,5},{2,6},{3,7},{4,8},{5,9},{6,10},{7,11},{8,12},{9,13},{1... | collective-permute-start | bytes 786440 | tf_op jit(solution)/shard_map/ppermute | solution.py:23
  32.4 21.5 %collective-permute-start.12 = (bf16[2,384,256]{2,1,0:T(8,128)(2,1)S(1)}, bf16[2,384,256]{2,1,0:T(8,128)(2,1)S(1)}, u32[]{:S(2)}, u32[]{:S(2)}) collective-permute-start(bf16[2,384,256]{2,1,0:T(8,128)(2,1)S(1)} %choose.9), channel_id=1, source_target_pairs={{0,2},{1,3},{2,0},{3,1},{4,6},{5,7},{6,4},{7,5},{8,10},{9,11},{10,... | collective-permute-start | bytes 1179656 | tf_op jit(solution)/shard_map/ppermute | solution.py:23
  33.7 14.5 %collective-permute-start.14 = (bf16[2,128,512]{2,1,0:T(8,128)(2,1)S(1)}, bf16[2,128,512]{2,1,0:T(8,128)(2,1)S(1)}, u32[]{:S(2)}, u32[]{:S(2)}) collective-permute-start(bf16[2,128,512]{2,1,0:T(8,128)(2,1)S(1)} %collective-permute-done.13.rest_4_), channel_id=1, source_target_pairs={{0,4},{1,5},{2,6},{3,7},{4,8},{5,9},{6,10},{7,11},{8,12},{9,13},{1... | collective-permute-start | bytes 786440 | tf_op jit(solution)/shard_map/ppermute | solution.py:23
  36.9 9.5 %collective-permute-start.4 = (bf16[2,128,256]{2,1,0:T(8,128)(2,1)S(1)}, bf16[2,128,256]{2,1,0:T(8,128)(2,1)S(1)}, u32[]{:S(2)}, u32[]{:S(2)}) collective-permute-start(bf16[2,128,256]{2,1,0:T(8,128)(2,1)S(1)} %get-tuple-element.35.rest_3_), channel_id=1, source_target_pairs={{0,2},{1,3},{2,0},{3,1},{4,6},{5,7},{6,4},{7,5},{8,10},{9,11},{10,... | collective-permute-start | bytes 393224 | tf_op jit(solution)/shard_map/ppermute | solution.py:23
  42.5 22.1 %collective-permute-start.8 = (bf16[2,512,128]{2,1,0:T(8,128)(2,1)S(1)}, bf16[2,512,128]{2,1,0:T(8,128)(2,1)S(1)}, u32[]{:S(2)}, u32[]{:S(2)}) collective-permute-start(bf16[2,512,128]{2,1,0:T(8,128)(2,1)S(1)} %choose.7), channel_id=1, source_target_pairs={{0,2},{1,3},{2,0},{3,1},{4,6},{5,7},{6,4},{7,5},{8,10},{9,11},{10,... | collective-permute-start | bytes 786440 | tf_op jit(solution)/shard_map/ppermute | solution.py:23
  46.4 11.4 %collective-permute-start.2 = (bf16[2,384,128]{2,1,0:T(8,128)(2,1)S(1)}, bf16[2,384,128]{2,1,0:T(8,128)(2,1)S(1)}, u32[]{:S(2)}, u32[]{:S(2)}) collective-permute-start(bf16[2,384,128]{2,1,0:T(8,128)(2,1)S(1)} %get-tuple-element.34.own.rest_0_), channel_id=1, source_target_pairs={{0,4},{1,5},{2,6},{3,7},{4,8},{5,9},{6,10},{7,11},{8,12},{9,13},{1... | collective-permute-start | bytes 589832 | tf_op jit(solution)/shard_map/ppermute | solution.py:23
  48.2 16.2 %collective-permute-start.5 = (bf16[2,128,256]{2,1,0:T(8,128)(2,1)S(1)}, bf16[2,128,256]{2,1,0:T(8,128)(2,1)S(1)}, u32[]{:S(2)}, u32[]{:S(2)}) collective-permute-start(bf16[2,128,256]{2,1,0:T(8,128)(2,1)S(1)} %collective-permute-done.4.rest_4_), channel_id=1, source_target_pairs={{0,4},{1,5},{2,6},{3,7},{4,8},{5,9},{6,10},{7,11},{8,12},{9,13},{1... | collective-permute-start | bytes 393224 | tf_op jit(solution)/shard_map/ppermute | solution.py:23
  48.8 19.5 %collective-permute-start.10 = (bf16[2,512,128]{2,1,0:T(8,128)(2,1)S(1)}, bf16[2,512,128]{2,1,0:T(8,128)(2,1)S(1)}, u32[]{:S(2)}, u32[]{:S(2)}) collective-permute-start(bf16[2,512,128]{2,1,0:T(8,128)(2,1)S(1)} %choose.8), channel_id=1, source_target_pairs={{0,2},{1,3},{2,0},{3,1},{4,6},{5,7},{6,4},{7,5},{8,10},{9,11},{10,... | collective-permute-start | bytes 786440 | tf_op jit(solution)/shard_map/ppermute | solution.py:23
  53.9 17.5 %collective-permute-start.18 = (bf16[2,384,128]{2,1,0:T(8,128)(2,1)S(1)}, bf16[2,384,128]{2,1,0:T(8,128)(2,1)S(1)}, u32[]{:S(2)}, u32[]{:S(2)}) collective-permute-start(bf16[2,384,128]{2,1,0:T(8,128)(2,1)S(1)} %choose.11), channel_id=1, source_target_pairs={{0,2},{1,3},{2,0},{3,1},{4,6},{5,7},{6,4},{7,5},{8,10},{9,11},{10,... | collective-permute-start | bytes 589832 | tf_op jit(solution)/shard_map/ppermute | solution.py:23
  57.8 16.5 %collective-permute-start.22 = (bf16[256,512]{1,0:T(8,128)(2,1)S(1)}, bf16[256,512]{1,0:T(8,128)(2,1)S(1)}, u32[]{:S(2)}, u32[]{:S(2)}) collective-permute-start(bf16[256,512]{1,0:T(8,128)(2,1)S(1)} %get-tuple-element.52), channel_id=1, source_target_pairs={{0,1},{1,0},{2,3},{3,2},{4,5},{5,4},{6,7},{7,6},{8,9},{9,8},{10,11... | collective-permute-start | bytes 786440 | tf_op jit(solution)/shard_map/ppermute | solution.py:23
  64.4 9.9 %collective-permute-start.21 = (bf16[256,512]{1,0:T(8,128)(2,1)S(1)}, bf16[256,512]{1,0:T(8,128)(2,1)S(1)}, u32[]{:S(2)}, u32[]{:S(2)}) collective-permute-start(bf16[256,512]{1,0:T(8,128)(2,1)S(1)} %get-tuple-element.51), channel_id=1, source_target_pairs={{0,1},{1,0},{2,3},{3,2},{4,5},{5,4},{6,7},{7,6},{8,9},{9,8},{10,11... | collective-permute-start | bytes 786440 | tf_op jit(solution)/shard_map/ppermute | solution.py:23
  64.6 9.8 %collective-permute-start.3 = (bf16[2,384,128]{2,1,0:T(8,128)(2,1)S(1)}, bf16[2,384,128]{2,1,0:T(8,128)(2,1)S(1)}, u32[]{:S(2)}, u32[]{:S(2)}) collective-permute-start(bf16[2,384,128]{2,1,0:T(8,128)(2,1)S(1)} %choose.6), channel_id=1, source_target_pairs={{0,2},{1,3},{2,0},{3,1},{4,6},{5,7},{6,4},{7,5},{8,10},{9,11},{10,... | collective-permute-start | bytes 589832 | tf_op jit(solution)/shard_map/ppermute | solution.py:23
  68.3 5.4 %collective-permute-start.19 = (bf16[256,256]{1,0:T(8,128)(2,1)S(1)}, bf16[256,256]{1,0:T(8,128)(2,1)S(1)}, u32[]{:S(2)}, u32[]{:S(2)}) collective-permute-start(bf16[256,256]{1,0:T(8,128)(2,1)S(1)} %get-tuple-element.49), channel_id=1, source_target_pairs={{0,1},{1,0},{2,3},{3,2},{4,5},{5,4},{6,7},{7,6},{8,9},{9,8},{10,11... | collective-permute-start | bytes 393224 | tf_op jit(solution)/shard_map/ppermute | solution.py:23
  71.4 2.9 %collective-permute-start.20 = (bf16[256,256]{1,0:T(8,128)(2,1)S(1)}, bf16[256,256]{1,0:T(8,128)(2,1)S(1)}, u32[]{:S(2)}, u32[]{:S(2)}) collective-permute-start(bf16[256,256]{1,0:T(8,128)(2,1)S(1)} %get-tuple-element.50), channel_id=1, source_target_pairs={{0,1},{1,0},{2,3},{3,2},{4,5},{5,4},{6,7},{7,6},{8,9},{9,8},{10,11... | collective-permute-start | bytes 393224 | tf_op jit(solution)/shard_map/ppermute | solution.py:23
  73.8 3.1 %collective-permute-start.23 = (bf16[256,256]{1,0:T(8,128)(2,1)S(1)}, bf16[256,256]{1,0:T(8,128)(2,1)S(1)}, u32[]{:S(2)}, u32[]{:S(2)}) collective-permute-start(bf16[256,256]{1,0:T(8,128)(2,1)S(1)} %get-tuple-element.54), channel_id=1, source_target_pairs={{0,1},{1,0},{2,3},{3,2},{4,5},{5,4},{6,7},{7,6},{8,9},{9,8},{10,11... | collective-permute-start | bytes 393224 | tf_op jit(solution)/shard_map/ppermute | solution.py:23
  76.8 1.4 %collective-permute-start.24 = (bf16[256,256]{1,0:T(8,128)(2,1)S(1)}, bf16[256,256]{1,0:T(8,128)(2,1)S(1)}, u32[]{:S(2)}, u32[]{:S(2)}) collective-permute-start(bf16[256,256]{1,0:T(8,128)(2,1)S(1)} %get-tuple-element.55), channel_id=1, source_target_pairs={{0,1},{1,0},{2,3},{3,2},{4,5},{5,4},{6,7},{7,6},{8,9},{9,8},{10,11... | collective-permute-start | bytes 393224 | tf_op jit(solution)/shard_map/ppermute | solution.py:23
